TPU v7x, 32 devices: a whole 2x2x4 slice. The times are simulated.
32 devices in a mesh: gr: 8 (over z, x), gc: 4 (over y, core).
Axes of the slice: x: 2, y: 2, z: 4, core: 2. Of those that a mesh axis runs over, the one named last changes fastest.
Arguments:
- orbitals: bfloat16 [1536, 16384], P(None, ('gr', 'gc')), may hold values from -0.046875 to 0.046875
- velocities: bfloat16 [1536, 16384], P(None, ('gr', 'gc')), may hold values from -40 to 40
Outputs:
- new_velocities: float32 [1536, 16384], P(None, ('gr', 'gc'))
- violations: float32 [1], replicated
All inputs are finite; a program needn't handle non-finite values.
Results may differ from a plain program's by a relative error of at most 0.0018.
Values may be sent and summed in bfloat16 or wider, within the bound.
No kernel may reach another device: no remote copies, remote signals or barrier semaphores. Data moves between devices by JAX's collectives and lax.ppermute only.
A program may use at most 64 MiB of HBM per device.

v0:
```python
import jax
import jax.numpy as jnp
from jax import lax
from jax.sharding import PartitionSpec as P

M = 1536


def local(orbitals, velocities):
    total_rows = orbitals.shape[0]
    local_cols = orbitals.shape[1]
    row_groups = lax.axis_size("gr")
    edge = total_rows // row_groups
    half = row_groups // 2 + 1
    offsets = jnp.arange(half, dtype=jnp.int32)
    mirror_mask = ((offsets >= 1) & (2 * offsets != row_groups)).astype(jnp.float32)
    orb_blocks = orbitals.reshape(row_groups, edge, local_cols)
    targets = jnp.arange(row_groups, dtype=jnp.int32)
    vel = velocities.astype(jnp.float32)
    vel_b = vel.astype(jnp.bfloat16)
    intersection = jnp.dot(orbitals, vel_b.T, preferred_element_type=jnp.float32)
    sym_local = intersection + intersection.T
    sym_four = sym_local.reshape(row_groups, edge, row_groups, edge)
    every_row = jnp.arange(row_groups, dtype=jnp.int32)
    every_col = (every_row[:, None] + offsets[None, :]) % row_groups
    full_term = sym_four[every_row[:, None], :, every_col, :].reshape(
        row_groups * half * edge, edge
    )
    share_rows = row_groups * half * edge // (row_groups * lax.axis_size("gc"))
    share = lax.psum_scatter(full_term, ("gr", "gc"), scatter_dimension=0, tiled=True)
    rows_here = lax.axis_index(("gr", "gc")) * share_rows + jnp.arange(share_rows, dtype=jnp.int32)
    offset_of = rows_here // edge % half
    weight = jnp.where((offset_of >= 1) & (2 * offset_of != row_groups), 2.0, 1.0)
    local_sq = jnp.sum(weight[:, None] * share * share)
    sym_b = share.astype(jnp.bfloat16)
    joined = lax.all_gather(sym_b, ("gr", "gc"), axis=0, tiled=True)
    piece = joined.reshape(row_groups, half * edge * edge)
    count = piece.shape[0]
    block_rows = jnp.arange(count, dtype=jnp.int32)
    block_cols = (block_rows[:, None] + offsets[None, :]) % row_groups
    blocks = piece.reshape(count, half, edge, edge)
    far_orb = jnp.take(orb_blocks, block_cols, axis=0)
    own_orb = jnp.take(orb_blocks, block_rows, axis=0)
    direct = jnp.einsum("jkab,jkbg->jag", blocks, far_orb, preferred_element_type=jnp.float32)
    mirrored = jnp.einsum("jkab,jag->jkbg", blocks, own_orb, preferred_element_type=jnp.float32)
    row_hot = (block_rows[:, None] == targets[None, :]).astype(jnp.float32)
    col_hot = (block_cols[:, :, None] == targets[None, None, :]).astype(jnp.float32) * mirror_mask[
        None, :, None
    ]
    carry = jnp.einsum("jq,jag->qag", row_hot, direct)
    carry = carry + jnp.einsum("jkq,jkbg->qbg", col_hot, mirrored)
    correction = carry.reshape(total_rows, local_cols)
    summed = lax.psum(local_sq, ("gr", "gc"))
    measured = [jnp.sqrt(summed) / M]
    vel = vel - 0.5 * correction
    return (vel, jnp.stack(measured))


def solution(mesh):
    in_specs = (P(None, ("gr", "gc")), P(None, ("gr", "gc")))
    out_specs = (P(None, ("gr", "gc")), P())
    return jax.shard_map(local, mesh=mesh, in_specs=in_specs, out_specs=out_specs, check_vma=False)
```

profile of v0, /device:TPU:0, one launch (start us, length us, event | category | flops | bytes accessed | tf_op | source)
XLA Modules:
  0.0 295.9 jit_solution(1562498942545767514)
XLA Ops:
  7.2 0.0 copy-start
  7.2 0.0 reduce-scatter.4.cloned.1.call-start
  7.2 1.3 copy-done
  8.6 6.4 %fusion.38 = f32[1536,1536]{1,0:T(8,128)} fusion(bf16[1536,512]{1,0:T(8,128)(2,1)S(1)} %copy-done, bf16[1536,512]{1,0:T(8,128)(2,1)} %param.3), kind=kOutput, calls=%fused_computation.61 | convolution fusion | flops 2415919104 | bytes 12582912 | tf_op jit(solution)/shard_map/dot_general | solution.py:21
  15.0 9.6 %copy.20 = f32[1536,1536]{0,1:T(8,128)} copy(f32[1536,1536]{1,0:T(8,128)} %fusion.38) | data formatting | bytes 18874368 | tf_op jit(solution)/shard_map/dot_general | solution.py:21
  24.6 12.1 %bitcast_add_fusion = f32[1536,1536]{1,0:T(8,128)} fusion(f32[1536,1536]{1,0:T(8,128)} %fusion.38, f32[1536,1536]{0,1:T(8,128)} %copy.20), kind=kLoop, calls=%fused_computation.5 | loop fusion | flops 2359296 | bytes 28311552 | tf_op jit(solution)/shard_map/add | solution.py:22
  36.7 12.5 %reshape.135 = f32[8,192,8,192]{3,2,1,0:T(8,128)} reshape(f32[1536,1536]{1,0:T(8,128)} %bitcast_add_fusion) | data formatting | bytes 18874368 | tf_op jit(solution)/shard_map/reshape | solution.py:23
  49.2 12.8 %copy.21 = f32[8,192,8,192]{3,1,2,0:T(8,128)} copy(f32[8,192,8,192]{3,2,1,0:T(8,128)} %reshape.135) | data formatting | bytes 18874368 | tf_op jit(solution)/shard_map/reshape | solution.py:23
  62.0 0.1 reshape.138
  62.1 9.0 %gather_fusion = f32[40,192,192]{2,1,0:T(8,128)} fusion(f32[8,192,8,192]{3,1,2,0:T(8,128)} %copy.21, s32[40]{0:T(128)S(1)} %reshape.138), kind=kCustom, calls=%fused_computation | custom fusion | bytes 11796800 | tf_op jit(solution)/shard_map/gather | solution.py:26
  71.1 0.0 reduce-scatter.4.cloned.1.call-update
  71.1 0.0 all-gather.3.cloned.1.call-start
  71.2 125.9 %reduce-scatter.4.cloned.1.call-done = f32[240,192]{1,0:T(8,128)} async-done(((f32[7680,192]{1,0:T(8,128)}), f32[240,192]{1,0:T(8,128)}) %reduce-scatter.4.cloned.1.call-update) | async-done | bytes 184336
  197.2 1.1 copy.35
  198.2 1.3 fusion.19
  199.5 0.0 all-gather.3.cloned.1.call-update
  199.5 0.1 reshape.146
  199.6 0.1 copy.24
  199.7 5.7 %gather_fusion.1 = bf16[40,192,512]{2,1,0:T(8,128)(2,1)} fusion(bf16[8,192,512]{2,1,0:T(8,128)(2,1)S(1)} %bitcast.39, s32[1024]{0:T(1024)S(1)} %pad_clamp_fusion.1), kind=kCustom, calls=%fused_computation.1 | custom fusion | bytes 15728800 | tf_op jit(solution)/shard_map/jit(_take)/gather | solution.py:42
  205.4 1.8 gather_fusion.2
  207.3 40.2 %psum.7 = f32[]{:T(128)} all-reduce(f32[]{:T(128)} %get-tuple-element.2), channel_id=1, replica_groups=mesh['gr'=8,'gc'=4] {'gr','gc'}, use_global_device_ids=true, to_apply=%region_2.3 | all-reduce | flops 1 | bytes 8 | tf_op jit(solution)/shard_map/psum | solution.py:53
  248.2 10.4 %all-gather.3.cloned.1.call-done = bf16[32,240,192]{1,2,0:T(8,128)(2,1)} async-done(((bf16[1,240,192]{1,2,0:T(8,128)(2,1)}), bf16[32,240,192]{1,2,0:T(8,128)(2,1)}) %all-gather.3.cloned.1.call-update) | async-done | bytes 2949136 | tf_op jit(solution)/shard_map/all_gather | solution.py:36
  258.6 5.7 %copy.23 = bf16[32,240,192]{2,1,0:T(8,128)(2,1)} copy(bf16[32,240,192]{1,2,0:T(8,128)(2,1)} %all-gather.3.cloned.1.call-done) | data formatting | bytes 5898240 | tf_op jit(solution)/shard_map/all_gather | solution.py:36
  264.4 6.4 %fusion.11 = bf16[8,192,512]{2,1,0:T(8,128)(2,1)S(1)} fusion(bf16[8,5,192,192]{3,2,1,0:T(8,128)(2,1)} %bitcast.42, bf16[8,5,192,512]{3,2,1,0:T(8,128)(2,1)} %bitcast.44, pred[8,5]{1,0:T(8,128)(4,1)S(1)} %copy.24), kind=kOutput, calls=%fused_computation.15 | convolution fusion | flops 1513881600 | bytes 12386344 | tf_op jit(solution)/shard_map/jkab,jkbg->jag/dot_general | solution.py:44
  270.8 0.0 copy-start.1
  270.8 2.7 fusion.7
  273.5 0.0 copy-done.1
  273.5 3.8 %fusion.14 = bf16[8,5,192,512]{3,2,1,0:T(8,128)(2,1)S(1)} fusion(bf16[8,5,192,192]{3,2,1,0:T(8,128)(2,1)S(1)} %bitcast.43, bf16[8,192,512]{2,1,0:T(8,128)(2,1)} %gather_fusion.2, pred[8]{0:T(512)(128)(4,1)S(1)} %iota_compare_fusion.3), kind=kOutput, calls=%fused_computation.16 | convolution fusion | flops 1510735872 | bytes 12386312 | tf_op jit(solution)/shard_map/jkab,jag->jkbg/dot_general | solution.py:45
  277.3 6.6 %fusion.6 = f32[8,192,512]{2,0,1:T(8,128)S(1)} fusion(f32[8,192,512]{2,0,1:T(8,128)} %fusion.7, bf16[8,5,192,512]{3,2,1,0:T(8,128)(2,1)S(1)} %fusion.14, bf16[5]{0:T(256)(128)(2,1)S(1)} %and_convert_fusion, s32[8,5]{0,1:T(8,128)S(1)} %add_select_fusion), kind=kOutput, calls=%fused_computation.12 | convolution fusion | flops 64488064 | bytes 14155946 | tf_op jit(solution)/shard_map/jkq,jkbg->qbg/dot_general | solution.py:51
  283.9 0.0 copy-start.2
  283.9 1.8 copy.28
  285.8 0.0 copy-done.2
  285.8 2.2 bitcast_subtract_fusion
  (10 shorter events, 0.1 us)
Async XLA Ops:
  7.2 1.4 copy-start
  7.2 190.0 %reduce-scatter.4.cloned.1.call-start = ((), (), s32[]{:S(2)}) async-start(), calls=%async_computation.2 | async-start | bytes 8110080
  71.1 187.5 %all-gather.3.cloned.1.call-start = ((), (), s32[]{:S(2)}) async-start(), calls=%async_computation.1 | async-start | bytes 3244032 | tf_op jit(solution)/shard_map/all_gather | solution.py:36
  270.8 2.7 copy-start.1
  283.9 1.8 copy-start.2
Sparse Core Ops, SparseCore 0:
  71.3 125.8 reduce-scatter.3
  200.6 57.9 all-gather.2
where the time goes:
time: 297 us; the launch traced here: 296 us
  waiting for transfers between devices  136 us (46%)
  local copies, waits for them, and re-layouts  61.7 us (21%)
  blocking collectives  40.2 us (14%)
  matrix products  25.9 us (9%)
  between operations  16 us (5%)
  other arithmetic  15.6 us (5%)
    unnamed x3, waiting for transfers between devices  126 us
    psum x1, blocking collectives, local(): summed = lax.psum(local_sq, ('gr', 'gc'))  40.2 us
    reshape x2, local copies, waits for them, and re-layouts, local(): sym_four = sym_local.reshape(row_groups, edge, row_groups, edge)  25.3 us
    add x1, other arithmetic, local(): sym_local = intersection + intersection.T  12.1 us
    all_gather x1, waiting for transfers between devices, local(): joined = lax.all_gather(sym_b, ('gr', 'gc'), axis=0, tiled=True)  10.4 us
    dot_general x1, local copies, waits for them, and re-layouts, local(): jnp.dot(orbitals, vel_b.T, preferred_element_type=jnp.float32)  9.62 us
    gather x1, local copies, waits for them, and re-layouts, local(): sym_four[every_row[:, None], :, every_col, :]  9.02 us
    dot_general x1, matrix products, local(): carry = carry + jnp.einsum('jkq,jkbg->qbg', col_hot, mirrored)  6.63 us
  transfers between devices with their start and end apart: 2, of which 2 were waited for; matrix products, arithmetic and copies ran while one was open for 3% of the time, Pallas kernels for 0%

commit v1 on v0

v1 whole, which is shorter than its diff:
```python
import jax
import jax.numpy as jnp
from jax import lax
from jax.experimental import pallas as pl
from jax.experimental.pallas import tpu as pltpu
from jax.sharding import PartitionSpec as P

TILE = 128
CHUNKS = 2
PAD = 16
AXES = ("gr", "gc")
BF16 = jnp.bfloat16
F32 = jnp.float32
VMEM = pl.BlockSpec(memory_space=pltpu.VMEM)
SMEM = pl.BlockSpec(memory_space=pltpu.SMEM)


def layout(total_rows):
    tiles = total_rows // TILE
    side = tiles // 2
    extra = side // 2
    where = {}
    for i in range(side):
        for k in range(side):
            where[(i, i + k)] = i * side + k
    count = side * side + extra
    return side, extra, where, count


def product_kernel(half_ref, orb_ref, vel_ref, *out_refs, total_rows):
    side, extra, where, count = layout(total_rows)
    chunk_rows = count * TILE // CHUNKS
    h = half_ref[0]
    low = pl.multiple_of(h * (side * TILE), TILE)
    up = pl.multiple_of((1 - h) * (side * TILE), TILE)

    def put(index, value):
        value = value.astype(BF16)
        row = index * TILE
        end = row + TILE
        while row < end:
            chunk = row // chunk_rows
            stop = min(end, (chunk + 1) * chunk_rows)
            begin = index * TILE
            out_refs[chunk][row - chunk * chunk_rows : stop - chunk * chunk_rows, :] = value[
                row - begin : stop - begin
            ]
            row = stop

    def both(r0, rows, c0, cols):
        dims = (((1,), (1,)), ((), ()))
        one = lax.dot_general(
            orb_ref[pl.ds(r0, rows), :], vel_ref[pl.ds(c0, cols), :], dims, preferred_element_type=F32
        )
        two = lax.dot_general(
            vel_ref[pl.ds(r0, rows), :], orb_ref[pl.ds(c0, cols), :], dims, preferred_element_type=F32
        )
        return one + two

    for c in range(0, 2 * side - 1, 2):
        wide = min(2, 2 * side - 1 - c)
        first = max(0, c - side + 1)
        last = min(side - 1, c + wide - 1)
        start = low + c * TILE if c < side else up + (c - side) * TILE
        value = both(low + first * TILE, (last - first + 1) * TILE, start, wide * TILE)
        for i in range(first, last + 1):
            for k in range(wide):
                if (i, c + k) in where:
                    put(
                        where[(i, c + k)],
                        value[(i - first) * TILE : (i - first + 1) * TILE, k * TILE : (k + 1) * TILE],
                    )
    for k in range(extra):
        shift = pl.multiple_of((h * extra + k) * TILE, TILE)
        put(side * side + k, both(low + shift, TILE, up + shift, TILE))


def product(half, orb, vel):
    rows = orb.shape[0]
    count = layout(rows)[3]
    shape = jax.ShapeDtypeStruct((count * TILE // CHUNKS, TILE), BF16)
    return pl.pallas_call(
        lambda *refs: product_kernel(*refs, total_rows=rows),
        out_shape=[shape] * CHUNKS,
        in_specs=[SMEM, VMEM, VMEM],
        out_specs=[VMEM] * CHUNKS,
    )(half, orb, vel)


def share_kernel(off_ref, a_ref, b_ref, out_ref, *, side):
    rows = a_ref.shape[0]
    total = a_ref[...].astype(F32) + b_ref[...].astype(F32)
    out_ref[0:rows, :] = total.astype(BF16)
    row = lax.broadcasted_iota(jnp.int32, (rows, 1), 0) + off_ref[0]
    tile = row // TILE
    diagonal = (tile < side * side) & (tile % side == 0)
    weight = jnp.where(diagonal, 1.0, 2.0).astype(F32)
    square = jnp.sum(jnp.sum(total * total * weight, axis=0, keepdims=True), axis=1, keepdims=True)
    high = square.astype(BF16).astype(F32)
    rest = square - high
    middle = rest.astype(BF16).astype(F32)
    small = rest - middle
    line = lax.broadcasted_iota(jnp.int32, (PAD, TILE), 0)
    tail = jnp.where(line == 0, high, jnp.where(line == 1, middle, jnp.where(line == 2, small, 0.0)))
    out_ref[rows : rows + PAD, :] = tail.astype(BF16)


def make_share(offset, a, b, side):
    rows = a.shape[0]
    return pl.pallas_call(
        lambda *refs: share_kernel(*refs, side=side),
        out_shape=jax.ShapeDtypeStruct((rows + PAD, TILE), BF16),
        in_specs=[SMEM, VMEM, VMEM],
        out_specs=VMEM,
    )(offset, a, b)


def apply_kernel(half_ref, orb_ref, base_ref, *refs, total_rows, shares):
    side, extra, where, count = layout(total_rows)
    pieces = refs[:CHUNKS]
    out_ref, a_ref, b_ref, t_ref = refs[CHUNKS:]
    chunk_rows = count * TILE // CHUNKS
    share_rows = chunk_rows // shares
    h = half_ref[0]
    low = pl.multiple_of(h * (side * TILE), TILE)
    up = pl.multiple_of((1 - h) * (side * TILE), TILE)

    def tile(index):
        row, end = index * TILE, (index + 1) * TILE
        parts = []
        while row < end:
            chunk = row // chunk_rows
            inside = row - chunk * chunk_rows
            share = inside // share_rows
            stop = min(end, chunk * chunk_rows + (share + 1) * share_rows)
            at = share * (share_rows + PAD) + inside - share * share_rows
            parts.append(pieces[chunk][at : at + stop - row, :])
            row = stop
        return parts[0] if len(parts) == 1 else jnp.concatenate(parts, axis=0)

    zero = jnp.zeros((TILE, TILE), BF16)

    def block(ref, i, j, value):
        ref[i * TILE : (i + 1) * TILE, j * TILE : (j + 1) * TILE] = value

    for i in range(side):
        for j in range(i - i % 2, min(side, i - i % 2 + 2)):
            if j >= i:
                block(b_ref, i, j, zero)
                block(t_ref, j, i, zero)
    for (i, j), index in where.items():
        value = tile(index)
        if j < side:
            block(a_ref, i, j, value)
            if i != j:
                block(a_ref, j, i, value.T)
        else:
            block(b_ref, i, j - side, value)
            block(t_ref, j - side, i, value.T)
    for k in range(extra):
        value = tile(side * side + k)
        at = pl.multiple_of((h * extra + k) * TILE, TILE)
        b_ref[pl.ds(at, TILE), pl.ds(at, TILE)] = value
        t_ref[pl.ds(at, TILE), pl.ds(at, TILE)] = value.T

    wide = side * TILE
    panel = 2 * TILE
    for p in range(0, wide, panel):
        upto = min(p + panel, wide)
        rows = upto - p
        value = jnp.dot(a_ref[p:upto, :], orb_ref[pl.ds(low, wide), :], preferred_element_type=F32)
        value += jnp.dot(b_ref[p:upto, :upto], orb_ref[pl.ds(up, upto), :], preferred_element_type=F32)
        at = pl.ds(low + p, rows)
        out_ref[at, :] = base_ref[at, :].astype(F32) - 0.5 * value
        value = jnp.dot(
            t_ref[p:upto, p:], orb_ref[pl.ds(low + p, wide - p), :], preferred_element_type=F32
        )
        at = pl.ds(up + p, rows)
        out_ref[at, :] = base_ref[at, :].astype(F32) - 0.5 * value


def apply_half(half, orb, base, pieces, shares):
    rows = orb.shape[0]
    wide = layout(rows)[0] * TILE
    return pl.pallas_call(
        lambda *refs: apply_kernel(*refs, total_rows=rows, shares=shares),
        out_shape=jax.ShapeDtypeStruct(orb.shape, F32),
        in_specs=[SMEM] + [VMEM] * (2 + CHUNKS),
        out_specs=VMEM,
        scratch_shapes=[pltpu.VMEM((wide, wide), BF16)] * 3,
    )(half, orb, base, *pieces)


def pairs(nr, nc, even, odd):
    result = []
    for r in range(nr):
        for c in range(nc):
            flip = odd if c & 1 else even
            result.append((r * nc + c, (r ^ flip[0]) * nc + (c ^ flip[1])))
    return result


def local(orbitals, velocities):
    nr, nc = lax.axis_size("gr"), lax.axis_size("gc")
    r, c = lax.axis_index("gr"), lax.axis_index("gc")
    total_rows = orbitals.shape[0]
    side, _, _, count = layout(total_rows)
    core = c & 1
    on_r, on_c = r & 1, (c >> 1) & 1
    bit1 = jnp.where(core == 0, on_r, on_c)
    bit2 = jnp.where(core == 0, on_c, on_r)
    swap = pairs(nr, nc, (0, 1), (0, 1))
    first = pairs(nr, nc, (1, 0), (0, 2))
    second = pairs(nr, nc, (0, 2), (1, 0))
    rest = [(1 << b, 0) for b in range(1, nr.bit_length() - 1)]
    rest += [(0, 1 << b) for b in range(2, nc.bit_length() - 1)]
    doubling = [pairs(nr, nc, rest[k], rest[-1 - k]) for k in range(len(rest))]
    shares = 4
    chunk_rows = count * TILE // CHUNKS
    half_rows, share_rows = chunk_rows // 2, chunk_rows // 4

    def move(value, perm):
        return lax.ppermute(value, AXES, perm)

    def cut(value, index, rows):
        return lax.dynamic_slice_in_dim(value, index * rows, rows, 0).astype(F32)

    def rounded(value):
        return lax.reduce_precision(value, 8, 7)

    own = core.reshape(1)
    other = (1 - core).reshape(1)
    away = product(other, orbitals, velocities)
    away = [move(x, swap) for x in away]
    keep = product(own, orbitals, velocities)
    joined = []
    for k in range(CHUNKS):
        mine, got = keep[k], away[k]
        send = cut(mine, 1 - bit1, half_rows) + cut(got, 1 - bit1, half_rows)
        got1 = move(send.astype(BF16), first)
        mine1 = cut(mine, bit1, half_rows) + cut(got, bit1, half_rows)
        send = cut(mine1, 1 - bit2, share_rows) + cut(got1, 1 - bit2, share_rows)
        got2 = move(send.astype(BF16), second)
        mine2 = cut(mine1, bit2, share_rows) + cut(got1, bit2, share_rows)
        total = rounded(mine2 + got2.astype(F32))
        for j, perm in enumerate(doubling):
            sent = total.astype(BF16)
            back = move(sent, perm)
            if j < len(doubling) - 1:
                total = rounded(total + back.astype(F32))
        offset = k * chunk_rows + bit1 * half_rows + bit2 * share_rows
        share = make_share(offset.reshape(1), sent, back, side)
        back = move(share, second)
        low = jnp.where(bit2 == 0, share, back)
        high = jnp.where(bit2 == 0, back, share)
        quarter = jnp.concatenate([low, high], axis=0)
        back = move(quarter, first)
        low = jnp.where(bit1 == 0, quarter, back)
        high = jnp.where(bit1 == 0, back, quarter)
        joined.append(jnp.concatenate([low, high], axis=0))
    far = [move(x, swap) for x in joined]
    partial = apply_half(own, orbitals, velocities, joined, shares)
    new = apply_half(other, orbitals, partial, far, shares)

    def squares(pieces):
        total = 0.0
        for x in pieces:
            tails = x.reshape(shares, share_rows + PAD, TILE)[:, share_rows : share_rows + 3, 0]
            total = total + jnp.sum(tails.astype(F32))
        return total

    measured = jnp.sqrt(squares(joined) + squares(far)) / total_rows
    return new, measured.reshape(1)


def solution(mesh):
    in_specs = (P(None, AXES), P(None, AXES))
    out_specs = (P(None, AXES), P())
    return jax.shard_map(local, mesh=mesh, in_specs=in_specs, out_specs=out_specs, check_vma=False)
```

time: 297 us -> 91.3 us (0.31)
  waiting for transfers between devices: 136 us -> 34.2 us
  local copies, waits for them, and re-layouts: 61.7 us -> 2.09 us
  blocking collectives: 40.2 us -> 0 us
  matrix products: 25.9 us -> 0 us
  Pallas kernels: 0 us -> 25.6 us
  starting transfers between devices: 0.08 us -> 19.5 us
  between operations: 16 us -> 4.58 us
  other arithmetic: 15.6 us -> 5.03 us
    unnamed x3 -> x0, waiting for transfers between devices: 126 us -> none
    psum x1 -> x0, blocking collectives: 40.2 us -> none  [local(): summed = lax.psum(local_sq, ('gr', 'gc'))]
    ppermute x0 -> x16, waiting for transfers between devices: none -> 34.2 us  [move(): return lax.ppermute(value, AXES, perm)]
    dot_general x5 -> x0, matrix products: 25.9 us -> none  [the longest x1 6.63 us: local(): carry = carry + jnp.einsum('jkq,jkbg->qbg', col_hot, mirrored)]
    pallas_call x0 -> x6, Pallas kernels: none -> 25.6 us  [the longest x2 11.8 us: apply_half(): pl.pallas_call(lambda *refs: apply_kernel(*refs, total_rows=rows, shares=...]
    reshape x2 -> x0, local copies, waits for them, and re-layouts: 25.3 us -> none  [local(): sym_four = sym_local.reshape(row_groups, edge, row_groups, edge)]
    ppermute x0 -> x16, starting transfers between devices: none -> 19.5 us  [move(): return lax.ppermute(value, AXES, perm)]
    gather x3 -> x0, local copies, waits for them, and re-layouts: 16.5 us -> none  [the longest x1 9.02 us: local(): sym_four[every_row[:, None], :, every_col, :]]
  transfers between devices with their start and end apart: 2 -> 16, of which waited for: 2 -> 8; matrix products, arithmetic and copies ran while one was open for 3% -> 5% of each run, Pallas kernels for 0% -> 16%
where the time goes in v1:
time: 91.3 us; the launch traced here: 91 us
  waiting for transfers between devices  34.2 us (37%)
  Pallas kernels  25.6 us (28%)
  starting transfers between devices  19.5 us (21%)
  other arithmetic  5.03 us (6%)
  between operations  4.58 us (5%)
  local copies, waits for them, and re-layouts  2.09 us (2%)
    ppermute x16, waiting for transfers between devices, move(): return lax.ppermute(value, AXES, perm)  34.2 us
    ppermute x16, starting transfers between devices, move(): return lax.ppermute(value, AXES, perm)  19.5 us
    pallas_call x2, Pallas kernels, apply_half(): pl.pallas_call(lambda *refs: apply_kernel(*refs, total_rows=rows, shares=...  11.8 us
    pallas_call x2, Pallas kernels, product(): pl.pallas_call(lambda *refs: product_kernel(*refs, total_rows=rows), out_...  9.12 us
    pallas_call x2, Pallas kernels, make_share(): pl.pallas_call(lambda *refs: share_kernel(*refs, side=side), out_shape=ja...  4.64 us
    reduce_sum x3, other arithmetic, squares(): total = total + jnp.sum(tails.astype(F32))  2.76 us
    unnamed x22, local copies, waits for them, and re-layouts  2.09 us
  transfers between devices with their start and end apart: 16, of which 8 were waited for; matrix products, arithmetic and copies ran while one was open for 5% of the time, Pallas kernels for 16%

profile of v1, /device:TPU:0, one launch (start us, length us, event | category | flops | bytes accessed | tf_op | source)
XLA Modules:
  0.0 91.0 jit_solution(2223206608375366590)
XLA Ops:
  0.6 4.6 %shard_map.42 = (bf16[2496,128]{1,0:T(8,128)(2,1)}, bf16[2496,128]{1,0:T(8,128)(2,1)}) custom-call(s32[1]{0:T(128)} %bitcast.refs_0_, bf16[1536,512]{1,0:T(8,128)(2,1)} %refs_1_.7, bf16[1536,512]{1,0:T(8,128)(2,1)} %refs_2_.5), custom_call_target="tpu_custom_call" | custom-call | tf_op jit(solution)/shard_map/pallas_call | solution.py:82
  5.2 0.5 collective-permute-start.7
  5.7 0.0 collective-permute-start
  5.7 4.5 %shard_map.41 = (bf16[2496,128]{1,0:T(8,128)(2,1)}, bf16[2496,128]{1,0:T(8,128)(2,1)}) custom-call(s32[1]{0:T(128)} %bitcast.1.refs_0_, bf16[1536,512]{1,0:T(8,128)(2,1)} %refs_1_.7, bf16[1536,512]{1,0:T(8,128)(2,1)} %refs_2_.5), custom_call_target="tpu_custom_call" | custom-call | tf_op jit(solution)/shard_map/pallas_call | solution.py:82
  10.3 1.3 %add_convert_fusion = (bf16[1248,128]{1,0:T(8,128)(2,1)S(1)}, f32[1248,128]{1,0:T(8,128)S(1)}) fusion(bf16[2496,128]{1,0:T(8,128)(2,1)S(1)} %collective-permute-done.7, s32[]{:T(128)S(6)} %select_n.77, bf16[2496,128]{1,0:T(8,128)(2,1)} %get-tuple-element.8, s32[]{:T(128)S(6)} %select_n.75), kind=kLoop, calls=%fused_computation.2 | loop fusion | flops 1118208 | bytes 2236424 | tf_op jit(solution)/shard_map/convert_element_type | solution.py:240
  11.6 3.1 %collective-permute-start.8 = (bf16[1248,128]{1,0:T(8,128)(2,1)S(1)}, bf16[1248,128]{1,0:T(8,128)(2,1)S(1)}, u32[]{:S(2)}, u32[]{:S(2)}) collective-permute-start(bf16[1248,128]{1,0:T(8,128)(2,1)S(1)} %get-tuple-element.10), channel_id=1, source_target_pairs={{0,4},{1,3},{2,6},{3,1},{4,0},{5,7},{6,2},{7,5},{8,12},{9,11},{10,... | collective-permute-start | bytes 958472 | tf_op jit(solution)/shard_map/ppermute | solution.py:223
  14.6 5.0 %collective-permute-done.8 = bf16[1248,128]{1,0:T(8,128)(2,1)S(1)} collective-permute-done((bf16[1248,128]{1,0:T(8,128)(2,1)S(1)}, bf16[1248,128]{1,0:T(8,128)(2,1)S(1)}, u32[]{:S(2)}, u32[]{:S(2)}) %collective-permute-start.8) | collective-permute-done | bytes 319520 | tf_op jit(solution)/shard_map/ppermute | solution.py:223
  19.6 2.1 %collective-permute-start.9 = (bf16[624,128]{1,0:T(8,128)(2,1)S(1)}, bf16[624,128]{1,0:T(8,128)(2,1)S(1)}, u32[]{:S(2)}, u32[]{:S(2)}) collective-permute-start(bf16[624,128]{1,0:T(8,128)(2,1)S(1)} %add_convert_fusion.2), channel_id=1, source_target_pairs={{0,2},{1,5},{2,0},{3,7},{4,6},{5,1},{6,4},{7,3},{8,10},{9,13},{10,... | collective-permute-start | bytes 479240 | tf_op jit(solution)/shard_map/ppermute | solution.py:223
  21.7 0.0 collective-permute-done
  21.7 0.1 add_convert_fusion.1
  21.9 1.6 %collective-permute-start.1 = (bf16[1248,128]{1,0:T(8,128)(2,1)S(1)}, bf16[1248,128]{1,0:T(8,128)(2,1)S(1)}, u32[]{:S(2)}, u32[]{:S(2)}) collective-permute-start(bf16[1248,128]{1,0:T(8,128)(2,1)S(1)} %get-tuple-element.12), channel_id=1, source_target_pairs={{0,4},{1,3},{2,6},{3,1},{4,0},{5,7},{6,2},{7,5},{8,12},{9,11},{10,... | collective-permute-start | bytes 958472 | tf_op jit(solution)/shard_map/ppermute | solution.py:223
  23.4 3.1 %collective-permute-done.9 = bf16[624,128]{1,0:T(8,128)(2,1)S(1)} collective-permute-done((bf16[624,128]{1,0:T(8,128)(2,1)S(1)}, bf16[624,128]{1,0:T(8,128)(2,1)S(1)}, u32[]{:S(2)}, u32[]{:S(2)}) %collective-permute-start.9) | collective-permute-done | bytes 159776 | tf_op jit(solution)/shard_map/ppermute | solution.py:223
  26.6 0.1 fusion.1
  26.6 2.3 %collective-permute-start.10 = (bf16[624,128]{1,0:T(8,128)(2,1)S(1)}, bf16[624,128]{1,0:T(8,128)(2,1)S(1)}, u32[]{:S(2)}, u32[]{:S(2)}) collective-permute-start(bf16[624,128]{1,0:T(8,128)(2,1)S(1)} %fusion.1), channel_id=1, source_target_pairs={{0,8},{1,17},{2,10},{3,19},{4,12},{5,21},{6,14},{7,23},{8,0},{9,25... | collective-permute-start | bytes 479240 | tf_op jit(solution)/shard_map/ppermute | solution.py:223
  28.9 0.0 collective-permute-done.1
  29.0 1.6 %collective-permute-start.2 = (bf16[624,128]{1,0:T(8,128)(2,1)S(1)}, bf16[624,128]{1,0:T(8,128)(2,1)S(1)}, u32[]{:S(2)}, u32[]{:S(2)}) collective-permute-start(bf16[624,128]{1,0:T(8,128)(2,1)S(1)} %add_convert_fusion.3), channel_id=1, source_target_pairs={{0,2},{1,5},{2,0},{3,7},{4,6},{5,1},{6,4},{7,3},{8,10},{9,13},{10,... | collective-permute-start | bytes 479240 | tf_op jit(solution)/shard_map/ppermute | solution.py:223
  30.5 1.8 %collective-permute-done.10 = bf16[624,128]{1,0:T(8,128)(2,1)S(1)} collective-permute-done((bf16[624,128]{1,0:T(8,128)(2,1)S(1)}, bf16[624,128]{1,0:T(8,128)(2,1)S(1)}, u32[]{:S(2)}, u32[]{:S(2)}) %collective-permute-start.10) | collective-permute-done | bytes 159776 | tf_op jit(solution)/shard_map/ppermute | solution.py:223
  32.3 0.1 reduce-precision_convert_fusion.refs_1_
  32.4 0.0 copy-start.7
  32.4 2.9 %collective-permute-start.11 = (bf16[624,128]{1,0:T(8,128)(2,1)S(1)}, bf16[624,128]{1,0:T(8,128)(2,1)S(1)}, u32[]{:S(2)}, u32[]{:S(2)}) collective-permute-start(bf16[624,128]{1,0:T(8,128)(2,1)S(1)} %reduce-precision_convert_fusion.refs_1_), channel_id=1, source_target_pairs={{0,16},{1,9},{2,18},{3,11},{4,20},{5,13},{6,22},{7,15},{8,24},{9,1... | collective-permute-start | bytes 479240 | tf_op jit(solution)/shard_map/ppermute | solution.py:223
  35.3 0.1 fusion
  35.4 1.6 %collective-permute-start.3 = (bf16[624,128]{1,0:T(8,128)(2,1)S(1)}, bf16[624,128]{1,0:T(8,128)(2,1)S(1)}, u32[]{:S(2)}, u32[]{:S(2)}) collective-permute-start(bf16[624,128]{1,0:T(8,128)(2,1)S(1)} %fusion), channel_id=1, source_target_pairs={{0,8},{1,17},{2,10},{3,19},{4,12},{5,21},{6,14},{7,23},{8,0},{9,25... | collective-permute-start | bytes 479240 | tf_op jit(solution)/shard_map/ppermute | solution.py:223
  37.0 6.5 %collective-permute-done.11.refs_2_ = bf16[624,128]{1,0:T(8,128)(2,1)S(1)} collective-permute-done((bf16[624,128]{1,0:T(8,128)(2,1)S(1)}, bf16[624,128]{1,0:T(8,128)(2,1)S(1)}, u32[]{:S(2)}, u32[]{:S(2)}) %collective-permute-start.11) | collective-permute-done | bytes 159776 | tf_op jit(solution)/shard_map/ppermute | solution.py:223
  43.6 0.7 copy-done.9
  44.2 2.3 %shard_map.44 = bf16[640,128]{1,0:T(8,128)(2,1)} custom-call(s32[1]{0:T(128)} %bitcast.3.refs_0_, bf16[624,128]{1,0:T(8,128)(2,1)} %copy-done.7, bf16[624,128]{1,0:T(8,128)(2,1)} %copy-done.9), custom_call_target="tpu_custom_call" | custom-call | tf_op jit(solution)/shard_map/pallas_call | solution.py:110
  46.5 1.3 %collective-permute-start.12 = (bf16[640,128]{1,0:T(8,128)(2,1)}, bf16[640,128]{1,0:T(8,128)(2,1)S(1)}, u32[]{:S(2)}, u32[]{:S(2)}) collective-permute-start(bf16[640,128]{1,0:T(8,128)(2,1)} %shard_map.44), channel_id=1, source_target_pairs={{0,2},{1,5},{2,0},{3,7},{4,6},{5,1},{6,4},{7,3},{8,10},{9,13},{10,... | collective-permute-start | bytes 491528 | tf_op jit(solution)/shard_map/ppermute | solution.py:223
  47.8 0.1 reduce-precision_convert_fusion.1.refs_1_
  47.9 0.1 collective-permute-start.4
  48.0 7.9 %collective-permute-done.4.refs_2_ = bf16[624,128]{1,0:T(8,128)(2,1)S(1)} collective-permute-done((bf16[624,128]{1,0:T(8,128)(2,1)S(1)}, bf16[624,128]{1,0:T(8,128)(2,1)S(1)}, u32[]{:S(2)}, u32[]{:S(2)}) %collective-permute-start.4) | collective-permute-done | bytes 159776 | tf_op jit(solution)/shard_map/ppermute | solution.py:223
  55.9 0.7 copy-done.10
  56.6 2.3 %shard_map.43 = bf16[640,128]{1,0:T(8,128)(2,1)} custom-call(s32[1]{0:T(128)} %bitcast.2.refs_0_, bf16[624,128]{1,0:T(8,128)(2,1)} %copy-done.8, bf16[624,128]{1,0:T(8,128)(2,1)} %copy-done.10), custom_call_target="tpu_custom_call" | custom-call | tf_op jit(solution)/shard_map/pallas_call | solution.py:110
  58.9 0.7 collective-permute-start.5
  59.7 0.7 collective-permute-start.13
  60.4 4.0 %collective-permute-done.5 = bf16[640,128]{1,0:T(8,128)(2,1)S(1)} collective-permute-done((bf16[640,128]{1,0:T(8,128)(2,1)}, bf16[640,128]{1,0:T(8,128)(2,1)S(1)}, u32[]{:S(2)}, u32[]{:S(2)}) %collective-permute-start.5) | collective-permute-done | bytes 163872 | tf_op jit(solution)/shard_map/ppermute | solution.py:223
  64.5 1.0 %collective-permute-start.6 = (bf16[1280,128]{1,0:T(8,128)(2,1)S(1)}, bf16[1280,128]{1,0:T(8,128)(2,1)S(1)}, u32[]{:S(2)}, u32[]{:S(2)}) collective-permute-start(bf16[1280,128]{1,0:T(8,128)(2,1)S(1)} %pad_maximum_fusion.2), channel_id=1, source_target_pairs={{0,4},{1,3},{2,6},{3,1},{4,0},{5,7},{6,2},{7,5},{8,12},{9,11},{10,... | collective-permute-start | bytes 983048 | tf_op jit(solution)/shard_map/ppermute | solution.py:223
  65.5 1.3 %collective-permute-done.13 = bf16[1280,128]{1,0:T(8,128)(2,1)S(1)} collective-permute-done((bf16[1280,128]{1,0:T(8,128)(2,1)S(1)}, bf16[1280,128]{1,0:T(8,128)(2,1)S(1)}, u32[]{:S(2)}, u32[]{:S(2)}) %collective-permute-start.13) | collective-permute-done | bytes 327712 | tf_op jit(solution)/shard_map/ppermute | solution.py:223
  66.8 0.1 broadcast_select_fusion.1
  67.0 0.1 collective-permute-start.15
  67.1 4.5 %collective-permute-done.6 = bf16[1280,128]{1,0:T(8,128)(2,1)S(1)} collective-permute-done((bf16[1280,128]{1,0:T(8,128)(2,1)S(1)}, bf16[1280,128]{1,0:T(8,128)(2,1)S(1)}, u32[]{:S(2)}, u32[]{:S(2)}) %collective-permute-start.6) | collective-permute-done | bytes 327712 | tf_op jit(solution)/shard_map/ppermute | solution.py:223
  71.6 0.1 broadcast_select_fusion.3
  71.8 0.0 copy-start.1
  71.8 0.1 collective-permute-start.14
  71.9 0.7 copy-done.1
  72.7 5.7 %shard_map.45.refs_2_ = f32[1536,512]{1,0:T(8,128)} custom-call(s32[1]{0:T(128)} %bitcast.1.refs_0_, bf16[1536,512]{1,0:T(8,128)(2,1)} %refs_1_.7, bf16[1536,512]{1,0:T(8,128)(2,1)} %refs_2_.5, bf16[2560,128]{1,0:T(8,128)(2,1)} %copy-done.1, bf16[2560,128]{1,0:T(8,128)(2,1)} %copy-done), custom_call_target="tpu_custom_call" | custom-call | tf_op jit(solution)/shard_map/pallas_call | solution.py:185
  78.3 1.4 %convert_reduce_fusion.2 = (f32[]{:T(128)}, f32[]{:T(128)}) fusion(bf16[4,640,128]{2,1,0:T(8,128)(2,1)} %bitcast.9, bf16[4,640,128]{2,1,0:T(8,128)(2,1)} %bitcast.10), kind=kLoop, calls=%fused_computation.26 | loop fusion | flops 46 | bytes 56 | tf_op jit(solution)/shard_map/reduce_sum | solution.py:269
  81.0 0.7 convert_reduce_fusion
  81.7 0.7 convert_reduce_fusion.1
  83.7 6.2 %shard_map.46 = f32[1536,512]{1,0:T(8,128)} custom-call(s32[1]{0:T(128)} %bitcast.refs_0_, bf16[1536,512]{1,0:T(8,128)(2,1)} %refs_1_.7, f32[1536,512]{1,0:T(8,128)} %shard_map.45.refs_2_, bf16[2560,128]{1,0:T(8,128)(2,1)} %copy-done.3, bf16[2560,128]{1,0:T(8,128)(2,1)} %copy-done.2), custom_call_target="tpu_custom_call" | custom-call | tf_op jit(solution)/shard_map/pallas_call | solution.py:185
  (31 shorter events, 0.3 us)
Async XLA Ops:
  5.2 5.1 %collective-permute-start.7 = (bf16[2496,128]{1,0:T(8,128)(2,1)}, bf16[2496,128]{1,0:T(8,128)(2,1)S(1)}, u32[]{:S(2)}, u32[]{:S(2)}) collective-permute-start(bf16[2496,128]{1,0:T(8,128)(2,1)} %get-tuple-element.9), channel_id=1, source_target_pairs={{0,1},{1,0},{2,3},{3,2},{4,5},{5,4},{6,7},{7,6},{8,9},{9,8},{10,11... | collective-permute-start | bytes 1916936 | tf_op jit(solution)/shard_map/ppermute | solution.py:223
  5.7 16.0 %collective-permute-start = (bf16[2496,128]{1,0:T(8,128)(2,1)}, bf16[2496,128]{1,0:T(8,128)(2,1)S(1)}, u32[]{:S(2)}, u32[]{:S(2)}) collective-permute-start(bf16[2496,128]{1,0:T(8,128)(2,1)} %get-tuple-element.7), channel_id=1, source_target_pairs={{0,1},{1,0},{2,3},{3,2},{4,5},{5,4},{6,7},{7,6},{8,9},{9,8},{10,11... | collective-permute-start | bytes 1916936 | tf_op jit(solution)/shard_map/ppermute | solution.py:223
  10.3 11.4 %copy-start.6 = (bf16[2496,128]{1,0:T(8,128)(2,1)S(1)}, bf16[2496,128]{1,0:T(8,128)(2,1)}, u32[]{:S(2)}) copy-start(bf16[2496,128]{1,0:T(8,128)(2,1)} %get-tuple-element.6) | copy-start | bytes 1916932
  11.6 8.0 %collective-permute-start.8 = (bf16[1248,128]{1,0:T(8,128)(2,1)S(1)}, bf16[1248,128]{1,0:T(8,128)(2,1)S(1)}, u32[]{:S(2)}, u32[]{:S(2)}) collective-permute-start(bf16[1248,128]{1,0:T(8,128)(2,1)S(1)} %get-tuple-element.10), channel_id=1, source_target_pairs={{0,4},{1,3},{2,6},{3,1},{4,0},{5,7},{6,2},{7,5},{8,12},{9,11},{10,... | collective-permute-start | bytes 958472 | tf_op jit(solution)/shard_map/ppermute | solution.py:223
  19.6 6.9 %collective-permute-start.9 = (bf16[624,128]{1,0:T(8,128)(2,1)S(1)}, bf16[624,128]{1,0:T(8,128)(2,1)S(1)}, u32[]{:S(2)}, u32[]{:S(2)}) collective-permute-start(bf16[624,128]{1,0:T(8,128)(2,1)S(1)} %add_convert_fusion.2), channel_id=1, source_target_pairs={{0,2},{1,5},{2,0},{3,7},{4,6},{5,1},{6,4},{7,3},{8,10},{9,13},{10,... | collective-permute-start | bytes 479240 | tf_op jit(solution)/shard_map/ppermute | solution.py:223
  21.9 7.1 %collective-permute-start.1 = (bf16[1248,128]{1,0:T(8,128)(2,1)S(1)}, bf16[1248,128]{1,0:T(8,128)(2,1)S(1)}, u32[]{:S(2)}, u32[]{:S(2)}) collective-permute-start(bf16[1248,128]{1,0:T(8,128)(2,1)S(1)} %get-tuple-element.12), channel_id=1, source_target_pairs={{0,4},{1,3},{2,6},{3,1},{4,0},{5,7},{6,2},{7,5},{8,12},{9,11},{10,... | collective-permute-start | bytes 958472 | tf_op jit(solution)/shard_map/ppermute | solution.py:223
  26.6 5.7 %collective-permute-start.10 = (bf16[624,128]{1,0:T(8,128)(2,1)S(1)}, bf16[624,128]{1,0:T(8,128)(2,1)S(1)}, u32[]{:S(2)}, u32[]{:S(2)}) collective-permute-start(bf16[624,128]{1,0:T(8,128)(2,1)S(1)} %fusion.1), channel_id=1, source_target_pairs={{0,8},{1,17},{2,10},{3,19},{4,12},{5,21},{6,14},{7,23},{8,0},{9,25... | collective-permute-start | bytes 479240 | tf_op jit(solution)/shard_map/ppermute | solution.py:223
  29.0 6.4 %collective-permute-start.2 = (bf16[624,128]{1,0:T(8,128)(2,1)S(1)}, bf16[624,128]{1,0:T(8,128)(2,1)S(1)}, u32[]{:S(2)}, u32[]{:S(2)}) collective-permute-start(bf16[624,128]{1,0:T(8,128)(2,1)S(1)} %add_convert_fusion.3), channel_id=1, source_target_pairs={{0,2},{1,5},{2,0},{3,7},{4,6},{5,1},{6,4},{7,3},{8,10},{9,13},{10,... | collective-permute-start | bytes 479240 | tf_op jit(solution)/shard_map/ppermute | solution.py:223
  32.4 11.2 %copy-start.7 = (bf16[624,128]{1,0:T(8,128)(2,1)}, bf16[624,128]{1,0:T(8,128)(2,1)S(1)}, u32[]{:S(2)}) copy-start(bf16[624,128]{1,0:T(8,128)(2,1)S(1)} %reduce-precision_convert_fusion.refs_1_) | copy-start | bytes 479236
  32.4 11.1 %collective-permute-start.11 = (bf16[624,128]{1,0:T(8,128)(2,1)S(1)}, bf16[624,128]{1,0:T(8,128)(2,1)S(1)}, u32[]{:S(2)}, u32[]{:S(2)}) collective-permute-start(bf16[624,128]{1,0:T(8,128)(2,1)S(1)} %reduce-precision_convert_fusion.refs_1_), channel_id=1, source_target_pairs={{0,16},{1,9},{2,18},{3,11},{4,20},{5,13},{6,22},{7,15},{8,24},{9,1... | collective-permute-start | bytes 479240 | tf_op jit(solution)/shard_map/ppermute | solution.py:223
  35.4 12.4 %collective-permute-start.3 = (bf16[624,128]{1,0:T(8,128)(2,1)S(1)}, bf16[624,128]{1,0:T(8,128)(2,1)S(1)}, u32[]{:S(2)}, u32[]{:S(2)}) collective-permute-start(bf16[624,128]{1,0:T(8,128)(2,1)S(1)} %fusion), channel_id=1, source_target_pairs={{0,8},{1,17},{2,10},{3,19},{4,12},{5,21},{6,14},{7,23},{8,0},{9,25... | collective-permute-start | bytes 479240 | tf_op jit(solution)/shard_map/ppermute | solution.py:223
  43.6 0.7 copy-start.9
  46.5 13.1 %copy-start.4 = (bf16[640,128]{1,0:T(8,128)(2,1)S(1)}, bf16[640,128]{1,0:T(8,128)(2,1)}, u32[]{:S(2)}) copy-start(bf16[640,128]{1,0:T(8,128)(2,1)} %shard_map.44) | copy-start | bytes 491524
  46.5 13.1 %collective-permute-start.12 = (bf16[640,128]{1,0:T(8,128)(2,1)}, bf16[640,128]{1,0:T(8,128)(2,1)S(1)}, u32[]{:S(2)}, u32[]{:S(2)}) collective-permute-start(bf16[640,128]{1,0:T(8,128)(2,1)} %shard_map.44), channel_id=1, source_target_pairs={{0,2},{1,5},{2,0},{3,7},{4,6},{5,1},{6,4},{7,3},{8,10},{9,13},{10,... | collective-permute-start | bytes 491528 | tf_op jit(solution)/shard_map/ppermute | solution.py:223
  47.9 8.0 %copy-start.8 = (bf16[624,128]{1,0:T(8,128)(2,1)}, bf16[624,128]{1,0:T(8,128)(2,1)S(1)}, u32[]{:S(2)}) copy-start(bf16[624,128]{1,0:T(8,128)(2,1)S(1)} %reduce-precision_convert_fusion.1.refs_1_) | copy-start | bytes 479236
  47.9 8.0 %collective-permute-start.4 = (bf16[624,128]{1,0:T(8,128)(2,1)S(1)}, bf16[624,128]{1,0:T(8,128)(2,1)S(1)}, u32[]{:S(2)}, u32[]{:S(2)}) collective-permute-start(bf16[624,128]{1,0:T(8,128)(2,1)S(1)} %reduce-precision_convert_fusion.1.refs_1_), channel_id=1, source_target_pairs={{0,16},{1,9},{2,18},{3,11},{4,20},{5,13},{6,22},{7,15},{8,24},{9,1... | collective-permute-start | bytes 479240 | tf_op jit(solution)/shard_map/ppermute | solution.py:223
  55.9 0.7 copy-start.10
  58.9 5.5 %copy-start.5 = (bf16[640,128]{1,0:T(8,128)(2,1)S(1)}, bf16[640,128]{1,0:T(8,128)(2,1)}, u32[]{:S(2)}) copy-start(bf16[640,128]{1,0:T(8,128)(2,1)} %shard_map.43) | copy-start | bytes 491524
  58.9 5.5 %collective-permute-start.5 = (bf16[640,128]{1,0:T(8,128)(2,1)}, bf16[640,128]{1,0:T(8,128)(2,1)S(1)}, u32[]{:S(2)}, u32[]{:S(2)}) collective-permute-start(bf16[640,128]{1,0:T(8,128)(2,1)} %shard_map.43), channel_id=1, source_target_pairs={{0,2},{1,5},{2,0},{3,7},{4,6},{5,1},{6,4},{7,3},{8,10},{9,13},{10,... | collective-permute-start | bytes 491528 | tf_op jit(solution)/shard_map/ppermute | solution.py:223
  59.7 7.1 %collective-permute-start.13 = (bf16[1280,128]{1,0:T(8,128)(2,1)S(1)}, bf16[1280,128]{1,0:T(8,128)(2,1)S(1)}, u32[]{:S(2)}, u32[]{:S(2)}) collective-permute-start(bf16[1280,128]{1,0:T(8,128)(2,1)S(1)} %pad_maximum_fusion.3), channel_id=1, source_target_pairs={{0,4},{1,3},{2,6},{3,1},{4,0},{5,7},{6,2},{7,5},{8,12},{9,11},{10,... | collective-permute-start | bytes 983048 | tf_op jit(solution)/shard_map/ppermute | solution.py:223
  64.5 7.1 %collective-permute-start.6 = (bf16[1280,128]{1,0:T(8,128)(2,1)S(1)}, bf16[1280,128]{1,0:T(8,128)(2,1)S(1)}, u32[]{:S(2)}, u32[]{:S(2)}) collective-permute-start(bf16[1280,128]{1,0:T(8,128)(2,1)S(1)} %pad_maximum_fusion.2), channel_id=1, source_target_pairs={{0,4},{1,3},{2,6},{3,1},{4,0},{5,7},{6,2},{7,5},{8,12},{9,11},{10,... | collective-permute-start | bytes 983048 | tf_op jit(solution)/shard_map/ppermute | solution.py:223
  67.0 4.9 %copy-start = (bf16[2560,128]{1,0:T(8,128)(2,1)}, bf16[2560,128]{1,0:T(8,128)(2,1)S(1)}, u32[]{:S(2)}) copy-start(bf16[2560,128]{1,0:T(8,128)(2,1)S(1)} %pad_maximum_fusion.1.refs_4_) | copy-start | bytes 1966084
  67.0 13.9 %collective-permute-start.15 = (bf16[2560,128]{1,0:T(8,128)(2,1)S(1)}, bf16[2560,128]{1,0:T(8,128)(2,1)S(1)}, u32[]{:S(2)}, u32[]{:S(2)}) collective-permute-start(bf16[2560,128]{1,0:T(8,128)(2,1)S(1)} %pad_maximum_fusion.1.refs_4_), channel_id=1, source_target_pairs={{0,1},{1,0},{2,3},{3,2},{4,5},{5,4},{6,7},{7,6},{8,9},{9,8},{10,11... | collective-permute-start | bytes 1966088 | tf_op jit(solution)/shard_map/ppermute | solution.py:223
  71.8 0.8 copy-start.1
  71.8 9.8 %collective-permute-start.14 = (bf16[2560,128]{1,0:T(8,128)(2,1)S(1)}, bf16[2560,128]{1,0:T(8,128)(2,1)S(1)}, u32[]{:S(2)}, u32[]{:S(2)}) collective-permute-start(bf16[2560,128]{1,0:T(8,128)(2,1)S(1)} %pad_maximum_fusion.refs_3_), channel_id=1, source_target_pairs={{0,1},{1,0},{2,3},{3,2},{4,5},{5,4},{6,7},{7,6},{8,9},{9,8},{10,11... | collective-permute-start | bytes 1966088 | tf_op jit(solution)/shard_map/ppermute | solution.py:223
  80.9 2.8 %copy-start.2 = (bf16[2560,128]{1,0:T(8,128)(2,1)}, bf16[2560,128]{1,0:T(8,128)(2,1)S(1)}, u32[]{:S(2)}) copy-start(bf16[2560,128]{1,0:T(8,128)(2,1)S(1)} %collective-permute-done.15.refs_4_) | copy-start | bytes 1966084
  81.7 2.1 %copy-start.3 = (bf16[2560,128]{1,0:T(8,128)(2,1)}, bf16[2560,128]{1,0:T(8,128)(2,1)S(1)}, u32[]{:S(2)}) copy-start(bf16[2560,128]{1,0:T(8,128)(2,1)S(1)} %collective-permute-done.14.refs_3_) | copy-start | bytes 1966084

commit v2 on v0

v2 whole, which is shorter than its diff:
```python
import jax
import jax.numpy as jnp
from jax import lax
from jax.experimental import pallas as pl
from jax.experimental.pallas import tpu as pltpu
from jax.sharding import PartitionSpec as P


TILE = 128
PAD = 16
SHARES = 4
AXES = ("gr", "gc")
BF16 = jnp.bfloat16
F32 = jnp.float32
VMEM = pl.BlockSpec(memory_space=pltpu.VMEM)
SMEM = pl.BlockSpec(memory_space=pltpu.SMEM)
DIMS = (((1,), (1,)), ((), ()))


def params(mib):
    return pltpu.CompilerParams(vmem_limit_bytes=mib * 2**20)


def layout(total_rows):
    side = total_rows // TILE // 2
    extra = side // 2
    near = [(i, j) for i in range(side) for j in range(i, side)]
    far = [(i, j) for i in range(side) for j in range(i)]
    near_at = {ij: n for n, ij in enumerate(near)}
    far_at = {ij: n for n, ij in enumerate(far)}
    return side, extra, near_at, far_at


def starts(half_ref, side):
    h = half_ref[0]
    low = pl.multiple_of(h * (side * TILE), TILE)
    up = pl.multiple_of((1 - h) * (side * TILE), TILE)
    return h, low, up


def symmetric(orb_ref, vel_ref, r0, rows, c0, cols):
    one = lax.dot_general(
        orb_ref[pl.ds(r0, rows), :], vel_ref[pl.ds(c0, cols), :], DIMS, preferred_element_type=F32
    )
    two = lax.dot_general(
        vel_ref[pl.ds(r0, rows), :], orb_ref[pl.ds(c0, cols), :], DIMS, preferred_element_type=F32
    )
    return one + two


def product_kernel(half_ref, orb_ref, vel_ref, out_ref, *, chunk, total_rows):
    side, extra, near_at, far_at = layout(total_rows)
    h, low, up = starts(half_ref, side)
    table = far_at if chunk else near_at
    for c in range(0, side, 2):
        columns = [j for j in (c, c + 1) if j < side]
        rows = [i for i in range(side) if any((i, j) in table for j in columns)]
        columns = [j for j in columns if any((i, j) in table for i in rows)]
        if not rows:
            continue
        value = symmetric(
            orb_ref,
            vel_ref,
            low + rows[0] * TILE,
            len(rows) * TILE,
            (up if chunk else low) + columns[0] * TILE,
            len(columns) * TILE,
        )
        for i in rows:
            for j in columns:
                if (i, j) in table:
                    at = table[(i, j)] * TILE
                    row, col = (i - rows[0]) * TILE, (j - columns[0]) * TILE
                    out_ref[at : at + TILE, :] = value[row : row + TILE, col : col + TILE].astype(BF16)
    if chunk:
        for k in range(extra):
            shift = pl.multiple_of((h * extra + k) * TILE, TILE)
            at = (len(far_at) + k) * TILE
            value = symmetric(orb_ref, vel_ref, low + shift, TILE, up + shift, TILE)
            out_ref[at : at + TILE, :] = value.astype(BF16)


def tile_count(chunk, total_rows):
    _, extra, near_at, far_at = layout(total_rows)
    return len(far_at) + extra if chunk else len(near_at)


def product(half, orb, vel, chunk):
    rows = orb.shape[0]
    return pl.pallas_call(
        lambda *refs: product_kernel(*refs, chunk=chunk, total_rows=rows),
        out_shape=jax.ShapeDtypeStruct((tile_count(chunk, rows) * TILE, TILE), BF16),
        in_specs=[SMEM, VMEM, VMEM],
        out_specs=VMEM,
        compiler_params=params(16),
    )(half, orb, vel)


def share_kernel(off_ref, a_ref, b_ref, out_ref, *, diagonal):
    rows = a_ref.shape[0]
    total = a_ref[...].astype(F32) + b_ref[...].astype(F32)
    out_ref[0:rows, :] = total.astype(BF16)
    square = total * total
    if diagonal:
        tile = (lax.broadcasted_iota(jnp.int32, (rows, TILE), 0) + off_ref[0]) // TILE
        single = tile == diagonal[0]
        for at in diagonal[1:]:
            single |= tile == at
        square = jnp.where(single, square, 2.0 * square)
    else:
        square = 2.0 * square
    square = jnp.sum(jnp.sum(square, axis=0, keepdims=True), axis=1, keepdims=True)
    high = square.astype(BF16).astype(F32)
    rest = square - high
    middle = rest.astype(BF16).astype(F32)
    small = rest - middle
    line = lax.broadcasted_iota(jnp.int32, (PAD, TILE), 0)
    tail = jnp.where(line == 0, high, jnp.where(line == 1, middle, jnp.where(line == 2, small, 0.0)))
    out_ref[rows : rows + PAD, :] = tail.astype(BF16)


def make_share(offset, a, b, diagonal):
    rows = a.shape[0]
    return pl.pallas_call(
        lambda *refs: share_kernel(*refs, diagonal=diagonal),
        out_shape=jax.ShapeDtypeStruct((rows + PAD, TILE), BF16),
        in_specs=[SMEM, VMEM, VMEM],
        out_specs=VMEM,
        compiler_params=params(4),
    )(offset, a, b)


def take_tile(ref, index):
    share_rows = ref.shape[0] // SHARES - PAD
    row, end = index * TILE, (index + 1) * TILE
    parts = []
    while row < end:
        share = row // share_rows
        stop = min(end, (share + 1) * share_rows)
        parts.append(ref[row + share * PAD : stop + share * PAD, :])
        row = stop
    return parts[0] if len(parts) == 1 else jnp.concatenate(parts, axis=0)


def put_block(ref, i, j, value):
    ref[i * TILE : (i + 1) * TILE, j * TILE : (j + 1) * TILE] = value


def near_kernel(half_ref, orb_ref, vel_ref, own_ref, far_ref, out_ref, a_ref):
    side, _, near_at, _ = layout(orb_ref.shape[0])
    wide = side * TILE
    _, low, up = starts(half_ref, side)
    for ref, at, n in ((own_ref, low, 0), (far_ref, up, 1)):
        for (i, j), index in near_at.items():
            value = take_tile(ref, index)
            put_block(a_ref, i + n * side, j, value)
            if i != j:
                put_block(a_ref, j + n * side, i, value.T)
        value = jnp.dot(
            a_ref[n * wide : (n + 1) * wide, :], orb_ref[pl.ds(at, wide), :], preferred_element_type=F32
        )
        out_ref[pl.ds(at, wide), :] = vel_ref[pl.ds(at, wide), :].astype(F32) - 0.5 * value


def apply_near(half, orb, vel, own, far):
    wide = orb.shape[0] // 2
    return pl.pallas_call(
        near_kernel,
        out_shape=jax.ShapeDtypeStruct(orb.shape, F32),
        in_specs=[SMEM] + [VMEM] * 4,
        out_specs=VMEM,
        scratch_shapes=[pltpu.VMEM((2 * wide, wide), BF16)],
        compiler_params=params(20),
    )(half, orb, vel, own, far)


def tails(ref):
    share = ref.shape[0] // SHARES
    total = jnp.zeros((1, TILE), F32)
    for k in range(SHARES):
        lines = ref[(k + 1) * share - PAD : (k + 1) * share, :].astype(F32)
        total = total + jnp.sum(lines, axis=0, keepdims=True)
    return total


def far_kernel(half_ref, orb_ref, base_ref, piece_ref, *refs):
    total_rows = orb_ref.shape[0]
    side, extra, _, far_at = layout(total_rows)
    h, low, up = starts(half_ref, side)
    out_ref, b_ref, t_ref = refs[-3:]
    if len(refs) > 3:
        near_own, near_far, own, out_ref, norm_ref = refs[:5]
        square = (tails(near_own) + tails(own)) + (tails(near_far) + tails(piece_ref))
        norm_ref[0] = (jnp.sqrt(square) / total_rows)[0, 0]
    zero = jnp.zeros((TILE, TILE), BF16)
    for i in range(side):
        for j in range(i, i - i % 2 + 2):
            if j < side:
                put_block(b_ref, i, j, zero)
                put_block(t_ref, j, i, zero)
    for (i, j), index in far_at.items():
        value = take_tile(piece_ref, index)
        put_block(b_ref, i, j, value)
        put_block(t_ref, j, i, value.T)
    for k in range(extra):
        value = take_tile(piece_ref, len(far_at) + k)
        at = pl.multiple_of((h * extra + k) * TILE, TILE)
        b_ref[pl.ds(at, TILE), pl.ds(at, TILE)] = value
        t_ref[pl.ds(at, TILE), pl.ds(at, TILE)] = value.T
    wide = side * TILE
    panel = 2 * TILE
    for p in range(0, wide, panel):
        end = min(p + panel, wide)
        value = jnp.dot(b_ref[p:end, :end], orb_ref[pl.ds(up, end), :], preferred_element_type=F32)
        at = pl.ds(low + p, end - p)
        out_ref[at, :] = base_ref[at, :] - 0.5 * value
        value = jnp.dot(t_ref[p:end, p:], orb_ref[pl.ds(low + p, wide - p), :], preferred_element_type=F32)
        at = pl.ds(up + p, end - p)
        out_ref[at, :] = base_ref[at, :] - 0.5 * value


def apply_far(half, orb, base, piece, others=()):
    wide = orb.shape[0] // 2
    out_shape = [jax.ShapeDtypeStruct(orb.shape, F32)]
    out_specs = [VMEM]
    if others:
        out_shape.append(jax.ShapeDtypeStruct((1,), F32))
        out_specs.append(SMEM)
    return pl.pallas_call(
        far_kernel,
        out_shape=out_shape,
        in_specs=[SMEM] + [VMEM] * (3 + len(others)),
        out_specs=out_specs,
        scratch_shapes=[pltpu.VMEM((wide, wide), BF16)] * 2,
        compiler_params=params(20),
    )(half, orb, base, piece, *others)


def pairs(nr, nc, even, odd):
    result = []
    for r in range(nr):
        for c in range(nc):
            flip = odd if c & 1 else even
            result.append((r * nc + c, (r ^ flip[0]) * nc + (c ^ flip[1])))
    return result


def local(orbitals, velocities):
    nr, nc = lax.axis_size("gr"), lax.axis_size("gc")
    r, c = lax.axis_index("gr"), lax.axis_index("gc")
    side, _, near_at, _ = layout(orbitals.shape[0])
    core = c & 1
    on_r, on_c = r & 1, (c >> 1) & 1
    bit1 = jnp.where(core == 0, on_r, on_c)
    bit2 = jnp.where(core == 0, on_c, on_r)
    swap = pairs(nr, nc, (0, 1), (0, 1))
    first = pairs(nr, nc, (1, 0), (0, 2))
    second = pairs(nr, nc, (0, 2), (1, 0))
    rest = [(1 << b, 0) for b in range(1, nr.bit_length() - 1)]
    rest += [(0, 1 << b) for b in range(2, nc.bit_length() - 1)]
    doubling = [pairs(nr, nc, rest[k], rest[-1 - k]) for k in range(len(rest))]
    diagonals = [[near_at[(i, i)] for i in range(side)], []]

    def move(value, perm):
        return lax.ppermute(value, AXES, perm)

    def cut(value, index, rows):
        return lax.dynamic_slice_in_dim(value, index * rows, rows, 0).astype(F32)

    def rounded(value):
        return lax.reduce_precision(value, 8, 7)

    def join(bit, mine, got):
        return jnp.concatenate([jnp.where(bit == 0, mine, got), jnp.where(bit == 0, got, mine)], axis=0)

    own = core.reshape(1)
    other = (1 - core).reshape(1)
    joined = []
    for k in range(2):
        away = product(other, orbitals, velocities, k)
        got = move(away, swap)
        mine = product(own, orbitals, velocities, k)
        rows = mine.shape[0]
        half, quarter = rows // 2, rows // 4
        send = (cut(mine, 1 - bit1, half) + cut(got, 1 - bit1, half)).astype(BF16)
        mine1 = cut(mine, bit1, half) + cut(got, bit1, half)
        got1 = move(send, first)
        send = (cut(mine1, 1 - bit2, quarter) + cut(got1, 1 - bit2, quarter)).astype(BF16)
        mine2 = cut(mine1, bit2, quarter) + cut(got1, bit2, quarter)
        got2 = move(send, second)
        total = rounded(mine2 + got2.astype(F32))
        for j, perm in enumerate(doubling):
            sent = total.astype(BF16)
            back = move(sent, perm)
            if j < len(doubling) - 1:
                total = rounded(total + back.astype(F32))
        share = make_share((bit1 * half + bit2 * quarter).reshape(1), sent, back, diagonals[k])
        back = move(share, second)
        quarter = join(bit2, share, back)
        back = move(quarter, first)
        joined.append(join(bit1, quarter, back))
    far = [move(joined[k], swap) for k in range(2)]
    new = apply_near(own, orbitals, velocities, joined[0], far[0])
    (new,) = apply_far(own, orbitals, new, joined[1])
    new, measured = apply_far(other, orbitals, new, far[1], (joined[0], far[0], joined[1]))
    return new, measured


def solution(mesh):
    in_specs = (P(None, AXES), P(None, AXES))
    out_specs = (P(None, AXES), P())

    return jax.shard_map(local, mesh=mesh, in_specs=in_specs, out_specs=out_specs, check_vma=False)
```

time: 297 us -> 79.4 us (0.27)
  waiting for transfers between devices: 136 us -> 30.9 us
  local copies, waits for them, and re-layouts: 61.7 us -> 4.54 us
  blocking collectives: 40.2 us -> 0 us
  matrix products: 25.9 us -> 0 us
  starting transfers between devices: 0.08 us -> 18.4 us
  between operations: 16 us -> 0.79 us
  Pallas kernels: 0 us -> 12.4 us
  other arithmetic: 15.6 us -> 12.2 us
    unnamed x3 -> x0, waiting for transfers between devices: 126 us -> none
    psum x1 -> x0, blocking collectives: 40.2 us -> none  [local(): summed = lax.psum(local_sq, ('gr', 'gc'))]
    ppermute x0 -> x16, waiting for transfers between devices: none -> 30.9 us  [move(): return lax.ppermute(value, AXES, perm)]
    dot_general x5 -> x0, matrix products: 25.9 us -> none  [the longest x1 6.63 us: local(): carry = carry + jnp.einsum('jkq,jkbg->qbg', col_hot, mirrored)]
    reshape x2 -> x0, local copies, waits for them, and re-layouts: 25.3 us -> none  [local(): sym_four = sym_local.reshape(row_groups, edge, row_groups, edge)]
    ppermute x0 -> x16, starting transfers between devices: none -> 18.4 us  [move(): return lax.ppermute(value, AXES, perm)]
    gather x3 -> x0, local copies, waits for them, and re-layouts: 16.5 us -> none  [the longest x1 9.02 us: local(): sym_four[every_row[:, None], :, every_col, :]]
    pallas_call x0 -> x9, Pallas kernels: none -> 12.4 us  [the longest x4 5.71 us: product(): pl.pallas_call(lambda *refs: product_kernel(*refs, chunk=chunk, total_row...]
  transfers between devices with their start and end apart: 2 -> 16, of which waited for: 2 -> 10; matrix products, arithmetic and copies ran while one was open for 3% -> 15% of each run, Pallas kernels for 0% -> 9%
where the time goes in v2:
time: 79.4 us; the launch traced here: 79.1 us
  waiting for transfers between devices  30.9 us (39%)
  starting transfers between devices  18.4 us (23%)
  Pallas kernels  12.4 us (16%)
  other arithmetic  12.2 us (15%)
  local copies, waits for them, and re-layouts  4.54 us (6%)
    ppermute x16, waiting for transfers between devices, move(): return lax.ppermute(value, AXES, perm)  30.9 us
    ppermute x16, starting transfers between devices, move(): return lax.ppermute(value, AXES, perm)  18.4 us
    pallas_call x4, Pallas kernels, product(): pl.pallas_call(lambda *refs: product_kernel(*refs, chunk=chunk, total_row...  5.71 us
    convert_element_type x2, other arithmetic, local(): send = (cut(mine, 1 - bit1, half) + cut(got, 1 - bit1, half)).astype(BF16)  4.58 us
    unnamed x22, local copies, waits for them, and re-layouts  4.54 us
    convert_element_type x4, other arithmetic, local(): sent = total.astype(BF16)  4.3 us
    pallas_call x2, Pallas kernels, apply_far(): pl.pallas_call(far_kernel, out_shape=out_shape, in_specs=[SMEM] + [VMEM]...  4.23 us
    convert_element_type x2, other arithmetic, local(): (cut(mine1, 1 - bit2, quarter) + cut(got1, 1 - bit2, quarter)).astype(BF16)  2.83 us
  transfers between devices with their start and end apart: 16, of which 10 were waited for; matrix products, arithmetic and copies ran while one was open for 15% of the time, Pallas kernels for 9%

profile of v2, /device:TPU:0, one launch (start us, length us, event | category | flops | bytes accessed | tf_op | source)
XLA Modules:
  0.0 79.1 jit_solution(4454331432952998638)
XLA Ops:
  0.6 1.4 %copy-done = bf16[1536,512]{1,0:T(8,128)(2,1)S(1)} copy-done((bf16[1536,512]{1,0:T(8,128)(2,1)S(1)}, bf16[1536,512]{1,0:T(8,128)(2,1)}, u32[]{:S(2)}) %copy-start) | copy-done | bytes 1572888
  2.0 1.4 %copy-done.2 = bf16[1536,512]{1,0:T(8,128)(2,1)S(1)} copy-done((bf16[1536,512]{1,0:T(8,128)(2,1)S(1)}, bf16[1536,512]{1,0:T(8,128)(2,1)}, u32[]{:S(2)}) %copy-start.2) | copy-done | bytes 1572888
  3.5 1.8 %shard_map.46 = bf16[2304,128]{1,0:T(8,128)(2,1)} custom-call(s32[1]{0:T(128)} %bitcast.refs_0_.half_ref, bf16[1536,512]{1,0:T(8,128)(2,1)S(1)} %copy-done, bf16[1536,512]{1,0:T(8,128)(2,1)S(1)} %copy-done.2), custom_call_target="tpu_custom_call" | custom-call | tf_op jit(solution)/shard_map/pallas_call | solution.py:90
  5.3 0.5 collective-permute-start.8
  5.8 1.9 %shard_map.42 = bf16[2688,128]{1,0:T(8,128)(2,1)} custom-call(s32[1]{0:T(128)} %bitcast.refs_0_.half_ref, bf16[1536,512]{1,0:T(8,128)(2,1)S(1)} %copy-done, bf16[1536,512]{1,0:T(8,128)(2,1)S(1)} %copy-done.2), custom_call_target="tpu_custom_call" | custom-call | tf_op jit(solution)/shard_map/pallas_call | solution.py:90
  7.6 0.0 collective-permute-start
  7.7 1.0 %shard_map.45 = bf16[2304,128]{1,0:T(8,128)(2,1)S(1)} custom-call(s32[1]{0:T(128)} %bitcast.1.refs_0_.half_ref, bf16[1536,512]{1,0:T(8,128)(2,1)S(1)} %copy-done.1, bf16[1536,512]{1,0:T(8,128)(2,1)S(1)} %copy-done.3), custom_call_target="tpu_custom_call" | custom-call | tf_op jit(solution)/shard_map/pallas_call | solution.py:90
  8.7 0.8 %copy-done.6 = bf16[2304,128]{1,0:T(8,128)(2,1)} copy-done((bf16[2304,128]{1,0:T(8,128)(2,1)}, bf16[2304,128]{1,0:T(8,128)(2,1)S(1)}, u32[]{:S(2)}) %copy-start.6) | copy-done | bytes 589848
  9.5 1.0 %shard_map.41 = bf16[2688,128]{1,0:T(8,128)(2,1)S(1)} custom-call(s32[1]{0:T(128)} %bitcast.1.refs_0_.half_ref, bf16[1536,512]{1,0:T(8,128)(2,1)S(1)} %copy-done.1, bf16[1536,512]{1,0:T(8,128)(2,1)S(1)} %copy-done.3), custom_call_target="tpu_custom_call" | custom-call | tf_op jit(solution)/shard_map/pallas_call | solution.py:90
  10.5 0.9 %copy-done.4 = bf16[2688,128]{1,0:T(8,128)(2,1)} copy-done((bf16[2688,128]{1,0:T(8,128)(2,1)}, bf16[2688,128]{1,0:T(8,128)(2,1)S(1)}, u32[]{:S(2)}) %copy-start.4) | copy-done | bytes 688152
  11.4 2.3 %add_convert_fusion.1 = (bf16[1152,128]{1,0:T(8,128)(2,1)}, f32[1152,128]{1,0:T(8,128)}) fusion(bf16[2304,128]{1,0:T(8,128)(2,1)} %collective-permute-done.8, s32[]{:T(128)S(6)} %select_n.103, bf16[2304,128]{1,0:T(8,128)(2,1)} %copy-done.6, s32[]{:T(128)S(6)} %select_n.101), kind=kLoop, calls=%fused_computation.4 | loop fusion | flops 1032192 | bytes 2064392 | tf_op jit(solution)/shard_map/convert_element_type | solution.py:285
  13.8 3.0 %collective-permute-start.9 = (bf16[1152,128]{1,0:T(8,128)(2,1)}, bf16[1152,128]{1,0:T(8,128)(2,1)}, u32[]{:S(2)}, u32[]{:S(2)}) collective-permute-start(bf16[1152,128]{1,0:T(8,128)(2,1)} %get-tuple-element.4), channel_id=1, source_target_pairs={{0,4},{1,3},{2,6},{3,1},{4,0},{5,7},{6,2},{7,5},{8,12},{9,11},{10,... | collective-permute-start | bytes 884744 | tf_op jit(solution)/shard_map/ppermute | solution.py:265
  16.7 2.2 %add_convert_fusion = (bf16[1344,128]{1,0:T(8,128)(2,1)}, f32[1344,128]{1,0:T(8,128)}) fusion(bf16[2688,128]{1,0:T(8,128)(2,1)} %collective-permute-done, s32[]{:T(128)S(6)} %select_n.93, bf16[2688,128]{1,0:T(8,128)(2,1)S(1)} %copy-done.5, s32[]{:T(128)S(6)} %select_n.91), kind=kLoop, calls=%fused_computation.1 | loop fusion | flops 1204224 | bytes 2408456 | tf_op jit(solution)/shard_map/convert_element_type | solution.py:285
  19.0 2.8 %collective-permute-done.9 = bf16[1152,128]{1,0:T(8,128)(2,1)} collective-permute-done((bf16[1152,128]{1,0:T(8,128)(2,1)}, bf16[1152,128]{1,0:T(8,128)(2,1)}, u32[]{:S(2)}, u32[]{:S(2)}) %collective-permute-start.9) | collective-permute-done | bytes 294944 | tf_op jit(solution)/shard_map/ppermute | solution.py:265
  21.8 1.7 %add_convert_fusion.3 = bf16[576,128]{1,0:T(8,128)(2,1)} fusion(f32[1152,128]{1,0:T(8,128)} %get-tuple-element.5, s32[]{:T(128)S(6)} %select_n.104, bf16[1152,128]{1,0:T(8,128)(2,1)} %collective-permute-done.9), kind=kLoop, calls=%fused_computation.17 | loop fusion | flops 221184 | bytes 589828 | tf_op jit(solution)/shard_map/convert_element_type | solution.py:288
  23.4 2.0 %collective-permute-start.10 = (bf16[576,128]{1,0:T(8,128)(2,1)}, bf16[576,128]{1,0:T(8,128)(2,1)}, u32[]{:S(2)}, u32[]{:S(2)}) collective-permute-start(bf16[576,128]{1,0:T(8,128)(2,1)} %add_convert_fusion.3), channel_id=1, source_target_pairs={{0,2},{1,5},{2,0},{3,7},{4,6},{5,1},{6,4},{7,3},{8,10},{9,13},{10,... | collective-permute-start | bytes 442376 | tf_op jit(solution)/shard_map/ppermute | solution.py:265
  25.5 1.7 %collective-permute-done.1 = bf16[1344,128]{1,0:T(8,128)(2,1)S(1)} collective-permute-done((bf16[1344,128]{1,0:T(8,128)(2,1)}, bf16[1344,128]{1,0:T(8,128)(2,1)S(1)}, u32[]{:S(2)}, u32[]{:S(2)}) %collective-permute-start.1) | collective-permute-done | bytes 344096 | tf_op jit(solution)/shard_map/ppermute | solution.py:265
  27.2 1.1 %add_convert_fusion.2 = bf16[672,128]{1,0:T(8,128)(2,1)S(1)} fusion(f32[1344,128]{1,0:T(8,128)} %get-tuple-element.3, s32[]{:T(128)S(6)} %select_n.94, bf16[1344,128]{1,0:T(8,128)(2,1)S(1)} %collective-permute-done.1), kind=kLoop, calls=%fused_computation.11 | loop fusion | flops 258048 | bytes 688132 | tf_op jit(solution)/shard_map/convert_element_type | solution.py:288
  28.3 1.4 %collective-permute-start.2 = (bf16[672,128]{1,0:T(8,128)(2,1)S(1)}, bf16[672,128]{1,0:T(8,128)(2,1)S(1)}, u32[]{:S(2)}, u32[]{:S(2)}) collective-permute-start(bf16[672,128]{1,0:T(8,128)(2,1)S(1)} %add_convert_fusion.2), channel_id=1, source_target_pairs={{0,2},{1,5},{2,0},{3,7},{4,6},{5,1},{6,4},{7,3},{8,10},{9,13},{10,... | collective-permute-start | bytes 516104 | tf_op jit(solution)/shard_map/ppermute | solution.py:265
  29.7 1.2 %fusion.1 = bf16[576,128]{1,0:T(8,128)(2,1)S(1)} fusion(bf16[576,128]{1,0:T(8,128)(2,1)} %collective-permute-done.10, bf16[1152,128]{1,0:T(8,128)(2,1)} %collective-permute-done.9, s32[]{:T(128)S(6)} %select_n.102, f32[1152,128]{1,0:T(8,128)} %get-tuple-element.5), kind=kLoop, calls=%fused_computation.23 | loop fusion | flops 442368 | bytes 737284 | tf_op jit(solution)/shard_map/convert_element_type | solution.py:293
  30.8 1.6 %collective-permute-start.11 = (bf16[576,128]{1,0:T(8,128)(2,1)S(1)}, bf16[576,128]{1,0:T(8,128)(2,1)S(1)}, u32[]{:S(2)}, u32[]{:S(2)}) collective-permute-start(bf16[576,128]{1,0:T(8,128)(2,1)S(1)} %fusion.1), channel_id=1, source_target_pairs={{0,8},{1,17},{2,10},{3,19},{4,12},{5,21},{6,14},{7,23},{8,0},{9,25... | collective-permute-start | bytes 442376 | tf_op jit(solution)/shard_map/ppermute | solution.py:265
  32.5 1.3 %collective-permute-done.2 = bf16[672,128]{1,0:T(8,128)(2,1)S(1)} collective-permute-done((bf16[672,128]{1,0:T(8,128)(2,1)S(1)}, bf16[672,128]{1,0:T(8,128)(2,1)S(1)}, u32[]{:S(2)}, u32[]{:S(2)}) %collective-permute-start.2) | collective-permute-done | bytes 172064 | tf_op jit(solution)/shard_map/ppermute | solution.py:265
  33.8 0.7 fusion
  34.5 1.3 %collective-permute-start.3 = (bf16[672,128]{1,0:T(8,128)(2,1)}, bf16[672,128]{1,0:T(8,128)(2,1)}, u32[]{:S(2)}, u32[]{:S(2)}) collective-permute-start(bf16[672,128]{1,0:T(8,128)(2,1)} %fusion), channel_id=1, source_target_pairs={{0,8},{1,17},{2,10},{3,19},{4,12},{5,21},{6,14},{7,23},{8,0},{9,25... | collective-permute-start | bytes 516104 | tf_op jit(solution)/shard_map/ppermute | solution.py:265
  35.9 1.9 %collective-permute-done.11 = bf16[576,128]{1,0:T(8,128)(2,1)S(1)} collective-permute-done((bf16[576,128]{1,0:T(8,128)(2,1)S(1)}, bf16[576,128]{1,0:T(8,128)(2,1)S(1)}, u32[]{:S(2)}, u32[]{:S(2)}) %collective-permute-start.11) | collective-permute-done | bytes 147488 | tf_op jit(solution)/shard_map/ppermute | solution.py:265
  37.8 1.1 %reduce-precision_convert_fusion.1.refs_1_ = bf16[576,128]{1,0:T(8,128)(2,1)S(1)} fusion(bf16[576,128]{1,0:T(8,128)(2,1)S(1)} %collective-permute-done.11, bf16[576,128]{1,0:T(8,128)(2,1)} %collective-permute-done.10, bf16[1152,128]{1,0:T(8,128)(2,1)} %collective-permute-done.9, s32[]{:T(128)S(6)} %select_n.102, f32[1152,128]{1,0:T(8,128)S(1)} %copy-done.8), kind=kLoop, calls=%fused_computation.15 | loop fusion | flops 663552 | bytes 884740 | tf_op jit(solution)/shard_map/convert_element_type | solution.py:293
  38.9 1.7 %collective-permute-start.12 = (bf16[576,128]{1,0:T(8,128)(2,1)S(1)}, bf16[576,128]{1,0:T(8,128)(2,1)S(1)}, u32[]{:S(2)}, u32[]{:S(2)}) collective-permute-start(bf16[576,128]{1,0:T(8,128)(2,1)S(1)} %reduce-precision_convert_fusion.1.refs_1_), channel_id=1, source_target_pairs={{0,16},{1,9},{2,18},{3,11},{4,20},{5,13},{6,22},{7,15},{8,24},{9,1... | collective-permute-start | bytes 442376 | tf_op jit(solution)/shard_map/ppermute | solution.py:265
  40.6 6.0 %collective-permute-done.12.refs_2_ = bf16[576,128]{1,0:T(8,128)(2,1)S(1)} collective-permute-done((bf16[576,128]{1,0:T(8,128)(2,1)S(1)}, bf16[576,128]{1,0:T(8,128)(2,1)S(1)}, u32[]{:S(2)}, u32[]{:S(2)}) %collective-permute-start.12) | collective-permute-done | bytes 147488 | tf_op jit(solution)/shard_map/ppermute | solution.py:265
  46.6 0.2 shard_map.47
  46.8 1.1 %collective-permute-start.13 = (bf16[592,128]{1,0:T(8,128)(2,1)S(1)}, bf16[592,128]{1,0:T(8,128)(2,1)S(1)}, u32[]{:S(2)}, u32[]{:S(2)}) collective-permute-start(bf16[592,128]{1,0:T(8,128)(2,1)S(1)} %shard_map.47), channel_id=1, source_target_pairs={{0,2},{1,5},{2,0},{3,7},{4,6},{5,1},{6,4},{7,3},{8,10},{9,13},{10,... | collective-permute-start | bytes 454664 | tf_op jit(solution)/shard_map/ppermute | solution.py:265
  47.9 1.3 %reduce-precision_convert_fusion.refs_1_ = bf16[672,128]{1,0:T(8,128)(2,1)S(1)} fusion(bf16[672,128]{1,0:T(8,128)(2,1)} %collective-permute-done.3, bf16[672,128]{1,0:T(8,128)(2,1)} %copy-done.10, bf16[1344,128]{1,0:T(8,128)(2,1)} %copy-done.9, s32[]{:T(128)S(6)} %select_n.92, f32[1344,128]{1,0:T(8,128)} %get-tuple-element.3), kind=kLoop, calls=%fused_computation.9 | loop fusion | flops 774144 | bytes 1032196 | tf_op jit(solution)/shard_map/convert_element_type | solution.py:293
  49.2 0.2 collective-permute-start.4
  49.4 2.6 %collective-permute-done.13 = bf16[592,128]{1,0:T(8,128)(2,1)S(1)} collective-permute-done((bf16[592,128]{1,0:T(8,128)(2,1)S(1)}, bf16[592,128]{1,0:T(8,128)(2,1)S(1)}, u32[]{:S(2)}, u32[]{:S(2)}) %collective-permute-start.13) | collective-permute-done | bytes 151584 | tf_op jit(solution)/shard_map/ppermute | solution.py:265
  52.0 5.1 %collective-permute-done.4.refs_2_ = bf16[672,128]{1,0:T(8,128)(2,1)S(1)} collective-permute-done((bf16[672,128]{1,0:T(8,128)(2,1)S(1)}, bf16[672,128]{1,0:T(8,128)(2,1)S(1)}, u32[]{:S(2)}, u32[]{:S(2)}) %collective-permute-start.4) | collective-permute-done | bytes 172064 | tf_op jit(solution)/shard_map/ppermute | solution.py:265
  57.1 0.7 shard_map.43
  57.9 0.9 %collective-permute-start.5 = (bf16[688,128]{1,0:T(8,128)(2,1)S(1)}, bf16[688,128]{1,0:T(8,128)(2,1)S(1)}, u32[]{:S(2)}, u32[]{:S(2)}) collective-permute-start(bf16[688,128]{1,0:T(8,128)(2,1)S(1)} %shard_map.43), channel_id=1, source_target_pairs={{0,2},{1,5},{2,0},{3,7},{4,6},{5,1},{6,4},{7,3},{8,10},{9,13},{10,... | collective-permute-start | bytes 528392 | tf_op jit(solution)/shard_map/ppermute | solution.py:265
  58.8 1.8 %collective-permute-start.14 = (bf16[1184,128]{1,0:T(8,128)(2,1)S(1)}, bf16[1184,128]{1,0:T(8,128)(2,1)S(1)}, u32[]{:S(2)}, u32[]{:S(2)}) collective-permute-start(bf16[1184,128]{1,0:T(8,128)(2,1)S(1)} %pad_maximum_fusion.3), channel_id=1, source_target_pairs={{0,4},{1,3},{2,6},{3,1},{4,0},{5,7},{6,2},{7,5},{8,12},{9,11},{10,... | collective-permute-start | bytes 909320 | tf_op jit(solution)/shard_map/ppermute | solution.py:265
  60.5 2.8 %collective-permute-done.5 = bf16[688,128]{1,0:T(8,128)(2,1)S(1)} collective-permute-done((bf16[688,128]{1,0:T(8,128)(2,1)S(1)}, bf16[688,128]{1,0:T(8,128)(2,1)S(1)}, u32[]{:S(2)}, u32[]{:S(2)}) %collective-permute-start.5) | collective-permute-done | bytes 176160 | tf_op jit(solution)/shard_map/ppermute | solution.py:265
  63.4 2.2 %collective-permute-start.6 = (bf16[1376,128]{1,0:T(8,128)(2,1)S(1)}, bf16[1376,128]{1,0:T(8,128)(2,1)S(1)}, u32[]{:S(2)}, u32[]{:S(2)}) collective-permute-start(bf16[1376,128]{1,0:T(8,128)(2,1)S(1)} %pad_maximum_fusion.2), channel_id=1, source_target_pairs={{0,4},{1,3},{2,6},{3,1},{4,0},{5,7},{6,2},{7,5},{8,12},{9,11},{10,... | collective-permute-start | bytes 1056776 | tf_op jit(solution)/shard_map/ppermute | solution.py:265
  65.7 0.1 broadcast_select_fusion.3
  65.8 5.2 %collective-permute-done.6 = bf16[1376,128]{1,0:T(8,128)(2,1)S(1)} collective-permute-done((bf16[1376,128]{1,0:T(8,128)(2,1)S(1)}, bf16[1376,128]{1,0:T(8,128)(2,1)S(1)}, u32[]{:S(2)}, u32[]{:S(2)}) %collective-permute-start.6) | collective-permute-done | bytes 352288 | tf_op jit(solution)/shard_map/ppermute | solution.py:265
  71.0 0.1 broadcast_select_fusion.1
  71.2 0.1 collective-permute-start.7
  71.3 0.6 collective-permute-start.15
  71.9 1.5 %collective-permute-done.7.far_ref.refs_1_ = bf16[2752,128]{1,0:T(8,128)(2,1)S(1)} collective-permute-done((bf16[2752,128]{1,0:T(8,128)(2,1)S(1)}, bf16[2752,128]{1,0:T(8,128)(2,1)S(1)}, u32[]{:S(2)}, u32[]{:S(2)}) %collective-permute-start.7) | collective-permute-done | bytes 704544 | tf_op jit(solution)/shard_map/ppermute | solution.py:265
  73.4 1.5 %shard_map.44.base_ref = f32[1536,512]{1,0:T(8,128)S(1)} custom-call(s32[1]{0:T(128)} %bitcast.1.refs_0_.half_ref, bf16[1536,512]{1,0:T(8,128)(2,1)S(1)} %copy-done.1, bf16[1536,512]{1,0:T(8,128)(2,1)S(1)} %copy-done.3, bf16[2752,128]{1,0:T(8,128)(2,1)S(1)} %pad_maximum_fusion.own_ref.refs_0_, bf16[2752,128]{1,0:T(8,128)(2,1)S(1)} %collective-permute-done.7.far_ref.refs_1_), custom_call_target="tpu_custom_call" | custom-call | tf_op jit(solution)/shard_map/pallas_call | solution.py:167
  74.9 1.3 %shard_map.48.base_ref = f32[1536,512]{1,0:T(8,128)S(1)} custom-call(s32[1]{0:T(128)} %bitcast.1.refs_0_.half_ref, bf16[1536,512]{1,0:T(8,128)(2,1)S(1)} %copy-done.1, f32[1536,512]{1,0:T(8,128)S(1)} %shard_map.44.base_ref, bf16[2368,128]{1,0:T(8,128)(2,1)S(1)} %pad_maximum_fusion.1.piece_ref.refs_2_), custom_call_target="tpu_custom_call" | custom-call | tf_op jit(solution)/shard_map/pallas_call | solution.py:229
  76.2 3.0 %shard_map.49 = (f32[1536,512]{1,0:T(8,128)}, f32[1]{0:T(128)}) custom-call(s32[1]{0:T(128)} %bitcast.refs_0_.half_ref, bf16[1536,512]{1,0:T(8,128)(2,1)S(1)} %copy-done.1, f32[1536,512]{1,0:T(8,128)S(1)} %shard_map.48.base_ref, bf16[2368,128]{1,0:T(8,128)(2,1)S(1)} %collective-permute-done.15.piece_ref, ...), custom_call_target="tpu_custom_call" | custom-call | tf_op jit(solution)/shard_map/pallas_call | solution.py:229
  (31 shorter events, 0.3 us)
Async XLA Ops:
  0.6 1.4 %copy-start = (bf16[1536,512]{1,0:T(8,128)(2,1)S(1)}, bf16[1536,512]{1,0:T(8,128)(2,1)}, u32[]{:S(2)}) copy-start(bf16[1536,512]{1,0:T(8,128)(2,1)} %orb_ref.5) | copy-start | bytes 4718596
  2.0 1.4 %copy-start.2 = (bf16[1536,512]{1,0:T(8,128)(2,1)S(1)}, bf16[1536,512]{1,0:T(8,128)(2,1)}, u32[]{:S(2)}) copy-start(bf16[1536,512]{1,0:T(8,128)(2,1)} %refs_2_.7) | copy-start | bytes 4718596
  5.3 2.4 %copy-start.1 = (bf16[1536,512]{1,0:T(8,128)(2,1)S(1)}, bf16[1536,512]{1,0:T(8,128)(2,1)}, u32[]{:S(2)}) copy-start(bf16[1536,512]{1,0:T(8,128)(2,1)} %orb_ref.5) | copy-start | bytes 4718596
  5.3 2.4 %copy-start.3 = (bf16[1536,512]{1,0:T(8,128)(2,1)S(1)}, bf16[1536,512]{1,0:T(8,128)(2,1)}, u32[]{:S(2)}) copy-start(bf16[1536,512]{1,0:T(8,128)(2,1)} %refs_2_.7) | copy-start | bytes 4718596
  5.3 6.1 %collective-permute-start.8 = (bf16[2304,128]{1,0:T(8,128)(2,1)}, bf16[2304,128]{1,0:T(8,128)(2,1)}, u32[]{:S(2)}, u32[]{:S(2)}) collective-permute-start(bf16[2304,128]{1,0:T(8,128)(2,1)} %shard_map.46), channel_id=1, source_target_pairs={{0,1},{1,0},{2,3},{3,2},{4,5},{5,4},{6,7},{7,6},{8,9},{9,8},{10,11... | collective-permute-start | bytes 1769480 | tf_op jit(solution)/shard_map/ppermute | solution.py:265
  7.6 9.1 %collective-permute-start = (bf16[2688,128]{1,0:T(8,128)(2,1)}, bf16[2688,128]{1,0:T(8,128)(2,1)}, u32[]{:S(2)}, u32[]{:S(2)}) collective-permute-start(bf16[2688,128]{1,0:T(8,128)(2,1)} %shard_map.42), channel_id=1, source_target_pairs={{0,1},{1,0},{2,3},{3,2},{4,5},{5,4},{6,7},{7,6},{8,9},{9,8},{10,11... | collective-permute-start | bytes 2064392 | tf_op jit(solution)/shard_map/ppermute | solution.py:265
  8.7 0.8 %copy-start.6 = (bf16[2304,128]{1,0:T(8,128)(2,1)}, bf16[2304,128]{1,0:T(8,128)(2,1)S(1)}, u32[]{:S(2)}) copy-start(bf16[2304,128]{1,0:T(8,128)(2,1)S(1)} %shard_map.45) | copy-start | bytes 1769476
  10.5 0.9 %copy-start.4 = (bf16[2688,128]{1,0:T(8,128)(2,1)}, bf16[2688,128]{1,0:T(8,128)(2,1)S(1)}, u32[]{:S(2)}) copy-start(bf16[2688,128]{1,0:T(8,128)(2,1)S(1)} %shard_map.41) | copy-start | bytes 2064388
  11.4 5.3 %copy-start.5 = (bf16[2688,128]{1,0:T(8,128)(2,1)S(1)}, bf16[2688,128]{1,0:T(8,128)(2,1)}, u32[]{:S(2)}) copy-start(bf16[2688,128]{1,0:T(8,128)(2,1)} %copy-done.4) | copy-start | bytes 2064388
  13.8 8.0 %collective-permute-start.9 = (bf16[1152,128]{1,0:T(8,128)(2,1)}, bf16[1152,128]{1,0:T(8,128)(2,1)}, u32[]{:S(2)}, u32[]{:S(2)}) collective-permute-start(bf16[1152,128]{1,0:T(8,128)(2,1)} %get-tuple-element.4), channel_id=1, source_target_pairs={{0,4},{1,3},{2,6},{3,1},{4,0},{5,7},{6,2},{7,5},{8,12},{9,11},{10,... | collective-permute-start | bytes 884744 | tf_op jit(solution)/shard_map/ppermute | solution.py:265
  19.0 8.2 %collective-permute-start.1 = (bf16[1344,128]{1,0:T(8,128)(2,1)}, bf16[1344,128]{1,0:T(8,128)(2,1)S(1)}, u32[]{:S(2)}, u32[]{:S(2)}) collective-permute-start(bf16[1344,128]{1,0:T(8,128)(2,1)} %get-tuple-element.2), channel_id=1, source_target_pairs={{0,4},{1,3},{2,6},{3,1},{4,0},{5,7},{6,2},{7,5},{8,12},{9,11},{10,... | collective-permute-start | bytes 1032200 | tf_op jit(solution)/shard_map/ppermute | solution.py:265
  23.4 6.2 %collective-permute-start.10 = (bf16[576,128]{1,0:T(8,128)(2,1)}, bf16[576,128]{1,0:T(8,128)(2,1)}, u32[]{:S(2)}, u32[]{:S(2)}) collective-permute-start(bf16[576,128]{1,0:T(8,128)(2,1)} %add_convert_fusion.3), channel_id=1, source_target_pairs={{0,2},{1,5},{2,0},{3,7},{4,6},{5,1},{6,4},{7,3},{8,10},{9,13},{10,... | collective-permute-start | bytes 442376 | tf_op jit(solution)/shard_map/ppermute | solution.py:265
  25.5 8.3 %copy-start.7 = (f32[1344,128]{1,0:T(8,128)S(1)}, f32[1344,128]{1,0:T(8,128)}, u32[]{:S(2)}) copy-start(f32[1344,128]{1,0:T(8,128)} %get-tuple-element.3) | copy-start | bytes 2064388
  25.5 12.3 %copy-start.8 = (f32[1152,128]{1,0:T(8,128)S(1)}, f32[1152,128]{1,0:T(8,128)}, u32[]{:S(2)}) copy-start(f32[1152,128]{1,0:T(8,128)} %get-tuple-element.5) | copy-start | bytes 1769476
  27.2 8.7 %copy-start.9 = (bf16[1344,128]{1,0:T(8,128)(2,1)}, bf16[1344,128]{1,0:T(8,128)(2,1)S(1)}, u32[]{:S(2)}) copy-start(bf16[1344,128]{1,0:T(8,128)(2,1)S(1)} %collective-permute-done.1) | copy-start | bytes 1032196
  28.3 5.5 %collective-permute-start.2 = (bf16[672,128]{1,0:T(8,128)(2,1)S(1)}, bf16[672,128]{1,0:T(8,128)(2,1)S(1)}, u32[]{:S(2)}, u32[]{:S(2)}) collective-permute-start(bf16[672,128]{1,0:T(8,128)(2,1)S(1)} %add_convert_fusion.2), channel_id=1, source_target_pairs={{0,2},{1,5},{2,0},{3,7},{4,6},{5,1},{6,4},{7,3},{8,10},{9,13},{10,... | collective-permute-start | bytes 516104 | tf_op jit(solution)/shard_map/ppermute | solution.py:265
  30.8 7.0 %collective-permute-start.11 = (bf16[576,128]{1,0:T(8,128)(2,1)S(1)}, bf16[576,128]{1,0:T(8,128)(2,1)S(1)}, u32[]{:S(2)}, u32[]{:S(2)}) collective-permute-start(bf16[576,128]{1,0:T(8,128)(2,1)S(1)} %fusion.1), channel_id=1, source_target_pairs={{0,8},{1,17},{2,10},{3,19},{4,12},{5,21},{6,14},{7,23},{8,0},{9,25... | collective-permute-start | bytes 442376 | tf_op jit(solution)/shard_map/ppermute | solution.py:265
  33.8 5.1 %copy-start.10 = (bf16[672,128]{1,0:T(8,128)(2,1)}, bf16[672,128]{1,0:T(8,128)(2,1)S(1)}, u32[]{:S(2)}) copy-start(bf16[672,128]{1,0:T(8,128)(2,1)S(1)} %collective-permute-done.2) | copy-start | bytes 516100
  34.5 13.3 %collective-permute-start.3 = (bf16[672,128]{1,0:T(8,128)(2,1)}, bf16[672,128]{1,0:T(8,128)(2,1)}, u32[]{:S(2)}, u32[]{:S(2)}) collective-permute-start(bf16[672,128]{1,0:T(8,128)(2,1)} %fusion), channel_id=1, source_target_pairs={{0,8},{1,17},{2,10},{3,19},{4,12},{5,21},{6,14},{7,23},{8,0},{9,25... | collective-permute-start | bytes 516104 | tf_op jit(solution)/shard_map/ppermute | solution.py:265
  38.9 7.7 %collective-permute-start.12 = (bf16[576,128]{1,0:T(8,128)(2,1)S(1)}, bf16[576,128]{1,0:T(8,128)(2,1)S(1)}, u32[]{:S(2)}, u32[]{:S(2)}) collective-permute-start(bf16[576,128]{1,0:T(8,128)(2,1)S(1)} %reduce-precision_convert_fusion.1.refs_1_), channel_id=1, source_target_pairs={{0,16},{1,9},{2,18},{3,11},{4,20},{5,13},{6,22},{7,15},{8,24},{9,1... | collective-permute-start | bytes 442376 | tf_op jit(solution)/shard_map/ppermute | solution.py:265
  46.8 5.2 %collective-permute-start.13 = (bf16[592,128]{1,0:T(8,128)(2,1)S(1)}, bf16[592,128]{1,0:T(8,128)(2,1)S(1)}, u32[]{:S(2)}, u32[]{:S(2)}) collective-permute-start(bf16[592,128]{1,0:T(8,128)(2,1)S(1)} %shard_map.47), channel_id=1, source_target_pairs={{0,2},{1,5},{2,0},{3,7},{4,6},{5,1},{6,4},{7,3},{8,10},{9,13},{10,... | collective-permute-start | bytes 454664 | tf_op jit(solution)/shard_map/ppermute | solution.py:265
  49.2 8.0 %collective-permute-start.4 = (bf16[672,128]{1,0:T(8,128)(2,1)S(1)}, bf16[672,128]{1,0:T(8,128)(2,1)S(1)}, u32[]{:S(2)}, u32[]{:S(2)}) collective-permute-start(bf16[672,128]{1,0:T(8,128)(2,1)S(1)} %reduce-precision_convert_fusion.refs_1_), channel_id=1, source_target_pairs={{0,16},{1,9},{2,18},{3,11},{4,20},{5,13},{6,22},{7,15},{8,24},{9,1... | collective-permute-start | bytes 516104 | tf_op jit(solution)/shard_map/ppermute | solution.py:265
  57.9 5.5 %collective-permute-start.5 = (bf16[688,128]{1,0:T(8,128)(2,1)S(1)}, bf16[688,128]{1,0:T(8,128)(2,1)S(1)}, u32[]{:S(2)}, u32[]{:S(2)}) collective-permute-start(bf16[688,128]{1,0:T(8,128)(2,1)S(1)} %shard_map.43), channel_id=1, source_target_pairs={{0,2},{1,5},{2,0},{3,7},{4,6},{5,1},{6,4},{7,3},{8,10},{9,13},{10,... | collective-permute-start | bytes 528392 | tf_op jit(solution)/shard_map/ppermute | solution.py:265
  58.8 6.9 %collective-permute-start.14 = (bf16[1184,128]{1,0:T(8,128)(2,1)S(1)}, bf16[1184,128]{1,0:T(8,128)(2,1)S(1)}, u32[]{:S(2)}, u32[]{:S(2)}) collective-permute-start(bf16[1184,128]{1,0:T(8,128)(2,1)S(1)} %pad_maximum_fusion.3), channel_id=1, source_target_pairs={{0,4},{1,3},{2,6},{3,1},{4,0},{5,7},{6,2},{7,5},{8,12},{9,11},{10,... | collective-permute-start | bytes 909320 | tf_op jit(solution)/shard_map/ppermute | solution.py:265
  63.4 7.6 %collective-permute-start.6 = (bf16[1376,128]{1,0:T(8,128)(2,1)S(1)}, bf16[1376,128]{1,0:T(8,128)(2,1)S(1)}, u32[]{:S(2)}, u32[]{:S(2)}) collective-permute-start(bf16[1376,128]{1,0:T(8,128)(2,1)S(1)} %pad_maximum_fusion.2), channel_id=1, source_target_pairs={{0,4},{1,3},{2,6},{3,1},{4,0},{5,7},{6,2},{7,5},{8,12},{9,11},{10,... | collective-permute-start | bytes 1056776 | tf_op jit(solution)/shard_map/ppermute | solution.py:265
  71.2 2.2 %collective-permute-start.7 = (bf16[2752,128]{1,0:T(8,128)(2,1)S(1)}, bf16[2752,128]{1,0:T(8,128)(2,1)S(1)}, u32[]{:S(2)}, u32[]{:S(2)}) collective-permute-start(bf16[2752,128]{1,0:T(8,128)(2,1)S(1)} %pad_maximum_fusion.own_ref.refs_0_), channel_id=1, source_target_pairs={{0,1},{1,0},{2,3},{3,2},{4,5},{5,4},{6,7},{7,6},{8,9},{9,8},{10,11... | collective-permute-start | bytes 2113544 | tf_op jit(solution)/shard_map/ppermute | solution.py:265
  71.3 4.9 %collective-permute-start.15 = (bf16[2368,128]{1,0:T(8,128)(2,1)S(1)}, bf16[2368,128]{1,0:T(8,128)(2,1)S(1)}, u32[]{:S(2)}, u32[]{:S(2)}) collective-permute-start(bf16[2368,128]{1,0:T(8,128)(2,1)S(1)} %pad_maximum_fusion.1.piece_ref.refs_2_), channel_id=1, source_target_pairs={{0,1},{1,0},{2,3},{3,2},{4,5},{5,4},{6,7},{7,6},{8,9},{9,8},{10,11... | collective-permute-start | bytes 1818632 | tf_op jit(solution)/shard_map/ppermute | solution.py:265

commit v3 on v2

--- a/solution.py
+++ b/solution.py
@@ -31,8 +31,16 @@
     return side, extra, near_at, far_at
 
 
-def starts(half_ref, side):
-    h = half_ref[0]
+def position():
+    r, c = lax.axis_index("gr"), lax.axis_index("gc")
+    core = c & 1
+    on_r, on_c = r & 1, (c >> 1) & 1
+    return core, jnp.where(core == 0, on_r, on_c), jnp.where(core == 0, on_c, on_r)
+
+
+def starts(flip, side):
+    core, _, _ = position()
+    h = core ^ flip
     low = pl.multiple_of(h * (side * TILE), TILE)
     up = pl.multiple_of((1 - h) * (side * TILE), TILE)
     return h, low, up
@@ -48,9 +56,9 @@
     return one + two
 
 
-def product_kernel(half_ref, orb_ref, vel_ref, out_ref, *, chunk, total_rows):
+def product_kernel(orb_ref, vel_ref, out_ref, *, flip, chunk, total_rows):
     side, extra, near_at, far_at = layout(total_rows)
-    h, low, up = starts(half_ref, side)
+    h, low, up = starts(flip, side)
     table = far_at if chunk else near_at
     for c in range(0, side, 2):
         columns = [j for j in (c, c + 1) if j < side]
@@ -85,24 +93,75 @@
     return len(far_at) + extra if chunk else len(near_at)
 
 
-def product(half, orb, vel, chunk):
+def call(kernel, out, mib, *operands, scratch=()):
+    return pl.pallas_call(
+        kernel,
+        out_shape=out,
+        in_specs=[VMEM] * len(operands),
+        out_specs=jax.tree.map(lambda _: VMEM, out),
+        scratch_shapes=scratch,
+        compiler_params=params(mib),
+    )(*operands)
+
+
+def product(flip, orb, vel, chunk):
     rows = orb.shape[0]
-    return pl.pallas_call(
-        lambda *refs: product_kernel(*refs, chunk=chunk, total_rows=rows),
-        out_shape=jax.ShapeDtypeStruct((tile_count(chunk, rows) * TILE, TILE), BF16),
-        in_specs=[SMEM, VMEM, VMEM],
-        out_specs=VMEM,
-        compiler_params=params(16),
-    )(half, orb, vel)
-
-
-def share_kernel(off_ref, a_ref, b_ref, out_ref, *, diagonal):
+    return call(
+        lambda *refs: product_kernel(*refs, flip=flip, chunk=chunk, total_rows=rows),
+        jax.ShapeDtypeStruct((tile_count(chunk, rows) * TILE, TILE), BF16),
+        6,
+        orb,
+        vel,
+    )
+
+
+def halve_kernel(mine_ref, got_ref, send_ref, keep_ref, *, which):
+    rows = send_ref.shape[0]
+    bit = position()[which]
+
+    def part(index):
+        at = pl.ds(pl.multiple_of(index * rows, PAD), rows)
+        return mine_ref[at, :].astype(F32) + got_ref[at, :].astype(F32)
+
+    send_ref[...] = part(1 - bit).astype(BF16)
+    keep_ref[...] = part(bit)
+
+
+def halve(mine, got, which):
+    rows = mine.shape[0] // 2
+    out = [jax.ShapeDtypeStruct((rows, TILE), BF16), jax.ShapeDtypeStruct((rows, TILE), F32)]
+    return call(lambda *refs: halve_kernel(*refs, which=which), out, 2, mine, got)
+
+
+def add_kernel(a_ref, b_ref, out_ref):
+    out_ref[...] = (a_ref[...].astype(F32) + b_ref[...].astype(F32)).astype(BF16)
+
+
+def add(a, b):
+    return call(add_kernel, jax.ShapeDtypeStruct(a.shape, BF16), 2, a, b)
+
+
+def join_kernel(mine_ref, got_ref, out_ref, *, which):
+    rows = mine_ref.shape[0]
+    bit = position()[which]
+    out_ref[pl.ds(pl.multiple_of(bit * rows, PAD), rows), :] = mine_ref[...]
+    out_ref[pl.ds(pl.multiple_of((1 - bit) * rows, PAD), rows), :] = got_ref[...]
+
+
+def join(mine, got, which):
+    out = jax.ShapeDtypeStruct((2 * mine.shape[0], TILE), BF16)
+    return call(lambda *refs: join_kernel(*refs, which=which), out, 2, mine, got)
+
+
+def share_kernel(a_ref, b_ref, out_ref, *, diagonal):
     rows = a_ref.shape[0]
+    _, bit1, bit2 = position()
+    offset = (2 * bit1 + bit2) * rows
     total = a_ref[...].astype(F32) + b_ref[...].astype(F32)
     out_ref[0:rows, :] = total.astype(BF16)
     square = total * total
     if diagonal:
-        tile = (lax.broadcasted_iota(jnp.int32, (rows, TILE), 0) + off_ref[0]) // TILE
+        tile = (lax.broadcasted_iota(jnp.int32, (rows, TILE), 0) + offset) // TILE
         single = tile == diagonal[0]
         for at in diagonal[1:]:
             single |= tile == at
@@ -119,15 +178,9 @@
     out_ref[rows : rows + PAD, :] = tail.astype(BF16)
 
 
-def make_share(offset, a, b, diagonal):
-    rows = a.shape[0]
-    return pl.pallas_call(
-        lambda *refs: share_kernel(*refs, diagonal=diagonal),
-        out_shape=jax.ShapeDtypeStruct((rows + PAD, TILE), BF16),
-        in_specs=[SMEM, VMEM, VMEM],
-        out_specs=VMEM,
-        compiler_params=params(4),
-    )(offset, a, b)
+def make_share(a, b, diagonal):
+    out = jax.ShapeDtypeStruct((a.shape[0] + PAD, TILE), BF16)
+    return call(lambda *refs: share_kernel(*refs, diagonal=diagonal), out, 3, a, b)
 
 
 def take_tile(ref, index):
@@ -146,10 +199,10 @@
     ref[i * TILE : (i + 1) * TILE, j * TILE : (j + 1) * TILE] = value
 
 
-def near_kernel(half_ref, orb_ref, vel_ref, own_ref, far_ref, out_ref, a_ref):
+def near_kernel(orb_ref, vel_ref, own_ref, far_ref, out_ref, a_ref):
     side, _, near_at, _ = layout(orb_ref.shape[0])
     wide = side * TILE
-    _, low, up = starts(half_ref, side)
+    _, low, up = starts(0, side)
     for ref, at, n in ((own_ref, low, 0), (far_ref, up, 1)):
         for (i, j), index in near_at.items():
             value = take_tile(ref, index)
@@ -162,16 +215,10 @@
         out_ref[pl.ds(at, wide), :] = vel_ref[pl.ds(at, wide), :].astype(F32) - 0.5 * value
 
 
-def apply_near(half, orb, vel, own, far):
+def apply_near(orb, vel, own, far):
     wide = orb.shape[0] // 2
-    return pl.pallas_call(
-        near_kernel,
-        out_shape=jax.ShapeDtypeStruct(orb.shape, F32),
-        in_specs=[SMEM] + [VMEM] * 4,
-        out_specs=VMEM,
-        scratch_shapes=[pltpu.VMEM((2 * wide, wide), BF16)],
-        compiler_params=params(20),
-    )(half, orb, vel, own, far)
+    out = jax.ShapeDtypeStruct(orb.shape, F32)
+    return call(near_kernel, out, 8, orb, vel, own, far, scratch=[pltpu.VMEM((2 * wide, wide), BF16)])
 
 
 def tails(ref):
@@ -183,10 +230,10 @@
     return total
 
 
-def far_kernel(half_ref, orb_ref, base_ref, piece_ref, *refs):
+def far_kernel(orb_ref, base_ref, piece_ref, *refs, flip):
     total_rows = orb_ref.shape[0]
     side, extra, _, far_at = layout(total_rows)
-    h, low, up = starts(half_ref, side)
+    h, low, up = starts(flip, side)
     out_ref, b_ref, t_ref = refs[-3:]
     if len(refs) > 3:
         near_own, near_far, own, out_ref, norm_ref = refs[:5]
@@ -219,7 +266,7 @@
         out_ref[at, :] = base_ref[at, :] - 0.5 * value
 
 
-def apply_far(half, orb, base, piece, others=()):
+def apply_far(flip, orb, base, piece, others=()):
     wide = orb.shape[0] // 2
     out_shape = [jax.ShapeDtypeStruct(orb.shape, F32)]
     out_specs = [VMEM]
@@ -227,13 +274,13 @@
         out_shape.append(jax.ShapeDtypeStruct((1,), F32))
         out_specs.append(SMEM)
     return pl.pallas_call(
-        far_kernel,
+        lambda *refs: far_kernel(*refs, flip=flip),
         out_shape=out_shape,
-        in_specs=[SMEM] + [VMEM] * (3 + len(others)),
+        in_specs=[VMEM] * (3 + len(others)),
         out_specs=out_specs,
         scratch_shapes=[pltpu.VMEM((wide, wide), BF16)] * 2,
-        compiler_params=params(20),
-    )(half, orb, base, piece, *others)
+        compiler_params=params(8),
+    )(orb, base, piece, *others)
 
 
 def pairs(nr, nc, even, odd):
@@ -247,12 +294,7 @@
 
 def local(orbitals, velocities):
     nr, nc = lax.axis_size("gr"), lax.axis_size("gc")
-    r, c = lax.axis_index("gr"), lax.axis_index("gc")
     side, _, near_at, _ = layout(orbitals.shape[0])
-    core = c & 1
-    on_r, on_c = r & 1, (c >> 1) & 1
-    bit1 = jnp.where(core == 0, on_r, on_c)
-    bit2 = jnp.where(core == 0, on_c, on_r)
     swap = pairs(nr, nc, (0, 1), (0, 1))
     first = pairs(nr, nc, (1, 0), (0, 2))
     second = pairs(nr, nc, (0, 2), (1, 0))
@@ -264,45 +306,27 @@
     def move(value, perm):
         return lax.ppermute(value, AXES, perm)
 
-    def cut(value, index, rows):
-        return lax.dynamic_slice_in_dim(value, index * rows, rows, 0).astype(F32)
-
-    def rounded(value):
-        return lax.reduce_precision(value, 8, 7)
-
-    def join(bit, mine, got):
-        return jnp.concatenate([jnp.where(bit == 0, mine, got), jnp.where(bit == 0, got, mine)], axis=0)
-
-    own = core.reshape(1)
-    other = (1 - core).reshape(1)
     joined = []
     for k in range(2):
-        away = product(other, orbitals, velocities, k)
+        away = product(1, orbitals, velocities, k)
         got = move(away, swap)
-        mine = product(own, orbitals, velocities, k)
-        rows = mine.shape[0]
-        half, quarter = rows // 2, rows // 4
-        send = (cut(mine, 1 - bit1, half) + cut(got, 1 - bit1, half)).astype(BF16)
-        mine1 = cut(mine, bit1, half) + cut(got, bit1, half)
-        got1 = move(send, first)
-        send = (cut(mine1, 1 - bit2, quarter) + cut(got1, 1 - bit2, quarter)).astype(BF16)
-        mine2 = cut(mine1, bit2, quarter) + cut(got1, bit2, quarter)
-        got2 = move(send, second)
-        total = rounded(mine2 + got2.astype(F32))
-        for j, perm in enumerate(doubling):
-            sent = total.astype(BF16)
-            back = move(sent, perm)
-            if j < len(doubling) - 1:
-                total = rounded(total + back.astype(F32))
-        share = make_share((bit1 * half + bit2 * quarter).reshape(1), sent, back, diagonals[k])
-        back = move(share, second)
-        quarter = join(bit2, share, back)
-        back = move(quarter, first)
-        joined.append(join(bit1, quarter, back))
+        mine = product(0, orbitals, velocities, k)
+        send, mine = halve(mine, got, 1)
+        got = move(send, first)
+        send, mine = halve(mine, got, 2)
+        got = move(send, second)
+        for perm in doubling:
+            mine = add(mine, got)
+            got = move(mine, perm)
+        share = make_share(mine, got, diagonals[k])
+        got = move(share, second)
+        quarter = join(share, got, 2)
+        got = move(quarter, first)
+        joined.append(join(quarter, got, 1))
     far = [move(joined[k], swap) for k in range(2)]
-    new = apply_near(own, orbitals, velocities, joined[0], far[0])
-    (new,) = apply_far(own, orbitals, new, joined[1])
-    new, measured = apply_far(other, orbitals, new, far[1], (joined[0], far[0], joined[1]))
+    new = apply_near(orbitals, velocities, joined[0], far[0])
+    (new,) = apply_far(0, orbitals, new, joined[1])
+    new, measured = apply_far(1, orbitals, new, far[1], (joined[0], far[0], joined[1]))
     return new, measured
 
 

time: 79.4 us -> 69 us (0.87)
  other arithmetic: 12.2 us -> 0 us
  waiting for transfers between devices: 30.9 us -> 34.2 us
  local copies, waits for them, and re-layouts: 4.54 us -> 2.82 us
  starting transfers between devices: 18.4 us -> 19.8 us
  Pallas kernels: 12.4 us -> 11.3 us
    convert_element_type x8 -> x0, other arithmetic: 11.7 us -> none  [the longest x2 4.58 us: local(): send = (cut(mine, 1 - bit1, half) + cut(got, 1 - bit1, half)).astype(BF16)]
    ppermute x16, waiting for transfers between devices: 30.9 us -> 34.2 us  [move(): return lax.ppermute(value, AXES, perm)]
    unnamed x22 -> x8, local copies, waits for them, and re-layouts: 4.54 us -> 2.82 us
    ppermute x16, starting transfers between devices: 18.4 us -> 19.8 us  [move(): return lax.ppermute(value, AXES, perm)]
    pallas_call x9 -> x21, Pallas kernels: 12.4 us -> 11.3 us  [the longest x19 7.21 us: call(): pl.pallas_call(kernel, out_shape=out, in_specs=[VMEM] * len(operands), ou...]
  transfers between devices with their start and end apart: 16 -> 16, of which waited for: 10 -> 7; matrix products, arithmetic and copies ran while one was open for 15% -> 0% of each run, Pallas kernels for 9% -> 11%
where the time goes in v3:
time: 69 us; the launch traced here: 68.9 us
  waiting for transfers between devices  34.2 us (50%)
  starting transfers between devices  19.8 us (29%)
  Pallas kernels  11.3 us (16%)
  local copies, waits for them, and re-layouts  2.82 us (4%)
  between operations  0.83 us (1%)
    ppermute x16, waiting for transfers between devices, move(): return lax.ppermute(value, AXES, perm)  34.2 us
    ppermute x16, starting transfers between devices, move(): return lax.ppermute(value, AXES, perm)  19.8 us
    pallas_call x19, Pallas kernels, call(): pl.pallas_call(kernel, out_shape=out, in_specs=[VMEM] * len(operands), ou...  7.21 us
    pallas_call x2, Pallas kernels, apply_far(): pl.pallas_call(lambda *refs: far_kernel(*refs, flip=flip), out_shape=out_...  4.05 us
    unnamed x8, local copies, waits for them, and re-layouts  2.82 us
  transfers between devices with their start and end apart: 16, of which 7 were waited for; matrix products, arithmetic and copies ran while one was open for 0% of the time, Pallas kernels for 11%

profile of v3, /device:TPU:0, one launch (start us, length us, event | category | flops | bytes accessed | tf_op | source)
XLA Modules:
  0.0 68.9 jit_solution(16457203129199506628)
XLA Ops:
  0.6 0.0 copy-start
  0.6 1.4 %copy-done = bf16[1536,512]{1,0:T(8,128)(2,1)S(1)} copy-done((bf16[1536,512]{1,0:T(8,128)(2,1)S(1)}, bf16[1536,512]{1,0:T(8,128)(2,1)}, u32[]{:S(2)}) %copy-start) | copy-done | bytes 1572888
  2.0 1.4 %copy-done.2 = bf16[1536,512]{1,0:T(8,128)(2,1)S(1)} copy-done((bf16[1536,512]{1,0:T(8,128)(2,1)S(1)}, bf16[1536,512]{1,0:T(8,128)(2,1)}, u32[]{:S(2)}) %copy-start.2) | copy-done | bytes 1572888
  3.4 1.0 %shard_map.42 = bf16[2688,128]{1,0:T(8,128)(2,1)S(1)} custom-call(bf16[1536,512]{1,0:T(8,128)(2,1)S(1)} %copy-done, bf16[1536,512]{1,0:T(8,128)(2,1)S(1)} %copy-done.2), custom_call_target="tpu_custom_call" | custom-call | tf_op jit(solution)/shard_map/pallas_call | solution.py:97
  4.5 0.6 collective-permute-start
  5.0 1.0 %shard_map.52 = bf16[2304,128]{1,0:T(8,128)(2,1)S(1)} custom-call(bf16[1536,512]{1,0:T(8,128)(2,1)S(1)} %copy-done, bf16[1536,512]{1,0:T(8,128)(2,1)S(1)} %copy-done.2), custom_call_target="tpu_custom_call" | custom-call | tf_op jit(solution)/shard_map/pallas_call | solution.py:97
  6.0 0.1 collective-permute-start.8
  6.1 1.0 %shard_map.41.refs_0_ = bf16[2688,128]{1,0:T(8,128)(2,1)S(1)} custom-call(bf16[1536,512]{1,0:T(8,128)(2,1)S(1)} %copy-done, bf16[1536,512]{1,0:T(8,128)(2,1)S(1)} %copy-done.2), custom_call_target="tpu_custom_call" | custom-call | tf_op jit(solution)/shard_map/pallas_call | solution.py:97
  7.1 0.0 collective-permute-done.refs_1_
  7.1 0.2 shard_map.43
  7.3 3.0 %collective-permute-start.1 = (bf16[1344,128]{1,0:T(8,128)(2,1)S(1)}, bf16[1344,128]{1,0:T(8,128)(2,1)S(1)}, u32[]{:S(2)}, u32[]{:S(2)}) collective-permute-start(bf16[1344,128]{1,0:T(8,128)(2,1)S(1)} %get-tuple-element.11), channel_id=1, source_target_pairs={{0,4},{1,3},{2,6},{3,1},{4,0},{5,7},{6,2},{7,5},{8,12},{9,11},{10,... | collective-permute-start | bytes 1032200 | tf_op jit(solution)/shard_map/ppermute | solution.py:307
  10.3 1.0 %shard_map.51.refs_0_ = bf16[2304,128]{1,0:T(8,128)(2,1)S(1)} custom-call(bf16[1536,512]{1,0:T(8,128)(2,1)S(1)} %copy-done, bf16[1536,512]{1,0:T(8,128)(2,1)S(1)} %copy-done.2), custom_call_target="tpu_custom_call" | custom-call | tf_op jit(solution)/shard_map/pallas_call | solution.py:97
  11.4 0.0 collective-permute-done.8.refs_1_
  11.4 0.1 shard_map.53
  11.5 0.1 collective-permute-start.9
  11.6 4.0 %collective-permute-done.1.refs_1_ = bf16[1344,128]{1,0:T(8,128)(2,1)S(1)} collective-permute-done((bf16[1344,128]{1,0:T(8,128)(2,1)S(1)}, bf16[1344,128]{1,0:T(8,128)(2,1)S(1)}, u32[]{:S(2)}, u32[]{:S(2)}) %collective-permute-start.1) | collective-permute-done | bytes 344096 | tf_op jit(solution)/shard_map/ppermute | solution.py:307
  15.6 0.1 shard_map.44
  15.6 2.1 %collective-permute-start.2 = (bf16[672,128]{1,0:T(8,128)(2,1)S(1)}, bf16[672,128]{1,0:T(8,128)(2,1)S(1)}, u32[]{:S(2)}, u32[]{:S(2)}) collective-permute-start(bf16[672,128]{1,0:T(8,128)(2,1)S(1)} %get-tuple-element.13), channel_id=1, source_target_pairs={{0,2},{1,5},{2,0},{3,7},{4,6},{5,1},{6,4},{7,3},{8,10},{9,13},{10,... | collective-permute-start | bytes 516104 | tf_op jit(solution)/shard_map/ppermute | solution.py:307
  17.8 3.4 %collective-permute-done.2.b_ref = bf16[672,128]{1,0:T(8,128)(2,1)S(1)} collective-permute-done((bf16[672,128]{1,0:T(8,128)(2,1)S(1)}, bf16[672,128]{1,0:T(8,128)(2,1)S(1)}, u32[]{:S(2)}, u32[]{:S(2)}) %collective-permute-start.2) | collective-permute-done | bytes 172064 | tf_op jit(solution)/shard_map/ppermute | solution.py:307
  21.2 2.1 %collective-permute-start.3 = (bf16[672,128]{1,0:T(8,128)(2,1)S(1)}, bf16[672,128]{1,0:T(8,128)(2,1)S(1)}, u32[]{:S(2)}, u32[]{:S(2)}) collective-permute-start(bf16[672,128]{1,0:T(8,128)(2,1)S(1)} %shard_map.45.a_ref), channel_id=1, source_target_pairs={{0,8},{1,17},{2,10},{3,19},{4,12},{5,21},{6,14},{7,23},{8,0},{9,25... | collective-permute-start | bytes 516104 | tf_op jit(solution)/shard_map/ppermute | solution.py:307
  23.4 0.0 copy-start.1
  23.4 0.0 copy-start.3
  23.4 1.6 %collective-permute-start.10 = (bf16[576,128]{1,0:T(8,128)(2,1)S(1)}, bf16[576,128]{1,0:T(8,128)(2,1)S(1)}, u32[]{:S(2)}, u32[]{:S(2)}) collective-permute-start(bf16[576,128]{1,0:T(8,128)(2,1)S(1)} %get-tuple-element.17), channel_id=1, source_target_pairs={{0,2},{1,5},{2,0},{3,7},{4,6},{5,1},{6,4},{7,3},{8,10},{9,13},{10,... | collective-permute-start | bytes 442376 | tf_op jit(solution)/shard_map/ppermute | solution.py:307
  25.0 3.1 %collective-permute-done.3.b_ref = bf16[672,128]{1,0:T(8,128)(2,1)S(1)} collective-permute-done((bf16[672,128]{1,0:T(8,128)(2,1)S(1)}, bf16[672,128]{1,0:T(8,128)(2,1)S(1)}, u32[]{:S(2)}, u32[]{:S(2)}) %collective-permute-start.3) | collective-permute-done | bytes 172064 | tf_op jit(solution)/shard_map/ppermute | solution.py:307
  28.2 2.6 %collective-permute-start.4 = (bf16[672,128]{1,0:T(8,128)(2,1)S(1)}, bf16[672,128]{1,0:T(8,128)(2,1)S(1)}, u32[]{:S(2)}, u32[]{:S(2)}) collective-permute-start(bf16[672,128]{1,0:T(8,128)(2,1)S(1)} %shard_map.46.refs_0_), channel_id=1, source_target_pairs={{0,16},{1,9},{2,18},{3,11},{4,20},{5,13},{6,22},{7,15},{8,24},{9,1... | collective-permute-start | bytes 516104 | tf_op jit(solution)/shard_map/ppermute | solution.py:307
  30.7 0.0 collective-permute-done.10.b_ref
  30.8 2.5 %collective-permute-start.11 = (bf16[576,128]{1,0:T(8,128)(2,1)S(1)}, bf16[576,128]{1,0:T(8,128)(2,1)S(1)}, u32[]{:S(2)}, u32[]{:S(2)}) collective-permute-start(bf16[576,128]{1,0:T(8,128)(2,1)S(1)} %shard_map.55.a_ref), channel_id=1, source_target_pairs={{0,8},{1,17},{2,10},{3,19},{4,12},{5,21},{6,14},{7,23},{8,0},{9,25... | collective-permute-start | bytes 442376 | tf_op jit(solution)/shard_map/ppermute | solution.py:307
  33.3 5.9 %collective-permute-done.4.refs_1_ = bf16[672,128]{1,0:T(8,128)(2,1)S(1)} collective-permute-done((bf16[672,128]{1,0:T(8,128)(2,1)S(1)}, bf16[672,128]{1,0:T(8,128)(2,1)S(1)}, u32[]{:S(2)}, u32[]{:S(2)}) %collective-permute-start.4) | collective-permute-done | bytes 172064 | tf_op jit(solution)/shard_map/ppermute | solution.py:307
  39.2 0.7 %shard_map.47.refs_0_ = bf16[688,128]{1,0:T(8,128)(2,1)S(1)} custom-call(bf16[672,128]{1,0:T(8,128)(2,1)S(1)} %shard_map.46.refs_0_, bf16[672,128]{1,0:T(8,128)(2,1)S(1)} %collective-permute-done.4.refs_1_), custom_call_target="tpu_custom_call" | custom-call | tf_op jit(solution)/shard_map/pallas_call | solution.py:97
  40.0 1.5 %collective-permute-start.5 = (bf16[688,128]{1,0:T(8,128)(2,1)S(1)}, bf16[688,128]{1,0:T(8,128)(2,1)S(1)}, u32[]{:S(2)}, u32[]{:S(2)}) collective-permute-start(bf16[688,128]{1,0:T(8,128)(2,1)S(1)} %shard_map.47.refs_0_), channel_id=1, source_target_pairs={{0,2},{1,5},{2,0},{3,7},{4,6},{5,1},{6,4},{7,3},{8,10},{9,13},{10,... | collective-permute-start | bytes 528392 | tf_op jit(solution)/shard_map/ppermute | solution.py:307
  41.5 0.1 collective-permute-start.12
  41.6 7.6 %collective-permute-done.12.refs_1_ = bf16[576,128]{1,0:T(8,128)(2,1)S(1)} collective-permute-done((bf16[576,128]{1,0:T(8,128)(2,1)S(1)}, bf16[576,128]{1,0:T(8,128)(2,1)S(1)}, u32[]{:S(2)}, u32[]{:S(2)}) %collective-permute-start.12) | collective-permute-done | bytes 147488 | tf_op jit(solution)/shard_map/ppermute | solution.py:307
  49.2 0.2 shard_map.57.refs_0_
  49.5 0.5 collective-permute-start.13
  49.9 0.0 collective-permute-done.5.refs_1_
  50.0 1.6 %collective-permute-start.6 = (bf16[1376,128]{1,0:T(8,128)(2,1)S(1)}, bf16[1376,128]{1,0:T(8,128)(2,1)S(1)}, u32[]{:S(2)}, u32[]{:S(2)}) collective-permute-start(bf16[1376,128]{1,0:T(8,128)(2,1)S(1)} %shard_map.48.refs_0_), channel_id=1, source_target_pairs={{0,4},{1,3},{2,6},{3,1},{4,0},{5,7},{6,2},{7,5},{8,12},{9,11},{10,... | collective-permute-start | bytes 1056776 | tf_op jit(solution)/shard_map/ppermute | solution.py:307
  51.6 4.6 %collective-permute-done.13.refs_1_ = bf16[592,128]{1,0:T(8,128)(2,1)S(1)} collective-permute-done((bf16[592,128]{1,0:T(8,128)(2,1)S(1)}, bf16[592,128]{1,0:T(8,128)(2,1)S(1)}, u32[]{:S(2)}, u32[]{:S(2)}) %collective-permute-start.13) | collective-permute-done | bytes 151584 | tf_op jit(solution)/shard_map/ppermute | solution.py:307
  56.3 1.2 %collective-permute-start.14 = (bf16[1184,128]{1,0:T(8,128)(2,1)S(1)}, bf16[1184,128]{1,0:T(8,128)(2,1)S(1)}, u32[]{:S(2)}, u32[]{:S(2)}) collective-permute-start(bf16[1184,128]{1,0:T(8,128)(2,1)S(1)} %shard_map.58.refs_0_), channel_id=1, source_target_pairs={{0,4},{1,3},{2,6},{3,1},{4,0},{5,7},{6,2},{7,5},{8,12},{9,11},{10,... | collective-permute-start | bytes 909320 | tf_op jit(solution)/shard_map/ppermute | solution.py:307
  57.5 0.0 collective-permute-done.6.refs_1_
  57.5 0.1 shard_map.49.own_ref.refs_3_
  57.6 0.1 collective-permute-start.7
  57.7 5.5 %collective-permute-done.14.refs_1_ = bf16[1184,128]{1,0:T(8,128)(2,1)S(1)} collective-permute-done((bf16[1184,128]{1,0:T(8,128)(2,1)S(1)}, bf16[1184,128]{1,0:T(8,128)(2,1)S(1)}, u32[]{:S(2)}, u32[]{:S(2)}) %collective-permute-start.14) | collective-permute-done | bytes 303136 | tf_op jit(solution)/shard_map/ppermute | solution.py:307
  63.2 0.1 shard_map.59.refs_2_.refs_5_
  63.2 0.1 collective-permute-start.15
  63.3 1.5 %shard_map.50.refs_1_ = f32[1536,512]{1,0:T(8,128)S(1)} custom-call(bf16[1536,512]{1,0:T(8,128)(2,1)S(1)} %copy-done.1, bf16[1536,512]{1,0:T(8,128)(2,1)S(1)} %copy-done.3, bf16[2752,128]{1,0:T(8,128)(2,1)S(1)} %shard_map.49.own_ref.refs_3_, bf16[2752,128]{1,0:T(8,128)(2,1)S(1)} %collective-permute-done.7.far_ref.refs_4_), custom_call_target="tpu_custom_call" | custom-call | tf_op jit(solution)/shard_map/pallas_call | solution.py:97
  64.8 1.1 %shard_map.60.refs_1_ = f32[1536,512]{1,0:T(8,128)S(1)} custom-call(bf16[1536,512]{1,0:T(8,128)(2,1)S(1)} %copy-done.1, f32[1536,512]{1,0:T(8,128)S(1)} %shard_map.50.refs_1_, bf16[2368,128]{1,0:T(8,128)(2,1)S(1)} %shard_map.59.refs_2_.refs_5_), custom_call_target="tpu_custom_call" | custom-call | tf_op jit(solution)/shard_map/pallas_call | solution.py:276
  65.9 0.0 collective-permute-done.15.refs_2_
  65.9 2.9 %shard_map.61 = (f32[1536,512]{1,0:T(8,128)}, f32[1]{0:T(128)}) custom-call(bf16[1536,512]{1,0:T(8,128)(2,1)S(1)} %copy-done.1, f32[1536,512]{1,0:T(8,128)S(1)} %shard_map.60.refs_1_, bf16[2368,128]{1,0:T(8,128)(2,1)S(1)} %collective-permute-done.15.refs_2_, bf16[2752,128]{1,0:T(8,128)(2,1)S(1)} %shard_map.49.own_ref.refs_3_, ...), custom_call_target="tpu_custom_call" | custom-call | tf_op jit(solution)/shard_map/pallas_call | solution.py:276
  (13 shorter events, 0.3 us)
Async XLA Ops:
  0.6 1.4 %copy-start = (bf16[1536,512]{1,0:T(8,128)(2,1)S(1)}, bf16[1536,512]{1,0:T(8,128)(2,1)}, u32[]{:S(2)}) copy-start(bf16[1536,512]{1,0:T(8,128)(2,1)} %refs_0_.11) | copy-start | bytes 4718596
  2.0 1.4 %copy-start.2 = (bf16[1536,512]{1,0:T(8,128)(2,1)S(1)}, bf16[1536,512]{1,0:T(8,128)(2,1)}, u32[]{:S(2)}) copy-start(bf16[1536,512]{1,0:T(8,128)(2,1)} %refs_1_.7) | copy-start | bytes 4718596
  4.5 2.7 %collective-permute-start = (bf16[2688,128]{1,0:T(8,128)(2,1)S(1)}, bf16[2688,128]{1,0:T(8,128)(2,1)S(1)}, u32[]{:S(2)}, u32[]{:S(2)}) collective-permute-start(bf16[2688,128]{1,0:T(8,128)(2,1)S(1)} %shard_map.42), channel_id=1, source_target_pairs={{0,1},{1,0},{2,3},{3,2},{4,5},{5,4},{6,7},{7,6},{8,9},{9,8},{10,11... | collective-permute-start | bytes 2064392 | tf_op jit(solution)/shard_map/ppermute | solution.py:307
  6.0 5.3 %collective-permute-start.8 = (bf16[2304,128]{1,0:T(8,128)(2,1)S(1)}, bf16[2304,128]{1,0:T(8,128)(2,1)S(1)}, u32[]{:S(2)}, u32[]{:S(2)}) collective-permute-start(bf16[2304,128]{1,0:T(8,128)(2,1)S(1)} %shard_map.52), channel_id=1, source_target_pairs={{0,1},{1,0},{2,3},{3,2},{4,5},{5,4},{6,7},{7,6},{8,9},{9,8},{10,11... | collective-permute-start | bytes 1769480 | tf_op jit(solution)/shard_map/ppermute | solution.py:307
  7.3 8.3 %collective-permute-start.1 = (bf16[1344,128]{1,0:T(8,128)(2,1)S(1)}, bf16[1344,128]{1,0:T(8,128)(2,1)S(1)}, u32[]{:S(2)}, u32[]{:S(2)}) collective-permute-start(bf16[1344,128]{1,0:T(8,128)(2,1)S(1)} %get-tuple-element.11), channel_id=1, source_target_pairs={{0,4},{1,3},{2,6},{3,1},{4,0},{5,7},{6,2},{7,5},{8,12},{9,11},{10,... | collective-permute-start | bytes 1032200 | tf_op jit(solution)/shard_map/ppermute | solution.py:307
  11.5 11.8 %collective-permute-start.9 = (bf16[1152,128]{1,0:T(8,128)(2,1)S(1)}, bf16[1152,128]{1,0:T(8,128)(2,1)S(1)}, u32[]{:S(2)}, u32[]{:S(2)}) collective-permute-start(bf16[1152,128]{1,0:T(8,128)(2,1)S(1)} %get-tuple-element.15), channel_id=1, source_target_pairs={{0,4},{1,3},{2,6},{3,1},{4,0},{5,7},{6,2},{7,5},{8,12},{9,11},{10,... | collective-permute-start | bytes 884744 | tf_op jit(solution)/shard_map/ppermute | solution.py:307
  15.6 5.5 %collective-permute-start.2 = (bf16[672,128]{1,0:T(8,128)(2,1)S(1)}, bf16[672,128]{1,0:T(8,128)(2,1)S(1)}, u32[]{:S(2)}, u32[]{:S(2)}) collective-permute-start(bf16[672,128]{1,0:T(8,128)(2,1)S(1)} %get-tuple-element.13), channel_id=1, source_target_pairs={{0,2},{1,5},{2,0},{3,7},{4,6},{5,1},{6,4},{7,3},{8,10},{9,13},{10,... | collective-permute-start | bytes 516104 | tf_op jit(solution)/shard_map/ppermute | solution.py:307
  21.2 6.9 %collective-permute-start.3 = (bf16[672,128]{1,0:T(8,128)(2,1)S(1)}, bf16[672,128]{1,0:T(8,128)(2,1)S(1)}, u32[]{:S(2)}, u32[]{:S(2)}) collective-permute-start(bf16[672,128]{1,0:T(8,128)(2,1)S(1)} %shard_map.45.a_ref), channel_id=1, source_target_pairs={{0,8},{1,17},{2,10},{3,19},{4,12},{5,21},{6,14},{7,23},{8,0},{9,25... | collective-permute-start | bytes 516104 | tf_op jit(solution)/shard_map/ppermute | solution.py:307
  23.4 39.9 %copy-start.1 = (bf16[1536,512]{1,0:T(8,128)(2,1)S(1)}, bf16[1536,512]{1,0:T(8,128)(2,1)}, u32[]{:S(2)}) copy-start(bf16[1536,512]{1,0:T(8,128)(2,1)} %refs_0_.11) | copy-start | bytes 4718596
  23.4 39.9 %copy-start.3 = (bf16[1536,512]{1,0:T(8,128)(2,1)S(1)}, bf16[1536,512]{1,0:T(8,128)(2,1)}, u32[]{:S(2)}) copy-start(bf16[1536,512]{1,0:T(8,128)(2,1)} %refs_1_.7) | copy-start | bytes 4718596
  23.4 7.3 %collective-permute-start.10 = (bf16[576,128]{1,0:T(8,128)(2,1)S(1)}, bf16[576,128]{1,0:T(8,128)(2,1)S(1)}, u32[]{:S(2)}, u32[]{:S(2)}) collective-permute-start(bf16[576,128]{1,0:T(8,128)(2,1)S(1)} %get-tuple-element.17), channel_id=1, source_target_pairs={{0,2},{1,5},{2,0},{3,7},{4,6},{5,1},{6,4},{7,3},{8,10},{9,13},{10,... | collective-permute-start | bytes 442376 | tf_op jit(solution)/shard_map/ppermute | solution.py:307
  28.2 11.1 %collective-permute-start.4 = (bf16[672,128]{1,0:T(8,128)(2,1)S(1)}, bf16[672,128]{1,0:T(8,128)(2,1)S(1)}, u32[]{:S(2)}, u32[]{:S(2)}) collective-permute-start(bf16[672,128]{1,0:T(8,128)(2,1)S(1)} %shard_map.46.refs_0_), channel_id=1, source_target_pairs={{0,16},{1,9},{2,18},{3,11},{4,20},{5,13},{6,22},{7,15},{8,24},{9,1... | collective-permute-start | bytes 516104 | tf_op jit(solution)/shard_map/ppermute | solution.py:307
  30.8 10.7 %collective-permute-start.11 = (bf16[576,128]{1,0:T(8,128)(2,1)S(1)}, bf16[576,128]{1,0:T(8,128)(2,1)S(1)}, u32[]{:S(2)}, u32[]{:S(2)}) collective-permute-start(bf16[576,128]{1,0:T(8,128)(2,1)S(1)} %shard_map.55.a_ref), channel_id=1, source_target_pairs={{0,8},{1,17},{2,10},{3,19},{4,12},{5,21},{6,14},{7,23},{8,0},{9,25... | collective-permute-start | bytes 442376 | tf_op jit(solution)/shard_map/ppermute | solution.py:307
  40.0 10.0 %collective-permute-start.5 = (bf16[688,128]{1,0:T(8,128)(2,1)S(1)}, bf16[688,128]{1,0:T(8,128)(2,1)S(1)}, u32[]{:S(2)}, u32[]{:S(2)}) collective-permute-start(bf16[688,128]{1,0:T(8,128)(2,1)S(1)} %shard_map.47.refs_0_), channel_id=1, source_target_pairs={{0,2},{1,5},{2,0},{3,7},{4,6},{5,1},{6,4},{7,3},{8,10},{9,13},{10,... | collective-permute-start | bytes 528392 | tf_op jit(solution)/shard_map/ppermute | solution.py:307
  41.5 7.7 %collective-permute-start.12 = (bf16[576,128]{1,0:T(8,128)(2,1)S(1)}, bf16[576,128]{1,0:T(8,128)(2,1)S(1)}, u32[]{:S(2)}, u32[]{:S(2)}) collective-permute-start(bf16[576,128]{1,0:T(8,128)(2,1)S(1)} %shard_map.56.refs_0_), channel_id=1, source_target_pairs={{0,16},{1,9},{2,18},{3,11},{4,20},{5,13},{6,22},{7,15},{8,24},{9,1... | collective-permute-start | bytes 442376 | tf_op jit(solution)/shard_map/ppermute | solution.py:307
  49.5 6.8 %collective-permute-start.13 = (bf16[592,128]{1,0:T(8,128)(2,1)S(1)}, bf16[592,128]{1,0:T(8,128)(2,1)S(1)}, u32[]{:S(2)}, u32[]{:S(2)}) collective-permute-start(bf16[592,128]{1,0:T(8,128)(2,1)S(1)} %shard_map.57.refs_0_), channel_id=1, source_target_pairs={{0,2},{1,5},{2,0},{3,7},{4,6},{5,1},{6,4},{7,3},{8,10},{9,13},{10,... | collective-permute-start | bytes 454664 | tf_op jit(solution)/shard_map/ppermute | solution.py:307
  50.0 7.6 %collective-permute-start.6 = (bf16[1376,128]{1,0:T(8,128)(2,1)S(1)}, bf16[1376,128]{1,0:T(8,128)(2,1)S(1)}, u32[]{:S(2)}, u32[]{:S(2)}) collective-permute-start(bf16[1376,128]{1,0:T(8,128)(2,1)S(1)} %shard_map.48.refs_0_), channel_id=1, source_target_pairs={{0,4},{1,3},{2,6},{3,1},{4,0},{5,7},{6,2},{7,5},{8,12},{9,11},{10,... | collective-permute-start | bytes 1056776 | tf_op jit(solution)/shard_map/ppermute | solution.py:307
  56.3 6.9 %collective-permute-start.14 = (bf16[1184,128]{1,0:T(8,128)(2,1)S(1)}, bf16[1184,128]{1,0:T(8,128)(2,1)S(1)}, u32[]{:S(2)}, u32[]{:S(2)}) collective-permute-start(bf16[1184,128]{1,0:T(8,128)(2,1)S(1)} %shard_map.58.refs_0_), channel_id=1, source_target_pairs={{0,4},{1,3},{2,6},{3,1},{4,0},{5,7},{6,2},{7,5},{8,12},{9,11},{10,... | collective-permute-start | bytes 909320 | tf_op jit(solution)/shard_map/ppermute | solution.py:307
  57.6 5.7 %collective-permute-start.7 = (bf16[2752,128]{1,0:T(8,128)(2,1)S(1)}, bf16[2752,128]{1,0:T(8,128)(2,1)S(1)}, u32[]{:S(2)}, u32[]{:S(2)}) collective-permute-start(bf16[2752,128]{1,0:T(8,128)(2,1)S(1)} %shard_map.49.own_ref.refs_3_), channel_id=1, source_target_pairs={{0,1},{1,0},{2,3},{3,2},{4,5},{5,4},{6,7},{7,6},{8,9},{9,8},{10,11... | collective-permute-start | bytes 2113544 | tf_op jit(solution)/shard_map/ppermute | solution.py:307
  63.2 2.7 %collective-permute-start.15 = (bf16[2368,128]{1,0:T(8,128)(2,1)S(1)}, bf16[2368,128]{1,0:T(8,128)(2,1)S(1)}, u32[]{:S(2)}, u32[]{:S(2)}) collective-permute-start(bf16[2368,128]{1,0:T(8,128)(2,1)S(1)} %shard_map.59.refs_2_.refs_5_), channel_id=1, source_target_pairs={{0,1},{1,0},{2,3},{3,2},{4,5},{5,4},{6,7},{7,6},{8,9},{9,8},{10,11... | collective-permute-start | bytes 1818632 | tf_op jit(solution)/shard_map/ppermute | solution.py:307

commit v4 on v3

--- a/solution.py
+++ b/solution.py
@@ -31,16 +31,20 @@
     return side, extra, near_at, far_at
 
 
+def parity(r, c):
+    return (r ^ (r >> 1) ^ (c >> 1)) & 1
+
+
 def position():
     r, c = lax.axis_index("gr"), lax.axis_index("gc")
-    core = c & 1
+    half = (c & 1) ^ parity(r, c)
     on_r, on_c = r & 1, (c >> 1) & 1
-    return core, jnp.where(core == 0, on_r, on_c), jnp.where(core == 0, on_c, on_r)
+    return half, jnp.where(half == 0, on_r, on_c), jnp.where(half == 0, on_c, on_r)
 
 
 def starts(flip, side):
-    core, _, _ = position()
-    h = core ^ flip
+    half, _, _ = position()
+    h = half ^ flip
     low = pl.multiple_of(h * (side * TILE), TILE)
     up = pl.multiple_of((1 - h) * (side * TILE), TILE)
     return h, low, up
@@ -104,6 +108,36 @@
     )(*operands)
 
 
+def load_kernel(orb_hbm, vel_hbm, away_ref, orb_ref, vel_ref, sems):
+    total_rows = orb_hbm.shape[0]
+    _, low, up = starts(1, layout(total_rows)[0])
+    rows = total_rows // 4
+    copies = []
+    for at in (low, low + rows, up, up + rows):
+        for source, target in ((orb_hbm, orb_ref), (vel_hbm, vel_ref)):
+            part = pl.ds(pl.multiple_of(at, TILE), rows)
+            copies.append(pltpu.make_async_copy(source.at[part], target.at[part], sems.at[len(copies)]))
+            copies[-1].start()
+    for copy in copies[:4]:
+        copy.wait()
+    product_kernel(orb_ref, vel_ref, away_ref, flip=1, chunk=0, total_rows=total_rows)
+    for copy in copies[4:]:
+        copy.wait()
+
+
+def load(orb, vel):
+    rows = orb.shape[0]
+    whole = jax.ShapeDtypeStruct(orb.shape, orb.dtype)
+    return pl.pallas_call(
+        load_kernel,
+        out_shape=[jax.ShapeDtypeStruct((tile_count(0, rows) * TILE, TILE), BF16), whole, whole],
+        in_specs=[pl.BlockSpec(memory_space=pltpu.HBM)] * 2,
+        out_specs=[VMEM] * 3,
+        scratch_shapes=[pltpu.SemaphoreType.DMA((8,))],
+        compiler_params=params(12),
+    )(orb, vel)
+
+
 def product(flip, orb, vel, chunk):
     rows = orb.shape[0]
     return call(
@@ -234,9 +268,12 @@
     total_rows = orb_ref.shape[0]
     side, extra, _, far_at = layout(total_rows)
     h, low, up = starts(flip, side)
-    out_ref, b_ref, t_ref = refs[-3:]
-    if len(refs) > 3:
-        near_own, near_far, own, out_ref, norm_ref = refs[:5]
+    if len(refs) == 3:
+        out_ref, b_ref, t_ref = refs
+        copies = None
+    else:
+        near_own, near_far, own, hbm_ref, norm_ref, b_ref, t_ref, out_ref, sems = refs
+        copies = []
         square = (tails(near_own) + tails(own)) + (tails(near_far) + tails(piece_ref))
         norm_ref[0] = (jnp.sqrt(square) / total_rows)[0, 0]
     zero = jnp.zeros((TILE, TILE), BF16)
@@ -254,32 +291,43 @@
         at = pl.multiple_of((h * extra + k) * TILE, TILE)
         b_ref[pl.ds(at, TILE), pl.ds(at, TILE)] = value
         t_ref[pl.ds(at, TILE), pl.ds(at, TILE)] = value.T
+
+    def put(at, value):
+        out_ref[at, :] = base_ref[at, :] - 0.5 * value
+        if copies is not None:
+            copy = pltpu.make_async_copy(out_ref.at[at], hbm_ref.at[at], sems.at[len(copies)])
+            copy.start()
+            copies.append(copy)
+
     wide = side * TILE
     panel = 2 * TILE
     for p in range(0, wide, panel):
         end = min(p + panel, wide)
         value = jnp.dot(b_ref[p:end, :end], orb_ref[pl.ds(up, end), :], preferred_element_type=F32)
-        at = pl.ds(low + p, end - p)
-        out_ref[at, :] = base_ref[at, :] - 0.5 * value
+        put(pl.ds(pl.multiple_of(low + p, TILE), end - p), value)
         value = jnp.dot(t_ref[p:end, p:], orb_ref[pl.ds(low + p, wide - p), :], preferred_element_type=F32)
-        at = pl.ds(up + p, end - p)
-        out_ref[at, :] = base_ref[at, :] - 0.5 * value
+        put(pl.ds(pl.multiple_of(up + p, TILE), end - p), value)
+    for copy in copies or ():
+        copy.wait()
 
 
 def apply_far(flip, orb, base, piece, others=()):
     wide = orb.shape[0] // 2
     out_shape = [jax.ShapeDtypeStruct(orb.shape, F32)]
     out_specs = [VMEM]
+    scratch = [pltpu.VMEM((wide, wide), BF16)] * 2
     if others:
         out_shape.append(jax.ShapeDtypeStruct((1,), F32))
-        out_specs.append(SMEM)
+        out_specs = [pl.BlockSpec(memory_space=pltpu.HBM), SMEM]
+        panels = -(-wide // (2 * TILE))
+        scratch += [pltpu.VMEM(orb.shape, F32), pltpu.SemaphoreType.DMA((2 * panels,))]
     return pl.pallas_call(
         lambda *refs: far_kernel(*refs, flip=flip),
         out_shape=out_shape,
         in_specs=[VMEM] * (3 + len(others)),
         out_specs=out_specs,
-        scratch_shapes=[pltpu.VMEM((wide, wide), BF16)] * 2,
-        compiler_params=params(8),
+        scratch_shapes=scratch,
+        compiler_params=params(12 if others else 8),
     )(orb, base, piece, *others)
 
 
@@ -287,15 +335,15 @@
     result = []
     for r in range(nr):
         for c in range(nc):
-            flip = odd if c & 1 else even
-            result.append((r * nc + c, (r ^ flip[0]) * nc + (c ^ flip[1])))
+            on_r, on_c = odd if (c & 1) ^ parity(r, c) else even
+            result.append((r * nc + c, (r ^ on_r) * nc + (c ^ on_c ^ parity(on_r, on_c))))
     return result
 
 
 def local(orbitals, velocities):
     nr, nc = lax.axis_size("gr"), lax.axis_size("gc")
     side, _, near_at, _ = layout(orbitals.shape[0])
-    swap = pairs(nr, nc, (0, 1), (0, 1))
+    swap = [(d, d ^ 1) for d in range(nr * nc)]
     first = pairs(nr, nc, (1, 0), (0, 2))
     second = pairs(nr, nc, (0, 2), (1, 0))
     rest = [(1 << b, 0) for b in range(1, nr.bit_length() - 1)]
@@ -308,7 +356,10 @@
 
     joined = []
     for k in range(2):
-        away = product(1, orbitals, velocities, k)
+        if k == 0:
+            away, orbitals, velocities = load(orbitals, velocities)
+        else:
+            away = product(1, orbitals, velocities, k)
         got = move(away, swap)
         mine = product(0, orbitals, velocities, k)
         send, mine = halve(mine, got, 1)

time: 69 us -> 66.3 us (0.961)
  waiting for transfers between devices: 34.2 us -> 29.6 us
  Pallas kernels: 11.3 us -> 12.8 us
    ppermute x16, waiting for transfers between devices: 34.2 us -> 29.6 us  [move(): return lax.ppermute(value, AXES, perm)]
    pallas_call x0 -> x1, Pallas kernels: none -> 2.59 us  [load(): pl.pallas_call(load_kernel, out_shape=[jax.ShapeDtypeStruct((tile_count(0...]
    pallas_call x19 -> x18, Pallas kernels: 7.21 us -> 6.21 us  [call(): pl.pallas_call(kernel, out_shape=out, in_specs=[VMEM] * len(operands), ou...]
    unnamed x8 -> x4, local copies, waits for them, and re-layouts: 2.82 us -> 2.81 us
  transfers between devices with their start and end apart: 16 -> 16, of which waited for: 7 -> 9; matrix products, arithmetic and copies ran while one was open for 0% -> 0% of each run, Pallas kernels for 11% -> 11%
where the time goes in v4:
time: 66.3 us; the launch traced here: 66.1 us
  waiting for transfers between devices  29.6 us (45%)
  starting transfers between devices  20.1 us (30%)
  Pallas kernels  12.8 us (19%)
  local copies, waits for them, and re-layouts  2.81 us (4%)
  between operations  0.8 us (1%)
    ppermute x16, waiting for transfers between devices, move(): return lax.ppermute(value, AXES, perm)  29.6 us
    ppermute x16, starting transfers between devices, move(): return lax.ppermute(value, AXES, perm)  20.1 us
    pallas_call x18, Pallas kernels, call(): pl.pallas_call(kernel, out_shape=out, in_specs=[VMEM] * len(operands), ou...  6.21 us
    pallas_call x2, Pallas kernels, apply_far(): pl.pallas_call(lambda *refs: far_kernel(*refs, flip=flip), out_shape=out_...  4.04 us
    unnamed x4, local copies, waits for them, and re-layouts  2.81 us
    pallas_call x1, Pallas kernels, load(): pl.pallas_call(load_kernel, out_shape=[jax.ShapeDtypeStruct((tile_count(0...  2.59 us
  transfers between devices with their start and end apart: 16, of which 9 were waited for; matrix products, arithmetic and copies ran while one was open for 0% of the time, Pallas kernels for 11%

profile of v4, /device:TPU:0, one launch (start us, length us, event | category | flops | bytes accessed | tf_op | source)
XLA Modules:
  0.0 66.1 jit_solution(14969714504348503443)
XLA Ops:
  0.6 1.4 %copy-done = bf16[1536,512]{1,0:T(8,128)(2,1)S(1)} copy-done((bf16[1536,512]{1,0:T(8,128)(2,1)S(1)}, bf16[1536,512]{1,0:T(8,128)(2,1)}, u32[]{:S(2)}) %copy-start) | copy-done | bytes 1572888
  2.0 1.4 %copy-done.1 = bf16[1536,512]{1,0:T(8,128)(2,1)S(1)} copy-done((bf16[1536,512]{1,0:T(8,128)(2,1)S(1)}, bf16[1536,512]{1,0:T(8,128)(2,1)}, u32[]{:S(2)}) %copy-start.1) | copy-done | bytes 1572888
  3.4 2.6 %shard_map.41 = (bf16[2688,128]{1,0:T(8,128)(2,1)S(1)}, bf16[1536,512]{1,0:T(8,128)(2,1)S(1)}, bf16[1536,512]{1,0:T(8,128)(2,1)S(1)}) custom-call(bf16[1536,512]{1,0:T(8,128)(2,1)S(1)} %copy-done, bf16[1536,512]{1,0:T(8,128)(2,1)S(1)} %copy-done.1), custom_call_target="tpu_custom_call" | custom-call | tf_op jit(solution)/shard_map/pallas_call | solution.py:131
  6.0 0.6 collective-permute-start
  6.6 1.0 %shard_map.52 = bf16[2304,128]{1,0:T(8,128)(2,1)S(1)} custom-call(bf16[1536,512]{1,0:T(8,128)(2,1)S(1)} %get-tuple-element.13.refs_0_.orb_ref, bf16[1536,512]{1,0:T(8,128)(2,1)S(1)} %get-tuple-element.14.refs_1_.vel_ref), custom_call_target="tpu_custom_call" | custom-call | tf_op jit(solution)/shard_map/pallas_call | solution.py:101
  7.6 0.1 collective-permute-start.8
  7.7 1.0 %shard_map.42.refs_0_ = bf16[2688,128]{1,0:T(8,128)(2,1)S(1)} custom-call(bf16[1536,512]{1,0:T(8,128)(2,1)S(1)} %get-tuple-element.13.refs_0_.orb_ref, bf16[1536,512]{1,0:T(8,128)(2,1)S(1)} %get-tuple-element.14.refs_1_.vel_ref), custom_call_target="tpu_custom_call" | custom-call | tf_op jit(solution)/shard_map/pallas_call | solution.py:101
  8.7 0.0 collective-permute-done.refs_1_
  8.7 0.2 shard_map.43
  8.9 2.6 %collective-permute-start.1 = (bf16[1344,128]{1,0:T(8,128)(2,1)S(1)}, bf16[1344,128]{1,0:T(8,128)(2,1)S(1)}, u32[]{:S(2)}, u32[]{:S(2)}) collective-permute-start(bf16[1344,128]{1,0:T(8,128)(2,1)S(1)} %get-tuple-element.17), channel_id=1, source_target_pairs={{0,5},{1,2},{2,1},{3,6},{4,7},{5,0},{6,3},{7,4},{8,11},{9,12},{10,... | collective-permute-start | bytes 1032200 | tf_op jit(solution)/shard_map/ppermute | solution.py:355
  11.6 1.0 %shard_map.51.refs_0_ = bf16[2304,128]{1,0:T(8,128)(2,1)S(1)} custom-call(bf16[1536,512]{1,0:T(8,128)(2,1)S(1)} %get-tuple-element.13.refs_0_.orb_ref, bf16[1536,512]{1,0:T(8,128)(2,1)S(1)} %get-tuple-element.14.refs_1_.vel_ref), custom_call_target="tpu_custom_call" | custom-call | tf_op jit(solution)/shard_map/pallas_call | solution.py:101
  12.6 0.0 collective-permute-done.8.refs_1_
  12.6 0.1 shard_map.53
  12.7 0.1 collective-permute-start.9
  12.8 3.7 %collective-permute-done.1.refs_1_ = bf16[1344,128]{1,0:T(8,128)(2,1)S(1)} collective-permute-done((bf16[1344,128]{1,0:T(8,128)(2,1)S(1)}, bf16[1344,128]{1,0:T(8,128)(2,1)S(1)}, u32[]{:S(2)}, u32[]{:S(2)}) %collective-permute-start.1) | collective-permute-done | bytes 344096 | tf_op jit(solution)/shard_map/ppermute | solution.py:355
  16.5 0.1 shard_map.44
  16.6 2.1 %collective-permute-start.2 = (bf16[672,128]{1,0:T(8,128)(2,1)S(1)}, bf16[672,128]{1,0:T(8,128)(2,1)S(1)}, u32[]{:S(2)}, u32[]{:S(2)}) collective-permute-start(bf16[672,128]{1,0:T(8,128)(2,1)S(1)} %get-tuple-element.19), channel_id=1, source_target_pairs={{0,3},{1,4},{2,7},{3,0},{4,1},{5,6},{6,5},{7,2},{8,13},{9,10},{10,... | collective-permute-start | bytes 516104 | tf_op jit(solution)/shard_map/ppermute | solution.py:355
  18.7 3.5 %collective-permute-done.2.b_ref = bf16[672,128]{1,0:T(8,128)(2,1)S(1)} collective-permute-done((bf16[672,128]{1,0:T(8,128)(2,1)S(1)}, bf16[672,128]{1,0:T(8,128)(2,1)S(1)}, u32[]{:S(2)}, u32[]{:S(2)}) %collective-permute-start.2) | collective-permute-done | bytes 172064 | tf_op jit(solution)/shard_map/ppermute | solution.py:355
  22.2 1.5 %collective-permute-start.3 = (bf16[672,128]{1,0:T(8,128)(2,1)S(1)}, bf16[672,128]{1,0:T(8,128)(2,1)S(1)}, u32[]{:S(2)}, u32[]{:S(2)}) collective-permute-start(bf16[672,128]{1,0:T(8,128)(2,1)S(1)} %shard_map.45.a_ref), channel_id=1, source_target_pairs={{0,9},{1,17},{2,18},{3,10},{4,20},{5,12},{6,15},{7,23},{8,24},{9,0... | collective-permute-start | bytes 516104 | tf_op jit(solution)/shard_map/ppermute | solution.py:355
  23.7 0.0 collective-permute-done.9.refs_1_
  23.8 1.6 %collective-permute-start.10 = (bf16[576,128]{1,0:T(8,128)(2,1)S(1)}, bf16[576,128]{1,0:T(8,128)(2,1)S(1)}, u32[]{:S(2)}, u32[]{:S(2)}) collective-permute-start(bf16[576,128]{1,0:T(8,128)(2,1)S(1)} %get-tuple-element.23), channel_id=1, source_target_pairs={{0,3},{1,4},{2,7},{3,0},{4,1},{5,6},{6,5},{7,2},{8,13},{9,10},{10,... | collective-permute-start | bytes 442376 | tf_op jit(solution)/shard_map/ppermute | solution.py:355
  25.4 3.6 %collective-permute-done.3.b_ref = bf16[672,128]{1,0:T(8,128)(2,1)S(1)} collective-permute-done((bf16[672,128]{1,0:T(8,128)(2,1)S(1)}, bf16[672,128]{1,0:T(8,128)(2,1)S(1)}, u32[]{:S(2)}, u32[]{:S(2)}) %collective-permute-start.3) | collective-permute-done | bytes 172064 | tf_op jit(solution)/shard_map/ppermute | solution.py:355
  29.0 2.3 %collective-permute-start.4 = (bf16[672,128]{1,0:T(8,128)(2,1)S(1)}, bf16[672,128]{1,0:T(8,128)(2,1)S(1)}, u32[]{:S(2)}, u32[]{:S(2)}) collective-permute-start(bf16[672,128]{1,0:T(8,128)(2,1)S(1)} %shard_map.46.refs_0_), channel_id=1, source_target_pairs={{0,16},{1,8},{2,11},{3,19},{4,13},{5,21},{6,22},{7,14},{8,1},{9,25... | collective-permute-start | bytes 516104 | tf_op jit(solution)/shard_map/ppermute | solution.py:355
  31.3 0.0 collective-permute-done.10.b_ref
  31.4 0.7 %collective-permute-start.11 = (bf16[576,128]{1,0:T(8,128)(2,1)S(1)}, bf16[576,128]{1,0:T(8,128)(2,1)S(1)}, u32[]{:S(2)}, u32[]{:S(2)}) collective-permute-start(bf16[576,128]{1,0:T(8,128)(2,1)S(1)} %shard_map.55.a_ref), channel_id=1, source_target_pairs={{0,9},{1,17},{2,18},{3,10},{4,20},{5,12},{6,15},{7,23},{8,24},{9,0... | collective-permute-start | bytes 442376 | tf_op jit(solution)/shard_map/ppermute | solution.py:355
  32.0 6.8 %collective-permute-done.4.refs_1_ = bf16[672,128]{1,0:T(8,128)(2,1)S(1)} collective-permute-done((bf16[672,128]{1,0:T(8,128)(2,1)S(1)}, bf16[672,128]{1,0:T(8,128)(2,1)S(1)}, u32[]{:S(2)}, u32[]{:S(2)}) %collective-permute-start.4) | collective-permute-done | bytes 172064 | tf_op jit(solution)/shard_map/ppermute | solution.py:355
  38.9 0.7 %shard_map.47.refs_0_ = bf16[688,128]{1,0:T(8,128)(2,1)S(1)} custom-call(bf16[672,128]{1,0:T(8,128)(2,1)S(1)} %shard_map.46.refs_0_, bf16[672,128]{1,0:T(8,128)(2,1)S(1)} %collective-permute-done.4.refs_1_), custom_call_target="tpu_custom_call" | custom-call | tf_op jit(solution)/shard_map/pallas_call | solution.py:101
  39.6 0.0 collective-permute-start.5
  39.6 0.6 collective-permute-done.11.b_ref
  40.2 0.2 collective-permute-start.12
  40.5 6.0 %collective-permute-done.12.refs_1_ = bf16[576,128]{1,0:T(8,128)(2,1)S(1)} collective-permute-done((bf16[576,128]{1,0:T(8,128)(2,1)S(1)}, bf16[576,128]{1,0:T(8,128)(2,1)S(1)}, u32[]{:S(2)}, u32[]{:S(2)}) %collective-permute-start.12) | collective-permute-done | bytes 147488 | tf_op jit(solution)/shard_map/ppermute | solution.py:355
  46.5 0.2 shard_map.57.refs_0_
  46.7 0.0 collective-permute-start.13
  46.7 0.0 collective-permute-done.5.refs_1_
  46.8 3.7 %collective-permute-start.6 = (bf16[1376,128]{1,0:T(8,128)(2,1)S(1)}, bf16[1376,128]{1,0:T(8,128)(2,1)S(1)}, u32[]{:S(2)}, u32[]{:S(2)}) collective-permute-start(bf16[1376,128]{1,0:T(8,128)(2,1)S(1)} %shard_map.48.refs_0_), channel_id=1, source_target_pairs={{0,5},{1,2},{2,1},{3,6},{4,7},{5,0},{6,3},{7,4},{8,11},{9,12},{10,... | collective-permute-start | bytes 1056776 | tf_op jit(solution)/shard_map/ppermute | solution.py:355
  50.4 1.1 %collective-permute-done.13.refs_1_ = bf16[592,128]{1,0:T(8,128)(2,1)S(1)} collective-permute-done((bf16[592,128]{1,0:T(8,128)(2,1)S(1)}, bf16[592,128]{1,0:T(8,128)(2,1)S(1)}, u32[]{:S(2)}, u32[]{:S(2)}) %collective-permute-start.13) | collective-permute-done | bytes 151584 | tf_op jit(solution)/shard_map/ppermute | solution.py:355
  51.5 4.4 %collective-permute-start.14 = (bf16[1184,128]{1,0:T(8,128)(2,1)S(1)}, bf16[1184,128]{1,0:T(8,128)(2,1)S(1)}, u32[]{:S(2)}, u32[]{:S(2)}) collective-permute-start(bf16[1184,128]{1,0:T(8,128)(2,1)S(1)} %shard_map.58.refs_0_), channel_id=1, source_target_pairs={{0,5},{1,2},{2,1},{3,6},{4,7},{5,0},{6,3},{7,4},{8,11},{9,12},{10,... | collective-permute-start | bytes 909320 | tf_op jit(solution)/shard_map/ppermute | solution.py:355
  55.9 0.2 collective-permute-done.6.refs_1_
  56.2 0.1 shard_map.49.own_ref.refs_3_
  56.2 0.1 collective-permute-start.7
  56.3 4.1 %collective-permute-done.14.refs_1_ = bf16[1184,128]{1,0:T(8,128)(2,1)S(1)} collective-permute-done((bf16[1184,128]{1,0:T(8,128)(2,1)S(1)}, bf16[1184,128]{1,0:T(8,128)(2,1)S(1)}, u32[]{:S(2)}, u32[]{:S(2)}) %collective-permute-start.14) | collective-permute-done | bytes 303136 | tf_op jit(solution)/shard_map/ppermute | solution.py:355
  60.4 0.1 shard_map.59.refs_2_.refs_5_
  60.5 0.1 collective-permute-start.15
  60.6 0.0 collective-permute-done.7.far_ref.refs_4_
  60.6 1.5 %shard_map.50.refs_1_ = f32[1536,512]{1,0:T(8,128)S(1)} custom-call(bf16[1536,512]{1,0:T(8,128)(2,1)S(1)} %get-tuple-element.13.refs_0_.orb_ref, bf16[1536,512]{1,0:T(8,128)(2,1)S(1)} %get-tuple-element.14.refs_1_.vel_ref, bf16[2752,128]{1,0:T(8,128)(2,1)S(1)} %shard_map.49.own_ref.refs_3_, bf16[2752,128]{1,0:T(8,128)(2,1)S(1)} %collective-permute-done.7.far_ref.refs_4_), custom_call_target="tpu_custom_call" | custom-call | tf_op jit(solution)/shard_map/pallas_call | solution.py:101
  62.1 1.3 %shard_map.60.refs_1_ = f32[1536,512]{1,0:T(8,128)S(1)} custom-call(bf16[1536,512]{1,0:T(8,128)(2,1)S(1)} %get-tuple-element.13.refs_0_.orb_ref, f32[1536,512]{1,0:T(8,128)S(1)} %shard_map.50.refs_1_, bf16[2368,128]{1,0:T(8,128)(2,1)S(1)} %shard_map.59.refs_2_.refs_5_), custom_call_target="tpu_custom_call" | custom-call | tf_op jit(solution)/shard_map/pallas_call | solution.py:324
  63.3 0.0 collective-permute-done.15.refs_2_
  63.4 2.8 %shard_map.61 = (f32[1536,512]{1,0:T(8,128)}, f32[1]{0:T(128)}) custom-call(bf16[1536,512]{1,0:T(8,128)(2,1)S(1)} %get-tuple-element.13.refs_0_.orb_ref, f32[1536,512]{1,0:T(8,128)S(1)} %shard_map.60.refs_1_, bf16[2368,128]{1,0:T(8,128)(2,1)S(1)} %collective-permute-done.15.refs_2_, bf16[2752,128]{1,0:T(8,128)(2,1)S(1)} %shard_map.49.own_ref.refs_3_, ...), custom_call_target="tpu_custom_call" | custom-call | tf_op jit(solution)/shard_map/pallas_call | solution.py:324
  (9 shorter events, 0.3 us)
Async XLA Ops:
  0.6 1.4 %copy-start = (bf16[1536,512]{1,0:T(8,128)(2,1)S(1)}, bf16[1536,512]{1,0:T(8,128)(2,1)}, u32[]{:S(2)}) copy-start(bf16[1536,512]{1,0:T(8,128)(2,1)} %orb_hbm.1) | copy-start | bytes 4718596
  2.0 1.4 %copy-start.1 = (bf16[1536,512]{1,0:T(8,128)(2,1)S(1)}, bf16[1536,512]{1,0:T(8,128)(2,1)}, u32[]{:S(2)}) copy-start(bf16[1536,512]{1,0:T(8,128)(2,1)} %vel_hbm.1) | copy-start | bytes 4718596
  6.0 2.7 %collective-permute-start = (bf16[2688,128]{1,0:T(8,128)(2,1)S(1)}, bf16[2688,128]{1,0:T(8,128)(2,1)S(1)}, u32[]{:S(2)}, u32[]{:S(2)}) collective-permute-start(bf16[2688,128]{1,0:T(8,128)(2,1)S(1)} %get-tuple-element.15), channel_id=1, source_target_pairs={{0,1},{1,0},{2,3},{3,2},{4,5},{5,4},{6,7},{7,6},{8,9},{9,8},{10,11... | collective-permute-start | bytes 2064392 | tf_op jit(solution)/shard_map/ppermute | solution.py:355
  7.6 5.0 %collective-permute-start.8 = (bf16[2304,128]{1,0:T(8,128)(2,1)S(1)}, bf16[2304,128]{1,0:T(8,128)(2,1)S(1)}, u32[]{:S(2)}, u32[]{:S(2)}) collective-permute-start(bf16[2304,128]{1,0:T(8,128)(2,1)S(1)} %shard_map.52), channel_id=1, source_target_pairs={{0,1},{1,0},{2,3},{3,2},{4,5},{5,4},{6,7},{7,6},{8,9},{9,8},{10,11... | collective-permute-start | bytes 1769480 | tf_op jit(solution)/shard_map/ppermute | solution.py:355
  8.9 7.6 %collective-permute-start.1 = (bf16[1344,128]{1,0:T(8,128)(2,1)S(1)}, bf16[1344,128]{1,0:T(8,128)(2,1)S(1)}, u32[]{:S(2)}, u32[]{:S(2)}) collective-permute-start(bf16[1344,128]{1,0:T(8,128)(2,1)S(1)} %get-tuple-element.17), channel_id=1, source_target_pairs={{0,5},{1,2},{2,1},{3,6},{4,7},{5,0},{6,3},{7,4},{8,11},{9,12},{10,... | collective-permute-start | bytes 1032200 | tf_op jit(solution)/shard_map/ppermute | solution.py:355
  12.7 11.0 %collective-permute-start.9 = (bf16[1152,128]{1,0:T(8,128)(2,1)S(1)}, bf16[1152,128]{1,0:T(8,128)(2,1)S(1)}, u32[]{:S(2)}, u32[]{:S(2)}) collective-permute-start(bf16[1152,128]{1,0:T(8,128)(2,1)S(1)} %get-tuple-element.21), channel_id=1, source_target_pairs={{0,5},{1,2},{2,1},{3,6},{4,7},{5,0},{6,3},{7,4},{8,11},{9,12},{10,... | collective-permute-start | bytes 884744 | tf_op jit(solution)/shard_map/ppermute | solution.py:355
  16.6 5.6 %collective-permute-start.2 = (bf16[672,128]{1,0:T(8,128)(2,1)S(1)}, bf16[672,128]{1,0:T(8,128)(2,1)S(1)}, u32[]{:S(2)}, u32[]{:S(2)}) collective-permute-start(bf16[672,128]{1,0:T(8,128)(2,1)S(1)} %get-tuple-element.19), channel_id=1, source_target_pairs={{0,3},{1,4},{2,7},{3,0},{4,1},{5,6},{6,5},{7,2},{8,13},{9,10},{10,... | collective-permute-start | bytes 516104 | tf_op jit(solution)/shard_map/ppermute | solution.py:355
  22.2 6.7 %collective-permute-start.3 = (bf16[672,128]{1,0:T(8,128)(2,1)S(1)}, bf16[672,128]{1,0:T(8,128)(2,1)S(1)}, u32[]{:S(2)}, u32[]{:S(2)}) collective-permute-start(bf16[672,128]{1,0:T(8,128)(2,1)S(1)} %shard_map.45.a_ref), channel_id=1, source_target_pairs={{0,9},{1,17},{2,18},{3,10},{4,20},{5,12},{6,15},{7,23},{8,24},{9,0... | collective-permute-start | bytes 516104 | tf_op jit(solution)/shard_map/ppermute | solution.py:355
  23.8 7.6 %collective-permute-start.10 = (bf16[576,128]{1,0:T(8,128)(2,1)S(1)}, bf16[576,128]{1,0:T(8,128)(2,1)S(1)}, u32[]{:S(2)}, u32[]{:S(2)}) collective-permute-start(bf16[576,128]{1,0:T(8,128)(2,1)S(1)} %get-tuple-element.23), channel_id=1, source_target_pairs={{0,3},{1,4},{2,7},{3,0},{4,1},{5,6},{6,5},{7,2},{8,13},{9,10},{10,... | collective-permute-start | bytes 442376 | tf_op jit(solution)/shard_map/ppermute | solution.py:355
  29.0 9.9 %collective-permute-start.4 = (bf16[672,128]{1,0:T(8,128)(2,1)S(1)}, bf16[672,128]{1,0:T(8,128)(2,1)S(1)}, u32[]{:S(2)}, u32[]{:S(2)}) collective-permute-start(bf16[672,128]{1,0:T(8,128)(2,1)S(1)} %shard_map.46.refs_0_), channel_id=1, source_target_pairs={{0,16},{1,8},{2,11},{3,19},{4,13},{5,21},{6,22},{7,14},{8,1},{9,25... | collective-permute-start | bytes 516104 | tf_op jit(solution)/shard_map/ppermute | solution.py:355
  31.4 8.8 %collective-permute-start.11 = (bf16[576,128]{1,0:T(8,128)(2,1)S(1)}, bf16[576,128]{1,0:T(8,128)(2,1)S(1)}, u32[]{:S(2)}, u32[]{:S(2)}) collective-permute-start(bf16[576,128]{1,0:T(8,128)(2,1)S(1)} %shard_map.55.a_ref), channel_id=1, source_target_pairs={{0,9},{1,17},{2,18},{3,10},{4,20},{5,12},{6,15},{7,23},{8,24},{9,0... | collective-permute-start | bytes 442376 | tf_op jit(solution)/shard_map/ppermute | solution.py:355
  39.6 7.1 %collective-permute-start.5 = (bf16[688,128]{1,0:T(8,128)(2,1)S(1)}, bf16[688,128]{1,0:T(8,128)(2,1)S(1)}, u32[]{:S(2)}, u32[]{:S(2)}) collective-permute-start(bf16[688,128]{1,0:T(8,128)(2,1)S(1)} %shard_map.47.refs_0_), channel_id=1, source_target_pairs={{0,3},{1,4},{2,7},{3,0},{4,1},{5,6},{6,5},{7,2},{8,13},{9,10},{10,... | collective-permute-start | bytes 528392 | tf_op jit(solution)/shard_map/ppermute | solution.py:355
  40.2 6.2 %collective-permute-start.12 = (bf16[576,128]{1,0:T(8,128)(2,1)S(1)}, bf16[576,128]{1,0:T(8,128)(2,1)S(1)}, u32[]{:S(2)}, u32[]{:S(2)}) collective-permute-start(bf16[576,128]{1,0:T(8,128)(2,1)S(1)} %shard_map.56.refs_0_), channel_id=1, source_target_pairs={{0,16},{1,8},{2,11},{3,19},{4,13},{5,21},{6,22},{7,14},{8,1},{9,25... | collective-permute-start | bytes 442376 | tf_op jit(solution)/shard_map/ppermute | solution.py:355
  46.7 4.8 %collective-permute-start.13 = (bf16[592,128]{1,0:T(8,128)(2,1)S(1)}, bf16[592,128]{1,0:T(8,128)(2,1)S(1)}, u32[]{:S(2)}, u32[]{:S(2)}) collective-permute-start(bf16[592,128]{1,0:T(8,128)(2,1)S(1)} %shard_map.57.refs_0_), channel_id=1, source_target_pairs={{0,3},{1,4},{2,7},{3,0},{4,1},{5,6},{6,5},{7,2},{8,13},{9,10},{10,... | collective-permute-start | bytes 454664 | tf_op jit(solution)/shard_map/ppermute | solution.py:355
  46.8 9.4 %collective-permute-start.6 = (bf16[1376,128]{1,0:T(8,128)(2,1)S(1)}, bf16[1376,128]{1,0:T(8,128)(2,1)S(1)}, u32[]{:S(2)}, u32[]{:S(2)}) collective-permute-start(bf16[1376,128]{1,0:T(8,128)(2,1)S(1)} %shard_map.48.refs_0_), channel_id=1, source_target_pairs={{0,5},{1,2},{2,1},{3,6},{4,7},{5,0},{6,3},{7,4},{8,11},{9,12},{10,... | collective-permute-start | bytes 1056776 | tf_op jit(solution)/shard_map/ppermute | solution.py:355
  51.5 8.9 %collective-permute-start.14 = (bf16[1184,128]{1,0:T(8,128)(2,1)S(1)}, bf16[1184,128]{1,0:T(8,128)(2,1)S(1)}, u32[]{:S(2)}, u32[]{:S(2)}) collective-permute-start(bf16[1184,128]{1,0:T(8,128)(2,1)S(1)} %shard_map.58.refs_0_), channel_id=1, source_target_pairs={{0,5},{1,2},{2,1},{3,6},{4,7},{5,0},{6,3},{7,4},{8,11},{9,12},{10,... | collective-permute-start | bytes 909320 | tf_op jit(solution)/shard_map/ppermute | solution.py:355
  56.2 4.4 %collective-permute-start.7 = (bf16[2752,128]{1,0:T(8,128)(2,1)S(1)}, bf16[2752,128]{1,0:T(8,128)(2,1)S(1)}, u32[]{:S(2)}, u32[]{:S(2)}) collective-permute-start(bf16[2752,128]{1,0:T(8,128)(2,1)S(1)} %shard_map.49.own_ref.refs_3_), channel_id=1, source_target_pairs={{0,1},{1,0},{2,3},{3,2},{4,5},{5,4},{6,7},{7,6},{8,9},{9,8},{10,11... | collective-permute-start | bytes 2113544 | tf_op jit(solution)/shard_map/ppermute | solution.py:355
  60.5 2.8 %collective-permute-start.15 = (bf16[2368,128]{1,0:T(8,128)(2,1)S(1)}, bf16[2368,128]{1,0:T(8,128)(2,1)S(1)}, u32[]{:S(2)}, u32[]{:S(2)}) collective-permute-start(bf16[2368,128]{1,0:T(8,128)(2,1)S(1)} %shard_map.59.refs_2_.refs_5_), channel_id=1, source_target_pairs={{0,1},{1,0},{2,3},{3,2},{4,5},{5,4},{6,7},{7,6},{8,9},{9,8},{10,11... | collective-permute-start | bytes 1818632 | tf_op jit(solution)/shard_map/ppermute | solution.py:355

commit v5 on v0

v5 whole, which is shorter than its diff:
```python
import jax
import jax.numpy as jnp
from jax import lax
from jax.experimental import pallas as pl
from jax.experimental.pallas import tpu as pltpu
from jax.sharding import PartitionSpec as P


TILE = 128
PAD = 16
SHARES = 4
CUTS = (16 / 39, 30 / 39)
TURNS = (0, 2, 1)
FAR_FIRST = 2
AXES = ("gr", "gc")
BF16 = jnp.bfloat16
F32 = jnp.float32
VMEM = pl.BlockSpec(memory_space=pltpu.VMEM)
SMEM = pl.BlockSpec(memory_space=pltpu.SMEM)
HBM = pl.BlockSpec(memory_space=pltpu.HBM)
DIMS = (((1,), (1,)), ((), ()))


def params(mib):
    return pltpu.CompilerParams(vmem_limit_bytes=mib * 2**20)


def call(kernel, out, mib, *operands, scratch=(), in_specs=None, out_specs=None):
    return pl.pallas_call(
        kernel,
        out_shape=out,
        in_specs=in_specs or [VMEM] * len(operands),
        out_specs=out_specs or jax.tree.map(lambda _: VMEM, out),
        scratch_shapes=scratch,
        compiler_params=params(mib),
    )(*operands)


def geometry(total_rows):
    side = total_rows // TILE // 2
    return side, side // 2


def chunk_tiles(total_rows):
    side, extra = geometry(total_rows)
    tiles = [("near", i, j) for j in range(side) for i in range(j + 1)]
    tiles += [("far", i, j) for j in range(side) for i in range(j + 1, side)]
    tiles += [("extra", k, k) for k in range(extra)]
    first, second = (round(cut * len(tiles)) for cut in CUTS)
    return [tiles[:first], tiles[first:second], tiles[second:]]


def parity(r, c):
    return (r ^ (r >> 1) ^ (c >> 1)) & 1


def pick(half, pair):
    return tuple(jnp.where(half == 0, a, b) for a, b in zip(*pair))


def position():
    r, c = lax.axis_index("gr"), lax.axis_index("gc")
    return r, c, (c & 1) ^ parity(r, c)


def side_bit(pair):
    r, c, half = position()
    on_r, on_c = pick(half, pair)
    return (((r & on_r) | (c & on_c)) != 0).astype(jnp.int32)


def starts(flip, side):
    _, _, half = position()
    h = half ^ flip
    low = pl.multiple_of(h * (side * TILE), TILE)
    up = pl.multiple_of((1 - h) * (side * TILE), TILE)
    return h, low, up


def symmetric(orb_ref, vel_ref, r0, rows, c0, cols):
    one = lax.dot_general(
        orb_ref[pl.ds(r0, rows), :], vel_ref[pl.ds(c0, cols), :], DIMS, preferred_element_type=F32
    )
    two = lax.dot_general(
        vel_ref[pl.ds(r0, rows), :], orb_ref[pl.ds(c0, cols), :], DIMS, preferred_element_type=F32
    )
    return one + two


def product_kernel(orb_ref, vel_ref, out_ref, *, flip, tiles, side, extra):
    h, low, up = starts(flip, side)
    for kind in ("near", "far"):
        table = {(i, j): n for n, (which, i, j) in enumerate(tiles) if which == kind}
        for c in range(0, side, 2):
            columns = [j for j in (c, c + 1) if any(at[1] == j for at in table)]
            if not columns:
                continue
            rows = [i for i in range(side) if any((i, j) in table for j in columns)]
            rows = list(range(rows[0], rows[-1] + 1))
            value = symmetric(
                orb_ref,
                vel_ref,
                low + rows[0] * TILE,
                len(rows) * TILE,
                (low if kind == "near" else up) + columns[0] * TILE,
                len(columns) * TILE,
            )
            for i in rows:
                for j in columns:
                    if (i, j) in table:
                        at = table[(i, j)] * TILE
                        row, col = (i - rows[0]) * TILE, (j - columns[0]) * TILE
                        out_ref[at : at + TILE, :] = value[row : row + TILE, col : col + TILE].astype(BF16)
    for n, (which, k, _) in enumerate(tiles):
        if which == "extra":
            shift = pl.multiple_of((h * extra + k) * TILE, TILE)
            value = symmetric(orb_ref, vel_ref, low + shift, TILE, up + shift, TILE)
            out_ref[n * TILE : (n + 1) * TILE, :] = value.astype(BF16)


def product(flip, orb, vel, tiles):
    side, extra = geometry(orb.shape[0])
    kernel = lambda *refs: product_kernel(*refs, flip=flip, tiles=tiles, side=side, extra=extra)
    return call(kernel, jax.ShapeDtypeStruct((len(tiles) * TILE, TILE), BF16), 6, orb, vel)


def load_kernel(orb_hbm, vel_hbm, away_ref, orb_ref, vel_ref, sems, *, tiles):
    total_rows = orb_hbm.shape[0]
    side, extra = geometry(total_rows)
    _, low, up = starts(1, side)
    rows = total_rows // 4
    copies = []
    for at in (low, low + rows, up, up + rows):
        for source, target in ((orb_hbm, orb_ref), (vel_hbm, vel_ref)):
            part = pl.ds(pl.multiple_of(at, TILE), rows)
            copies.append(pltpu.make_async_copy(source.at[part], target.at[part], sems.at[len(copies)]))
            copies[-1].start()
    for copy in copies[:4]:
        copy.wait()
    product_kernel(orb_ref, vel_ref, away_ref, flip=1, tiles=tiles, side=side, extra=extra)
    for copy in copies[4:]:
        copy.wait()


def load(orb, vel, tiles):
    whole = jax.ShapeDtypeStruct(orb.shape, orb.dtype)
    return call(
        lambda *refs: load_kernel(*refs, tiles=tiles),
        [jax.ShapeDtypeStruct((len(tiles) * TILE, TILE), BF16), whole, whole],
        12,
        pltpu.with_memory_space_constraint(orb, pltpu.HBM),
        pltpu.with_memory_space_constraint(vel, pltpu.HBM),
        scratch=[pltpu.SemaphoreType.DMA((8,))],
        in_specs=[HBM, HBM],
    )


def halve_kernel(mine_ref, got_ref, send_ref, keep_ref, *, pair):
    rows = send_ref.shape[0]
    bit = side_bit(pair)

    def part(index):
        at = pl.ds(pl.multiple_of(index * rows, PAD), rows)
        return mine_ref[at, :].astype(F32) + got_ref[at, :].astype(F32)

    send_ref[...] = part(1 - bit).astype(BF16)
    keep_ref[...] = part(bit)


def halve(mine, got, pair):
    rows = mine.shape[0] // 2
    out = [jax.ShapeDtypeStruct((rows, TILE), BF16), jax.ShapeDtypeStruct((rows, TILE), F32)]
    return call(lambda *refs: halve_kernel(*refs, pair=pair), out, 2, mine, got)


def add_kernel(a_ref, b_ref, out_ref):
    out_ref[...] = (a_ref[...].astype(F32) + b_ref[...].astype(F32)).astype(BF16)


def add(a, b):
    return call(add_kernel, jax.ShapeDtypeStruct(a.shape, BF16), 2, a, b)


def join_kernel(mine_ref, got_ref, out_ref, *, pair):
    rows = mine_ref.shape[0]
    bit = side_bit(pair)
    out_ref[pl.ds(pl.multiple_of(bit * rows, PAD), rows), :] = mine_ref[...]
    out_ref[pl.ds(pl.multiple_of((1 - bit) * rows, PAD), rows), :] = got_ref[...]


def join(mine, got, pair):
    out = jax.ShapeDtypeStruct((2 * mine.shape[0], TILE), BF16)
    return call(lambda *refs: join_kernel(*refs, pair=pair), out, 2, mine, got)


def share_kernel(a_ref, b_ref, out_ref, *, pairs, diagonal):
    rows = a_ref.shape[0]
    offset = (2 * side_bit(pairs[0]) + side_bit(pairs[1])) * rows
    total = a_ref[...].astype(F32) + b_ref[...].astype(F32)
    out_ref[0:rows, :] = total.astype(BF16)
    square = total * total
    if diagonal:
        tile = (lax.broadcasted_iota(jnp.int32, (rows, TILE), 0) + offset) // TILE
        single = tile == diagonal[0]
        for at in diagonal[1:]:
            single |= tile == at
        square = jnp.where(single, square, 2.0 * square)
    else:
        square = 2.0 * square
    square = jnp.sum(jnp.sum(square, axis=0, keepdims=True), axis=1, keepdims=True)
    high = square.astype(BF16).astype(F32)
    rest = square - high
    middle = rest.astype(BF16).astype(F32)
    small = rest - middle
    line = lax.broadcasted_iota(jnp.int32, (PAD, TILE), 0)
    tail = jnp.where(line == 0, high, jnp.where(line == 1, middle, jnp.where(line == 2, small, 0.0)))
    out_ref[rows : rows + PAD, :] = tail.astype(BF16)


def make_share(a, b, pairs, diagonal):
    out = jax.ShapeDtypeStruct((a.shape[0] + PAD, TILE), BF16)
    return call(lambda *refs: share_kernel(*refs, pairs=pairs, diagonal=diagonal), out, 3, a, b)


def take_tile(ref, index):
    share_rows = ref.shape[0] // SHARES - PAD
    row, end = index * TILE, (index + 1) * TILE
    parts = []
    while row < end:
        share = row // share_rows
        stop = min(end, (share + 1) * share_rows)
        parts.append(ref[row + share * PAD : stop + share * PAD, :])
        row = stop
    return parts[0] if len(parts) == 1 else jnp.concatenate(parts, axis=0)


def tails(refs):
    total = jnp.zeros((1, TILE), F32)
    for ref in refs:
        share = ref.shape[0] // SHARES
        for k in range(SHARES):
            lines = ref[(k + 1) * share - PAD : (k + 1) * share, :].astype(F32)
            total = total + jnp.sum(lines, axis=0, keepdims=True)
    return total


def put_block(ref, i, j, value):
    ref[i * TILE : (i + 1) * TILE, j * TILE : (j + 1) * TILE] = value


def piece_values(piece_ref, tiles, flip, orb_ref, mats, side, extra):
    h, low, up = starts(flip, side)
    near_ref, far_ref, flip_ref = mats
    near, far, back = {}, {}, {}
    extras = []
    for n, (which, i, j) in enumerate(tiles):
        if which == "near":
            near[(i, j)] = (n, False)
            if i != j:
                near[(j, i)] = (n, True)
        elif which == "far":
            far[(i, j)] = (n, False)
            back[(j, i)] = (n, True)
        else:
            extras.append((n, i))
    for table in (far, back):
        if extras:
            for i in range(side):
                table[(i, i)] = None
    spans = {}
    zero = jnp.zeros((TILE, TILE), BF16)
    for name, ref, table in (("near", near_ref, near), ("far", far_ref, far), ("back", flip_ref, back)):
        for p in range(0, side, 2):
            rows = range(p, min(p + 2, side))
            columns = [j for (i, j) in table if i in rows]
            if not columns:
                continue
            span = (min(columns), max(columns) + 1)
            spans[(name, p)] = span
            for i in rows:
                for j in range(*span):
                    if table.get((i, j)) is None:
                        put_block(ref, i, j, zero)
    for (i, j), (n, turned) in near.items():
        if not turned:
            value = take_tile(piece_ref, n)
            put_block(near_ref, i, j, value)
            if i != j:
                put_block(near_ref, j, i, value.T)
    for (i, j), entry in far.items():
        if entry is not None:
            value = take_tile(piece_ref, entry[0])
            put_block(far_ref, i, j, value)
            put_block(flip_ref, j, i, value.T)
    for n, k in extras:
        value = take_tile(piece_ref, n)
        at = pl.ds(pl.multiple_of((h * extra + k) * TILE, TILE), TILE)
        far_ref[at, at] = value
        flip_ref[at, at] = value.T

    def part(name, ref, p, base):
        if (name, p) not in spans:
            return None
        begin, end = spans[(name, p)]
        left = ref[p * TILE : min(p + 2, side) * TILE, begin * TILE : end * TILE]
        right = orb_ref[pl.ds(pl.multiple_of(base + begin * TILE, TILE), (end - begin) * TILE), :]
        return jnp.dot(left, right, preferred_element_type=F32)

    for p in range(0, side, 2):
        one, two = part("near", near_ref, p, low), part("far", far_ref, p, up)
        if one is not None or two is not None:
            yield flip, p, one if two is None else two if one is None else one + two
    for p in range(0, side, 2):
        value = part("back", flip_ref, p, low)
        if value is not None:
            yield 1 - flip, p, value


def apply_kernel(*refs, plan, blocks, side, extra, last):
    refs = list(refs)
    orb_ref = refs.pop(0)
    vel_ref = refs.pop(0) if blocks["vel"] else None
    bases = {b: refs.pop(0) for b in blocks["in"]}
    pieces = [refs.pop(0) for _ in plan]
    if last:
        squares = [refs.pop(0) for _ in range(blocks["squares"])]
        out_hbm, norm_ref = refs.pop(0), refs.pop(0)
        scratch = refs.pop(0)
        outs = {b: scratch.at[b] for b in (0, 1)}
    else:
        outs = {b: refs.pop(0) for b in blocks["out"]}
    mats = refs[:3]
    _, low, up = starts(0, side)
    base_row = (low, up)
    written = set()
    copies = []

    def rows_of(p):
        return slice(p * TILE, min(p + 2, side) * TILE)

    def before(b, p):
        if (b, p) in written:
            return outs[b][rows_of(p), :]
        if b in bases:
            return bases[b][rows_of(p), :]
        rows = rows_of(p)
        at = pl.ds(pl.multiple_of(base_row[b] + rows.start, TILE), rows.stop - rows.start)
        return vel_ref[at, :].astype(F32)

    def send(source, b, p):
        rows = rows_of(p)
        at = pl.ds(pl.multiple_of(base_row[b] + rows.start, TILE), rows.stop - rows.start)
        copy = pltpu.make_async_copy(source.at[rows], out_hbm.at[at], refs[3].at[len(copies)])
        copy.start()
        copies.append(copy)

    if last:
        (tiles, flip), piece = plan[0], pieces[0]
        touched = {("near", i // 2 * 2) for which, i, j in tiles if which == "near"}
        touched |= {("near", j // 2 * 2) for which, i, j in tiles if which == "near"}
        touched |= {("near", i // 2 * 2) for which, i, j in tiles if which == "far"}
        touched |= {("back", j // 2 * 2) for which, i, j in tiles if which == "far"}
        if any(which == "extra" for which, _, _ in tiles):
            touched |= {(name, p) for name in ("near", "back") for p in range(0, side, 2)}
        for b, name in ((flip, "near"), (1 - flip, "back")):
            for p in range(0, side, 2):
                if (name, p) not in touched:
                    send(bases[b], b, p)
    for (tiles, flip), piece in zip(plan, pieces):
        for b, p, value in piece_values(piece, tiles, flip, orb_ref, mats, side, extra):
            outs[b][rows_of(p), :] = before(b, p) - 0.5 * value
            written.add((b, p))
            if last:
                send(outs[b], b, p)
    if last:
        count = len(squares) // 2
        square = tails(squares[:count]) + tails(squares[count:])
        norm_ref[0] = (jnp.sqrt(square) / (2 * side * TILE))[0, 0]
        for copy in copies:
            copy.wait()
    else:
        for b in outs:
            for p in range(0, side, 2):
                if (b, p) not in written:
                    outs[b][rows_of(p), :] = before(b, p)


def apply(orb, vel, bases, plan, pieces, squares=None):
    side, extra = geometry(orb.shape[0])
    wide, columns = side * TILE, orb.shape[1]
    last = squares is not None
    touched = set()
    for tiles, flip in plan:
        touched.add(flip)
        if any(which != "near" for which, _, _ in tiles):
            touched.add(1 - flip)
    given = [b for b in (0, 1) if bases[b] is not None and (b in touched or last)]
    blocks = {"in": given, "out": sorted(touched), "vel": any(bases[b] is None for b in touched)}
    operands = [orb] + ([vel] if blocks["vel"] else []) + [bases[b] for b in given] + list(pieces)
    mats = [pltpu.VMEM((wide, wide), BF16)] * 3
    if last:
        blocks["squares"] = len(squares)
        operands += squares
        panels = 2 * -(-side // 2)
        return call(
            lambda *refs: apply_kernel(*refs, plan=plan, blocks=blocks, side=side, extra=extra, last=True),
            [jax.ShapeDtypeStruct(orb.shape, F32), jax.ShapeDtypeStruct((1,), F32)],
            14,
            *operands,
            scratch=[pltpu.VMEM((2, wide, columns), F32)] + mats + [pltpu.SemaphoreType.DMA((panels,))],
            out_specs=[HBM, SMEM],
        )
    outs = call(
        lambda *refs: apply_kernel(*refs, plan=plan, blocks=blocks, side=side, extra=extra, last=False),
        [jax.ShapeDtypeStruct((wide, columns), F32)] * len(touched),
        10,
        *operands,
        scratch=mats,
    )
    result = list(bases)
    for b, value in zip(sorted(touched), outs):
        result[b] = value
    return result


def permutation(nr, nc, pair):
    result = []
    for r in range(nr):
        for c in range(nc):
            on_r, on_c = pair[(c & 1) ^ parity(r, c)]
            result.append((r * nc + c, (r ^ on_r) * nc + (c ^ on_c ^ parity(on_r, on_c))))
    return result


def routes(nr, nc):
    low = [(1, 0), (0, 2)]
    rest = [(1 << b, 0) for b in range(1, nr.bit_length() - 1)]
    rest += [(0, 1 << b) for b in range(2, nc.bit_length() - 1)]

    def both_ways(bits):
        return list(zip(bits, bits[::-1]))

    usual = (both_ways(low), both_ways(rest))
    result = [usual] * 3
    if len(rest) > 1:
        result[FAR_FIRST] = (both_ways([rest[0], rest[-1]]), both_ways(low + rest[1:-1]))
    return result


def local(orbitals, velocities):
    nr, nc = lax.axis_size("gr"), lax.axis_size("gc")
    _, _ = geometry(orbitals.shape[0])
    chunks = chunk_tiles(orbitals.shape[0])
    plans = routes(nr, nc)
    swap = [(d, d ^ 1) for d in range(nr * nc)]
    joined, far = {}, {}
    for k in TURNS:
        tiles = chunks[k]
        halvings, doublings = plans[k]
        diagonal = [n for n, (which, i, j) in enumerate(tiles) if which == "near" and i == j]

        def move(value, pair):
            return lax.ppermute(value, AXES, swap if pair is None else permutation(nr, nc, pair))

        if k == TURNS[0]:
            send, orbitals, velocities = load(orbitals, velocities, tiles)
        else:
            send = product(1, orbitals, velocities, tiles)
        got = move(send, None)
        mine = product(0, orbitals, velocities, tiles)
        for pair in halvings:
            send, mine = halve(mine, got, pair)
            got = move(send, pair)
        for pair in doublings:
            mine = add(mine, got)
            got = move(mine, pair)
        mine = make_share(mine, got, halvings, diagonal)
        for pair in halvings[::-1]:
            got = move(mine, pair)
            mine = join(mine, got, pair)
        joined[k] = mine
        far[k] = move(mine, None)
    first, second, third = TURNS
    blocks = [None, None]
    blocks = apply(orbitals, velocities, blocks, [(chunks[first], 0)], [joined[first]])
    plan = [(chunks[first], 1), (chunks[second], 0)]
    blocks = apply(orbitals, velocities, blocks, plan, [far[first], joined[second]])
    plan = [(chunks[second], 1), (chunks[third], 0)]
    blocks = apply(orbitals, velocities, blocks, plan, [far[second], joined[third]])
    squares = [joined[k] for k in TURNS] + [far[k] for k in TURNS]
    return tuple(apply(orbitals, velocities, blocks, [(chunks[third], 1)], [far[third]], squares))


def solution(mesh):
    in_specs = (P(None, AXES), P(None, AXES))
    out_specs = (P(None, AXES), P())

    return jax.shard_map(local, mesh=mesh, in_specs=in_specs, out_specs=out_specs, check_vma=False)
```

time: 297 us -> 76 us (0.26)
  waiting for transfers between devices: 136 us -> 31.6 us
  local copies, waits for them, and re-layouts: 61.7 us -> 0 us
  blocking collectives: 40.2 us -> 0 us
  starting transfers between devices: 0.08 us -> 28.9 us
  matrix products: 25.9 us -> 0 us
  other arithmetic: 15.6 us -> 0 us
  between operations: 16 us -> 0.9 us
  Pallas kernels: 0 us -> 14.5 us
    unnamed x3 -> x0, waiting for transfers between devices: 126 us -> none
    psum x1 -> x0, blocking collectives: 40.2 us -> none  [local(): summed = lax.psum(local_sq, ('gr', 'gc'))]
    ppermute x0 -> x24, waiting for transfers between devices: none -> 31.6 us  [move(): lax.ppermute(value, AXES, swap if pair is None else permutation(nr, nc, p...]
    ppermute x0 -> x24, starting transfers between devices: none -> 28.9 us  [move(): lax.ppermute(value, AXES, swap if pair is None else permutation(nr, nc, p...]
    dot_general x5 -> x0, matrix products: 25.9 us -> none  [the longest x1 6.63 us: local(): carry = carry + jnp.einsum('jkq,jkbg->qbg', col_hot, mirrored)]
    reshape x2 -> x0, local copies, waits for them, and re-layouts: 25.3 us -> none  [local(): sym_four = sym_local.reshape(row_groups, edge, row_groups, edge)]
    gather x3 -> x0, local copies, waits for them, and re-layouts: 16.5 us -> none  [the longest x1 9.02 us: local(): sym_four[every_row[:, None], :, every_col, :]]
    pallas_call x0 -> x31, Pallas kernels: none -> 14.5 us  [call(): pl.pallas_call(kernel, out_shape=out, in_specs=in_specs or [VMEM] * len(o...]
  transfers between devices with their start and end apart: 2 -> 24, of which waited for: 2 -> 11; matrix products, arithmetic and copies ran while one was open for 3% -> 0% of each run, Pallas kernels for 0% -> 13%
where the time goes in v5:
time: 76 us; the launch traced here: 75.9 us
  waiting for transfers between devices  31.6 us (42%)
  starting transfers between devices  28.9 us (38%)
  Pallas kernels  14.5 us (19%)
  between operations  0.9 us (1%)
    ppermute x24, waiting for transfers between devices, move(): lax.ppermute(value, AXES, swap if pair is None else permutation(nr, nc, p...  31.6 us
    ppermute x24, starting transfers between devices, move(): lax.ppermute(value, AXES, swap if pair is None else permutation(nr, nc, p...  28.9 us
    pallas_call x31, Pallas kernels, call(): pl.pallas_call(kernel, out_shape=out, in_specs=in_specs or [VMEM] * len(o...  14.5 us
  transfers between devices with their start and end apart: 24, of which 11 were waited for; matrix products, arithmetic and copies ran while one was open for 0% of the time, Pallas kernels for 13%

profile of v5, /device:TPU:0, one launch (start us, length us, event | category | flops | bytes accessed | tf_op | source)
XLA Modules:
  0.0 75.9 jit_solution(16966347255473636741)
XLA Ops:
  0.6 2.4 %shard_map.41 = (bf16[2048,128]{1,0:T(8,128)(2,1)S(1)}, bf16[1536,512]{1,0:T(8,128)(2,1)S(1)}, bf16[1536,512]{1,0:T(8,128)(2,1)S(1)}) custom-call(bf16[1536,512]{1,0:T(8,128)(2,1)} %refs_0_.1, bf16[1536,512]{1,0:T(8,128)(2,1)} %refs_1_.1), custom_call_target="tpu_custom_call" | custom-call | tf_op jit(solution)/shard_map/pallas_call | solution.py:29
  3.0 0.6 collective-permute-start
  3.6 0.8 %shard_map.62 = bf16[1792,128]{1,0:T(8,128)(2,1)S(1)} custom-call(bf16[1536,512]{1,0:T(8,128)(2,1)S(1)} %get-tuple-element.21.refs_0_, bf16[1536,512]{1,0:T(8,128)(2,1)S(1)} %get-tuple-element.22.refs_1_), custom_call_target="tpu_custom_call" | custom-call | tf_op jit(solution)/shard_map/pallas_call | solution.py:29
  4.4 0.1 collective-permute-start.16
  4.5 0.9 %shard_map.42.refs_0_ = bf16[2048,128]{1,0:T(8,128)(2,1)S(1)} custom-call(bf16[1536,512]{1,0:T(8,128)(2,1)S(1)} %get-tuple-element.21.refs_0_, bf16[1536,512]{1,0:T(8,128)(2,1)S(1)} %get-tuple-element.22.refs_1_), custom_call_target="tpu_custom_call" | custom-call | tf_op jit(solution)/shard_map/pallas_call | solution.py:29
  5.5 0.1 shard_map.43
  5.6 2.7 %collective-permute-start.1 = (bf16[1024,128]{1,0:T(8,128)(2,1)S(1)}, bf16[1024,128]{1,0:T(8,128)(2,1)S(1)}, u32[]{:S(2)}, u32[]{:S(2)}) collective-permute-start(bf16[1024,128]{1,0:T(8,128)(2,1)S(1)} %get-tuple-element.25), channel_id=1, source_target_pairs={{0,5},{1,2},{2,1},{3,6},{4,7},{5,0},{6,3},{7,4},{8,11},{9,12},{10,... | collective-permute-start | bytes 786440 | tf_op jit(solution)/shard_map/ppermute | solution.py:463
  8.3 0.8 %shard_map.61.refs_0_ = bf16[1792,128]{1,0:T(8,128)(2,1)S(1)} custom-call(bf16[1536,512]{1,0:T(8,128)(2,1)S(1)} %get-tuple-element.21.refs_0_, bf16[1536,512]{1,0:T(8,128)(2,1)S(1)} %get-tuple-element.22.refs_1_), custom_call_target="tpu_custom_call" | custom-call | tf_op jit(solution)/shard_map/pallas_call | solution.py:29
  9.2 0.1 shard_map.63
  9.3 0.1 collective-permute-start.17
  9.4 3.0 %collective-permute-done.1.refs_1_ = bf16[1024,128]{1,0:T(8,128)(2,1)S(1)} collective-permute-done((bf16[1024,128]{1,0:T(8,128)(2,1)S(1)}, bf16[1024,128]{1,0:T(8,128)(2,1)S(1)}, u32[]{:S(2)}, u32[]{:S(2)}) %collective-permute-start.1) | collective-permute-done | bytes 262176 | tf_op jit(solution)/shard_map/ppermute | solution.py:463
  12.4 2.1 %collective-permute-start.2 = (bf16[512,128]{1,0:T(8,128)(2,1)S(1)}, bf16[512,128]{1,0:T(8,128)(2,1)S(1)}, u32[]{:S(2)}, u32[]{:S(2)}) collective-permute-start(bf16[512,128]{1,0:T(8,128)(2,1)S(1)} %get-tuple-element.27), channel_id=1, source_target_pairs={{0,3},{1,4},{2,7},{3,0},{4,1},{5,6},{6,5},{7,2},{8,13},{9,10},{10,... | collective-permute-start | bytes 393224 | tf_op jit(solution)/shard_map/ppermute | solution.py:463
  14.5 0.6 shard_map.52
  15.2 0.2 collective-permute-start.8
  15.4 1.8 %collective-permute-done.2.b_ref = bf16[512,128]{1,0:T(8,128)(2,1)S(1)} collective-permute-done((bf16[512,128]{1,0:T(8,128)(2,1)S(1)}, bf16[512,128]{1,0:T(8,128)(2,1)S(1)}, u32[]{:S(2)}, u32[]{:S(2)}) %collective-permute-start.2) | collective-permute-done | bytes 131104 | tf_op jit(solution)/shard_map/ppermute | solution.py:463
  17.2 1.9 %collective-permute-start.3 = (bf16[512,128]{1,0:T(8,128)(2,1)S(1)}, bf16[512,128]{1,0:T(8,128)(2,1)S(1)}, u32[]{:S(2)}, u32[]{:S(2)}) collective-permute-start(bf16[512,128]{1,0:T(8,128)(2,1)S(1)} %shard_map.45.a_ref), channel_id=1, source_target_pairs={{0,9},{1,17},{2,18},{3,10},{4,20},{5,12},{6,15},{7,23},{8,24},{9,0... | collective-permute-start | bytes 393224 | tf_op jit(solution)/shard_map/ppermute | solution.py:463
  19.1 1.4 %collective-permute-start.18 = (bf16[448,128]{1,0:T(8,128)(2,1)S(1)}, bf16[448,128]{1,0:T(8,128)(2,1)S(1)}, u32[]{:S(2)}, u32[]{:S(2)}) collective-permute-start(bf16[448,128]{1,0:T(8,128)(2,1)S(1)} %get-tuple-element.37), channel_id=1, source_target_pairs={{0,3},{1,4},{2,7},{3,0},{4,1},{5,6},{6,5},{7,2},{8,13},{9,10},{10,... | collective-permute-start | bytes 344072 | tf_op jit(solution)/shard_map/ppermute | solution.py:463
  20.5 2.6 %collective-permute-done.3.b_ref = bf16[512,128]{1,0:T(8,128)(2,1)S(1)} collective-permute-done((bf16[512,128]{1,0:T(8,128)(2,1)S(1)}, bf16[512,128]{1,0:T(8,128)(2,1)S(1)}, u32[]{:S(2)}, u32[]{:S(2)}) %collective-permute-start.3) | collective-permute-done | bytes 131104 | tf_op jit(solution)/shard_map/ppermute | solution.py:463
  23.2 2.4 %collective-permute-start.4 = (bf16[512,128]{1,0:T(8,128)(2,1)S(1)}, bf16[512,128]{1,0:T(8,128)(2,1)S(1)}, u32[]{:S(2)}, u32[]{:S(2)}) collective-permute-start(bf16[512,128]{1,0:T(8,128)(2,1)S(1)} %shard_map.46.refs_0_), channel_id=1, source_target_pairs={{0,16},{1,8},{2,11},{3,19},{4,13},{5,21},{6,22},{7,14},{8,1},{9,25... | collective-permute-start | bytes 393224 | tf_op jit(solution)/shard_map/ppermute | solution.py:463
  25.6 1.1 %collective-permute-start.19 = (bf16[448,128]{1,0:T(8,128)(2,1)S(1)}, bf16[448,128]{1,0:T(8,128)(2,1)S(1)}, u32[]{:S(2)}, u32[]{:S(2)}) collective-permute-start(bf16[448,128]{1,0:T(8,128)(2,1)S(1)} %shard_map.65.a_ref), channel_id=1, source_target_pairs={{0,9},{1,17},{2,18},{3,10},{4,20},{5,12},{6,15},{7,23},{8,24},{9,0... | collective-permute-start | bytes 344072 | tf_op jit(solution)/shard_map/ppermute | solution.py:463
  26.7 4.6 %collective-permute-done.4.refs_1_ = bf16[512,128]{1,0:T(8,128)(2,1)S(1)} collective-permute-done((bf16[512,128]{1,0:T(8,128)(2,1)S(1)}, bf16[512,128]{1,0:T(8,128)(2,1)S(1)}, u32[]{:S(2)}, u32[]{:S(2)}) %collective-permute-start.4) | collective-permute-done | bytes 131104 | tf_op jit(solution)/shard_map/ppermute | solution.py:463
  31.3 0.5 shard_map.47.refs_0_
  31.8 1.0 %collective-permute-done.19.b_ref = bf16[448,128]{1,0:T(8,128)(2,1)S(1)} collective-permute-done((bf16[448,128]{1,0:T(8,128)(2,1)S(1)}, bf16[448,128]{1,0:T(8,128)(2,1)S(1)}, u32[]{:S(2)}, u32[]{:S(2)}) %collective-permute-start.19) | collective-permute-done | bytes 114720 | tf_op jit(solution)/shard_map/ppermute | solution.py:463
  32.9 1.0 %collective-permute-start.20 = (bf16[448,128]{1,0:T(8,128)(2,1)S(1)}, bf16[448,128]{1,0:T(8,128)(2,1)S(1)}, u32[]{:S(2)}, u32[]{:S(2)}) collective-permute-start(bf16[448,128]{1,0:T(8,128)(2,1)S(1)} %shard_map.66.refs_0_), channel_id=1, source_target_pairs={{0,16},{1,8},{2,11},{3,19},{4,13},{5,21},{6,22},{7,14},{8,1},{9,25... | collective-permute-start | bytes 344072 | tf_op jit(solution)/shard_map/ppermute | solution.py:463
  33.9 0.6 shard_map.51.refs_0_
  34.5 0.1 shard_map.53
  34.6 4.0 %collective-permute-start.9 = (bf16[576,128]{1,0:T(8,128)(2,1)S(1)}, bf16[576,128]{1,0:T(8,128)(2,1)S(1)}, u32[]{:S(2)}, u32[]{:S(2)}) collective-permute-start(bf16[576,128]{1,0:T(8,128)(2,1)S(1)} %get-tuple-element.29), channel_id=1, source_target_pairs={{0,9},{1,17},{2,18},{3,10},{4,20},{5,12},{6,15},{7,23},{8,24},{9,0... | collective-permute-start | bytes 442376 | tf_op jit(solution)/shard_map/ppermute | solution.py:463
  38.7 0.2 collective-permute-done.20.refs_1_
  38.9 0.4 shard_map.67.refs_0_
  39.4 4.5 %collective-permute-start.6 = (bf16[1056,128]{1,0:T(8,128)(2,1)S(1)}, bf16[1056,128]{1,0:T(8,128)(2,1)S(1)}, u32[]{:S(2)}, u32[]{:S(2)}) collective-permute-start(bf16[1056,128]{1,0:T(8,128)(2,1)S(1)} %shard_map.48.refs_0_), channel_id=1, source_target_pairs={{0,5},{1,2},{2,1},{3,6},{4,7},{5,0},{6,3},{7,4},{8,11},{9,12},{10,... | collective-permute-start | bytes 811016 | tf_op jit(solution)/shard_map/ppermute | solution.py:463
  43.9 0.1 collective-permute-start.10
  44.1 4.0 %collective-permute-start.22 = (bf16[928,128]{1,0:T(8,128)(2,1)S(1)}, bf16[928,128]{1,0:T(8,128)(2,1)S(1)}, u32[]{:S(2)}, u32[]{:S(2)}) collective-permute-start(bf16[928,128]{1,0:T(8,128)(2,1)S(1)} %shard_map.68.refs_0_), channel_id=1, source_target_pairs={{0,5},{1,2},{2,1},{3,6},{4,7},{5,0},{6,3},{7,4},{8,11},{9,12},{10,... | collective-permute-start | bytes 712712 | tf_op jit(solution)/shard_map/ppermute | solution.py:463
  48.1 1.9 %collective-permute-done.10.b_ref = bf16[288,128]{1,0:T(8,128)(2,1)S(1)} collective-permute-done((bf16[288,128]{1,0:T(8,128)(2,1)S(1)}, bf16[288,128]{1,0:T(8,128)(2,1)S(1)}, u32[]{:S(2)}, u32[]{:S(2)}) %collective-permute-start.10) | collective-permute-done | bytes 73760 | tf_op jit(solution)/shard_map/ppermute | solution.py:463
  50.0 0.1 collective-permute-start.11
  50.1 3.8 %collective-permute-done.11.b_ref = bf16[288,128]{1,0:T(8,128)(2,1)S(1)} collective-permute-done((bf16[288,128]{1,0:T(8,128)(2,1)S(1)}, bf16[288,128]{1,0:T(8,128)(2,1)S(1)}, u32[]{:S(2)}, u32[]{:S(2)}) %collective-permute-start.11) | collective-permute-done | bytes 73760 | tf_op jit(solution)/shard_map/ppermute | solution.py:463
  53.9 0.2 collective-permute-start.12
  54.1 3.6 %collective-permute-done.12.refs_1_ = bf16[288,128]{1,0:T(8,128)(2,1)S(1)} collective-permute-done((bf16[288,128]{1,0:T(8,128)(2,1)S(1)}, bf16[288,128]{1,0:T(8,128)(2,1)S(1)}, u32[]{:S(2)}, u32[]{:S(2)}) %collective-permute-start.12) | collective-permute-done | bytes 73760 | tf_op jit(solution)/shard_map/ppermute | solution.py:463
  57.7 0.2 shard_map.57.refs_0_
  57.9 0.1 collective-permute-start.7
  58.1 0.5 collective-permute-start.23
  58.6 4.5 %collective-permute-done.13.refs_1_ = bf16[304,128]{1,0:T(8,128)(2,1)S(1)} collective-permute-done((bf16[304,128]{1,0:T(8,128)(2,1)S(1)}, bf16[304,128]{1,0:T(8,128)(2,1)S(1)}, u32[]{:S(2)}, u32[]{:S(2)}) %collective-permute-start.13) | collective-permute-done | bytes 77856 | tf_op jit(solution)/shard_map/ppermute | solution.py:463
  63.2 1.7 %collective-permute-start.14 = (bf16[608,128]{1,0:T(8,128)(2,1)S(1)}, bf16[608,128]{1,0:T(8,128)(2,1)S(1)}, u32[]{:S(2)}, u32[]{:S(2)}) collective-permute-start(bf16[608,128]{1,0:T(8,128)(2,1)S(1)} %shard_map.58.refs_0_), channel_id=1, source_target_pairs={{0,9},{1,17},{2,18},{3,10},{4,20},{5,12},{6,15},{7,23},{8,24},{9,0... | collective-permute-start | bytes 466952 | tf_op jit(solution)/shard_map/ppermute | solution.py:463
  64.9 4.6 %collective-permute-done.14.refs_1_ = bf16[608,128]{1,0:T(8,128)(2,1)S(1)} collective-permute-done((bf16[608,128]{1,0:T(8,128)(2,1)S(1)}, bf16[608,128]{1,0:T(8,128)(2,1)S(1)}, u32[]{:S(2)}, u32[]{:S(2)}) %collective-permute-start.14) | collective-permute-done | bytes 155680 | tf_op jit(solution)/shard_map/ppermute | solution.py:463
  69.5 0.1 collective-permute-start.15
  69.6 0.8 %shard_map.50.refs_2_ = f32[768,512]{1,0:T(8,128)S(1)} custom-call(bf16[1536,512]{1,0:T(8,128)(2,1)S(1)} %get-tuple-element.21.refs_0_, bf16[1536,512]{1,0:T(8,128)(2,1)S(1)} %get-tuple-element.22.refs_1_, bf16[2112,128]{1,0:T(8,128)(2,1)S(1)} %shard_map.49.refs_2_.refs_4_), custom_call_target="tpu_custom_call" | custom-call | tf_op jit(solution)/shard_map/pallas_call | solution.py:29
  70.4 1.4 %shard_map.60 = (f32[768,512]{1,0:T(8,128)S(1)}, f32[768,512]{1,0:T(8,128)S(1)}) custom-call(bf16[1536,512]{1,0:T(8,128)(2,1)S(1)} %get-tuple-element.21.refs_0_, bf16[1536,512]{1,0:T(8,128)(2,1)S(1)} %get-tuple-element.22.refs_1_, f32[768,512]{1,0:T(8,128)S(1)} %shard_map.50.refs_2_, bf16[2112,128]{1,0:T(8,128)(2,1)S(1)} %collective-permute-done.7.refs_3_.refs_7_, ...), custom_call_target="tpu_custom_call" | custom-call | tf_op jit(solution)/shard_map/pallas_call | solution.py:29
  71.9 1.7 %shard_map.70 = (f32[768,512]{1,0:T(8,128)S(1)}, f32[768,512]{1,0:T(8,128)S(1)}) custom-call(bf16[1536,512]{1,0:T(8,128)(2,1)S(1)} %get-tuple-element.21.refs_0_, f32[768,512]{1,0:T(8,128)S(1)} %get-tuple-element.32.refs_1_, f32[768,512]{1,0:T(8,128)S(1)} %get-tuple-element.33.refs_2_, bf16[1216,128]{1,0:T(8,128)(2,1)S(1)} %collective-permute-done.15.refs_3_.refs_8_, ...), custom_call_target="tpu_custom_call" | custom-call | tf_op jit(solution)/shard_map/pallas_call | solution.py:29
  73.6 2.3 %shard_map.71 = (f32[1536,512]{1,0:T(8,128)}, f32[1]{0:T(128)}) custom-call(bf16[1536,512]{1,0:T(8,128)(2,1)S(1)} %get-tuple-element.21.refs_0_, f32[768,512]{1,0:T(8,128)S(1)} %get-tuple-element.38.refs_1_, f32[768,512]{1,0:T(8,128)S(1)} %get-tuple-element.39.refs_2_, bf16[1856,128]{1,0:T(8,128)(2,1)S(1)} %collective-permute-done.23.refs_3_.refs_9_, ...), custom_call_target="tpu_custom_call" | custom-call | tf_op jit(solution)/shard_map/pallas_call | solution.py:29
  (31 shorter events, 0.7 us)
Async XLA Ops:
  3.0 2.5 %collective-permute-start = (bf16[2048,128]{1,0:T(8,128)(2,1)S(1)}, bf16[2048,128]{1,0:T(8,128)(2,1)S(1)}, u32[]{:S(2)}, u32[]{:S(2)}) collective-permute-start(bf16[2048,128]{1,0:T(8,128)(2,1)S(1)} %get-tuple-element.23), channel_id=1, source_target_pairs={{0,1},{1,0},{2,3},{3,2},{4,5},{5,4},{6,7},{7,6},{8,9},{9,8},{10,11... | collective-permute-start | bytes 1572872 | tf_op jit(solution)/shard_map/ppermute | solution.py:463
  4.4 4.7 %collective-permute-start.16 = (bf16[1792,128]{1,0:T(8,128)(2,1)S(1)}, bf16[1792,128]{1,0:T(8,128)(2,1)S(1)}, u32[]{:S(2)}, u32[]{:S(2)}) collective-permute-start(bf16[1792,128]{1,0:T(8,128)(2,1)S(1)} %shard_map.62), channel_id=1, source_target_pairs={{0,1},{1,0},{2,3},{3,2},{4,5},{5,4},{6,7},{7,6},{8,9},{9,8},{10,11... | collective-permute-start | bytes 1376264 | tf_op jit(solution)/shard_map/ppermute | solution.py:463
  5.6 6.7 %collective-permute-start.1 = (bf16[1024,128]{1,0:T(8,128)(2,1)S(1)}, bf16[1024,128]{1,0:T(8,128)(2,1)S(1)}, u32[]{:S(2)}, u32[]{:S(2)}) collective-permute-start(bf16[1024,128]{1,0:T(8,128)(2,1)S(1)} %get-tuple-element.25), channel_id=1, source_target_pairs={{0,5},{1,2},{2,1},{3,6},{4,7},{5,0},{6,3},{7,4},{8,11},{9,12},{10,... | collective-permute-start | bytes 786440 | tf_op jit(solution)/shard_map/ppermute | solution.py:463
  9.3 9.8 %collective-permute-start.17 = (bf16[896,128]{1,0:T(8,128)(2,1)S(1)}, bf16[896,128]{1,0:T(8,128)(2,1)S(1)}, u32[]{:S(2)}, u32[]{:S(2)}) collective-permute-start(bf16[896,128]{1,0:T(8,128)(2,1)S(1)} %get-tuple-element.35), channel_id=1, source_target_pairs={{0,5},{1,2},{2,1},{3,6},{4,7},{5,0},{6,3},{7,4},{8,11},{9,12},{10,... | collective-permute-start | bytes 688136 | tf_op jit(solution)/shard_map/ppermute | solution.py:463
  12.4 4.8 %collective-permute-start.2 = (bf16[512,128]{1,0:T(8,128)(2,1)S(1)}, bf16[512,128]{1,0:T(8,128)(2,1)S(1)}, u32[]{:S(2)}, u32[]{:S(2)}) collective-permute-start(bf16[512,128]{1,0:T(8,128)(2,1)S(1)} %get-tuple-element.27), channel_id=1, source_target_pairs={{0,3},{1,4},{2,7},{3,0},{4,1},{5,6},{6,5},{7,2},{8,13},{9,10},{10,... | collective-permute-start | bytes 393224 | tf_op jit(solution)/shard_map/ppermute | solution.py:463
  15.2 19.4 %collective-permute-start.8 = (bf16[1152,128]{1,0:T(8,128)(2,1)S(1)}, bf16[1152,128]{1,0:T(8,128)(2,1)S(1)}, u32[]{:S(2)}, u32[]{:S(2)}) collective-permute-start(bf16[1152,128]{1,0:T(8,128)(2,1)S(1)} %shard_map.52), channel_id=1, source_target_pairs={{0,1},{1,0},{2,3},{3,2},{4,5},{5,4},{6,7},{7,6},{8,9},{9,8},{10,11... | collective-permute-start | bytes 884744 | tf_op jit(solution)/shard_map/ppermute | solution.py:463
  17.2 5.9 %collective-permute-start.3 = (bf16[512,128]{1,0:T(8,128)(2,1)S(1)}, bf16[512,128]{1,0:T(8,128)(2,1)S(1)}, u32[]{:S(2)}, u32[]{:S(2)}) collective-permute-start(bf16[512,128]{1,0:T(8,128)(2,1)S(1)} %shard_map.45.a_ref), channel_id=1, source_target_pairs={{0,9},{1,17},{2,18},{3,10},{4,20},{5,12},{6,15},{7,23},{8,24},{9,0... | collective-permute-start | bytes 393224 | tf_op jit(solution)/shard_map/ppermute | solution.py:463
  19.1 6.5 %collective-permute-start.18 = (bf16[448,128]{1,0:T(8,128)(2,1)S(1)}, bf16[448,128]{1,0:T(8,128)(2,1)S(1)}, u32[]{:S(2)}, u32[]{:S(2)}) collective-permute-start(bf16[448,128]{1,0:T(8,128)(2,1)S(1)} %get-tuple-element.37), channel_id=1, source_target_pairs={{0,3},{1,4},{2,7},{3,0},{4,1},{5,6},{6,5},{7,2},{8,13},{9,10},{10,... | collective-permute-start | bytes 344072 | tf_op jit(solution)/shard_map/ppermute | solution.py:463
  23.2 8.1 %collective-permute-start.4 = (bf16[512,128]{1,0:T(8,128)(2,1)S(1)}, bf16[512,128]{1,0:T(8,128)(2,1)S(1)}, u32[]{:S(2)}, u32[]{:S(2)}) collective-permute-start(bf16[512,128]{1,0:T(8,128)(2,1)S(1)} %shard_map.46.refs_0_), channel_id=1, source_target_pairs={{0,16},{1,8},{2,11},{3,19},{4,13},{5,21},{6,22},{7,14},{8,1},{9,25... | collective-permute-start | bytes 393224 | tf_op jit(solution)/shard_map/ppermute | solution.py:463
  25.6 7.2 %collective-permute-start.19 = (bf16[448,128]{1,0:T(8,128)(2,1)S(1)}, bf16[448,128]{1,0:T(8,128)(2,1)S(1)}, u32[]{:S(2)}, u32[]{:S(2)}) collective-permute-start(bf16[448,128]{1,0:T(8,128)(2,1)S(1)} %shard_map.65.a_ref), channel_id=1, source_target_pairs={{0,9},{1,17},{2,18},{3,10},{4,20},{5,12},{6,15},{7,23},{8,24},{9,0... | collective-permute-start | bytes 344072 | tf_op jit(solution)/shard_map/ppermute | solution.py:463
  31.8 7.5 %collective-permute-start.5 = (bf16[528,128]{1,0:T(8,128)(2,1)S(1)}, bf16[528,128]{1,0:T(8,128)(2,1)S(1)}, u32[]{:S(2)}, u32[]{:S(2)}) collective-permute-start(bf16[528,128]{1,0:T(8,128)(2,1)S(1)} %shard_map.47.refs_0_), channel_id=1, source_target_pairs={{0,3},{1,4},{2,7},{3,0},{4,1},{5,6},{6,5},{7,2},{8,13},{9,10},{10,... | collective-permute-start | bytes 405512 | tf_op jit(solution)/shard_map/ppermute | solution.py:463
  32.9 6.0 %collective-permute-start.20 = (bf16[448,128]{1,0:T(8,128)(2,1)S(1)}, bf16[448,128]{1,0:T(8,128)(2,1)S(1)}, u32[]{:S(2)}, u32[]{:S(2)}) collective-permute-start(bf16[448,128]{1,0:T(8,128)(2,1)S(1)} %shard_map.66.refs_0_), channel_id=1, source_target_pairs={{0,16},{1,8},{2,11},{3,19},{4,13},{5,21},{6,22},{7,14},{8,1},{9,25... | collective-permute-start | bytes 344072 | tf_op jit(solution)/shard_map/ppermute | solution.py:463
  34.6 9.3 %collective-permute-start.9 = (bf16[576,128]{1,0:T(8,128)(2,1)S(1)}, bf16[576,128]{1,0:T(8,128)(2,1)S(1)}, u32[]{:S(2)}, u32[]{:S(2)}) collective-permute-start(bf16[576,128]{1,0:T(8,128)(2,1)S(1)} %get-tuple-element.29), channel_id=1, source_target_pairs={{0,9},{1,17},{2,18},{3,10},{4,20},{5,12},{6,15},{7,23},{8,24},{9,0... | collective-permute-start | bytes 442376 | tf_op jit(solution)/shard_map/ppermute | solution.py:463
  39.3 4.8 %collective-permute-start.21 = (bf16[464,128]{1,0:T(8,128)(2,1)S(1)}, bf16[464,128]{1,0:T(8,128)(2,1)S(1)}, u32[]{:S(2)}, u32[]{:S(2)}) collective-permute-start(bf16[464,128]{1,0:T(8,128)(2,1)S(1)} %shard_map.67.refs_0_), channel_id=1, source_target_pairs={{0,3},{1,4},{2,7},{3,0},{4,1},{5,6},{6,5},{7,2},{8,13},{9,10},{10,... | collective-permute-start | bytes 356360 | tf_op jit(solution)/shard_map/ppermute | solution.py:463
  39.4 18.5 %collective-permute-start.6 = (bf16[1056,128]{1,0:T(8,128)(2,1)S(1)}, bf16[1056,128]{1,0:T(8,128)(2,1)S(1)}, u32[]{:S(2)}, u32[]{:S(2)}) collective-permute-start(bf16[1056,128]{1,0:T(8,128)(2,1)S(1)} %shard_map.48.refs_0_), channel_id=1, source_target_pairs={{0,5},{1,2},{2,1},{3,6},{4,7},{5,0},{6,3},{7,4},{8,11},{9,12},{10,... | collective-permute-start | bytes 811016 | tf_op jit(solution)/shard_map/ppermute | solution.py:463
  43.9 6.0 %collective-permute-start.10 = (bf16[288,128]{1,0:T(8,128)(2,1)S(1)}, bf16[288,128]{1,0:T(8,128)(2,1)S(1)}, u32[]{:S(2)}, u32[]{:S(2)}) collective-permute-start(bf16[288,128]{1,0:T(8,128)(2,1)S(1)} %get-tuple-element.31), channel_id=1, source_target_pairs={{0,16},{1,8},{2,11},{3,19},{4,13},{5,21},{6,22},{7,14},{8,1},{9,25... | collective-permute-start | bytes 221192 | tf_op jit(solution)/shard_map/ppermute | solution.py:463
  44.1 13.9 %collective-permute-start.22 = (bf16[928,128]{1,0:T(8,128)(2,1)S(1)}, bf16[928,128]{1,0:T(8,128)(2,1)S(1)}, u32[]{:S(2)}, u32[]{:S(2)}) collective-permute-start(bf16[928,128]{1,0:T(8,128)(2,1)S(1)} %shard_map.68.refs_0_), channel_id=1, source_target_pairs={{0,5},{1,2},{2,1},{3,6},{4,7},{5,0},{6,3},{7,4},{8,11},{9,12},{10,... | collective-permute-start | bytes 712712 | tf_op jit(solution)/shard_map/ppermute | solution.py:463
  50.0 3.8 %collective-permute-start.11 = (bf16[288,128]{1,0:T(8,128)(2,1)S(1)}, bf16[288,128]{1,0:T(8,128)(2,1)S(1)}, u32[]{:S(2)}, u32[]{:S(2)}) collective-permute-start(bf16[288,128]{1,0:T(8,128)(2,1)S(1)} %shard_map.55.a_ref), channel_id=1, source_target_pairs={{0,5},{1,2},{2,1},{3,6},{4,7},{5,0},{6,3},{7,4},{8,11},{9,12},{10,... | collective-permute-start | bytes 221192 | tf_op jit(solution)/shard_map/ppermute | solution.py:463
  53.9 3.8 %collective-permute-start.12 = (bf16[288,128]{1,0:T(8,128)(2,1)S(1)}, bf16[288,128]{1,0:T(8,128)(2,1)S(1)}, u32[]{:S(2)}, u32[]{:S(2)}) collective-permute-start(bf16[288,128]{1,0:T(8,128)(2,1)S(1)} %shard_map.56.refs_0_), channel_id=1, source_target_pairs={{0,3},{1,4},{2,7},{3,0},{4,1},{5,6},{6,5},{7,2},{8,13},{9,10},{10,... | collective-permute-start | bytes 221192 | tf_op jit(solution)/shard_map/ppermute | solution.py:463
  57.9 5.3 %collective-permute-start.13 = (bf16[304,128]{1,0:T(8,128)(2,1)S(1)}, bf16[304,128]{1,0:T(8,128)(2,1)S(1)}, u32[]{:S(2)}, u32[]{:S(2)}) collective-permute-start(bf16[304,128]{1,0:T(8,128)(2,1)S(1)} %shard_map.57.refs_0_), channel_id=1, source_target_pairs={{0,16},{1,8},{2,11},{3,19},{4,13},{5,21},{6,22},{7,14},{8,1},{9,25... | collective-permute-start | bytes 233480 | tf_op jit(solution)/shard_map/ppermute | solution.py:463
  57.9 12.5 %collective-permute-start.7 = (bf16[2112,128]{1,0:T(8,128)(2,1)S(1)}, bf16[2112,128]{1,0:T(8,128)(2,1)S(1)}, u32[]{:S(2)}, u32[]{:S(2)}) collective-permute-start(bf16[2112,128]{1,0:T(8,128)(2,1)S(1)} %shard_map.49.refs_2_.refs_4_), channel_id=1, source_target_pairs={{0,1},{1,0},{2,3},{3,2},{4,5},{5,4},{6,7},{7,6},{8,9},{9,8},{10,11... | collective-permute-start | bytes 1622024 | tf_op jit(solution)/shard_map/ppermute | solution.py:463
  58.1 15.5 %collective-permute-start.23 = (bf16[1856,128]{1,0:T(8,128)(2,1)S(1)}, bf16[1856,128]{1,0:T(8,128)(2,1)S(1)}, u32[]{:S(2)}, u32[]{:S(2)}) collective-permute-start(bf16[1856,128]{1,0:T(8,128)(2,1)S(1)} %shard_map.69.refs_4_.refs_6_), channel_id=1, source_target_pairs={{0,1},{1,0},{2,3},{3,2},{4,5},{5,4},{6,7},{7,6},{8,9},{9,8},{10,11... | collective-permute-start | bytes 1425416 | tf_op jit(solution)/shard_map/ppermute | solution.py:463
  63.2 6.3 %collective-permute-start.14 = (bf16[608,128]{1,0:T(8,128)(2,1)S(1)}, bf16[608,128]{1,0:T(8,128)(2,1)S(1)}, u32[]{:S(2)}, u32[]{:S(2)}) collective-permute-start(bf16[608,128]{1,0:T(8,128)(2,1)S(1)} %shard_map.58.refs_0_), channel_id=1, source_target_pairs={{0,9},{1,17},{2,18},{3,10},{4,20},{5,12},{6,15},{7,23},{8,24},{9,0... | collective-permute-start | bytes 466952 | tf_op jit(solution)/shard_map/ppermute | solution.py:463
  69.5 2.4 %collective-permute-start.15 = (bf16[1216,128]{1,0:T(8,128)(2,1)S(1)}, bf16[1216,128]{1,0:T(8,128)(2,1)S(1)}, u32[]{:S(2)}, u32[]{:S(2)}) collective-permute-start(bf16[1216,128]{1,0:T(8,128)(2,1)S(1)} %shard_map.59.refs_4_.refs_5_), channel_id=1, source_target_pairs={{0,1},{1,0},{2,3},{3,2},{4,5},{5,4},{6,7},{7,6},{8,9},{9,8},{10,11... | collective-permute-start | bytes 933896 | tf_op jit(solution)/shard_map/ppermute | solution.py:463

commit v6 on v5

--- a/solution.py
+++ b/solution.py
@@ -9,8 +9,8 @@
 TILE = 128
 PAD = 16
 SHARES = 4
-CUTS = (16 / 39, 30 / 39)
-TURNS = (0, 2, 1)
+CUTS = (17 / 39, 31 / 39)
+TURNS = (0, 1, 2)
 FAR_FIRST = 2
 AXES = ("gr", "gc")
 BF16 = jnp.bfloat16
@@ -200,7 +200,7 @@
     out_ref[0:rows, :] = total.astype(BF16)
     square = total * total
     if diagonal:
-        tile = (lax.broadcasted_iota(jnp.int32, (rows, TILE), 0) + offset) // TILE
+        tile = (lax.broadcasted_iota(jnp.int32, (rows, TILE), 0) + offset) >> (TILE.bit_length() - 1)
         single = tile == diagonal[0]
         for at in diagonal[1:]:
             single |= tile == at
@@ -248,177 +248,164 @@
     ref[i * TILE : (i + 1) * TILE, j * TILE : (j + 1) * TILE] = value
 
 
-def piece_values(piece_ref, tiles, flip, orb_ref, mats, side, extra):
-    h, low, up = starts(flip, side)
-    near_ref, far_ref, flip_ref = mats
-    near, far, back = {}, {}, {}
-    extras = []
+def tables(tiles, side):
+    result = {"near": {}, "far": {}, "back": {}}
     for n, (which, i, j) in enumerate(tiles):
         if which == "near":
-            near[(i, j)] = (n, False)
-            if i != j:
-                near[(j, i)] = (n, True)
+            result["near"][(i, j)] = n
+            result["near"][(j, i)] = n
         elif which == "far":
-            far[(i, j)] = (n, False)
-            back[(j, i)] = (n, True)
-        else:
-            extras.append((n, i))
-    for table in (far, back):
-        if extras:
+            result["far"][(i, j)] = n
+            result["back"][(j, i)] = n
+    if any(which == "extra" for which, _, _ in tiles):
+        for name in ("far", "back"):
             for i in range(side):
-                table[(i, i)] = None
+                result[name][(i, i)] = None
+    return {name: table for name, table in result.items() if table}
+
+
+def spans_of(table, side):
     spans = {}
+    for p in range(0, side, 2):
+        columns = [j for (i, j) in table if i in (p, p + 1)]
+        if columns:
+            spans[p] = (min(columns), max(columns) + 1)
+    return spans
+
+
+def reach(tiles, flip, side):
+    result = set()
+    for name, table in tables(tiles, side).items():
+        result |= {(1 - flip if name == "back" else flip, p) for p in spans_of(table, side)}
+    return result
+
+
+def fill(piece_ref, tiles, flip, mats, side, extra):
+    h, low, up = starts(flip, side)
+    found = tables(tiles, side)
     zero = jnp.zeros((TILE, TILE), BF16)
-    for name, ref, table in (("near", near_ref, near), ("far", far_ref, far), ("back", flip_ref, back)):
-        for p in range(0, side, 2):
-            rows = range(p, min(p + 2, side))
-            columns = [j for (i, j) in table if i in rows]
-            if not columns:
-                continue
-            span = (min(columns), max(columns) + 1)
-            spans[(name, p)] = span
-            for i in rows:
-                for j in range(*span):
+    terms = {}
+    for name, table in found.items():
+        ref = mats[name]
+        for p, (begin, end) in spans_of(table, side).items():
+            last = min(p + 2, side)
+            for i in range(p, last):
+                for j in range(begin, end):
                     if table.get((i, j)) is None:
                         put_block(ref, i, j, zero)
-    for (i, j), (n, turned) in near.items():
-        if not turned:
-            value = take_tile(piece_ref, n)
-            put_block(near_ref, i, j, value)
+            key = (1 - flip if name == "back" else flip, p)
+            left = (slice(p * TILE, last * TILE), slice(begin * TILE, end * TILE))
+            base = up if name == "far" else low
+            terms.setdefault(key, []).append((ref, left, base + begin * TILE, (end - begin) * TILE))
+    for n, (which, i, j) in enumerate(tiles):
+        value = take_tile(piece_ref, n)
+        if which == "near":
+            put_block(mats["near"], i, j, value)
             if i != j:
-                put_block(near_ref, j, i, value.T)
-    for (i, j), entry in far.items():
-        if entry is not None:
-            value = take_tile(piece_ref, entry[0])
-            put_block(far_ref, i, j, value)
-            put_block(flip_ref, j, i, value.T)
-    for n, k in extras:
-        value = take_tile(piece_ref, n)
-        at = pl.ds(pl.multiple_of((h * extra + k) * TILE, TILE), TILE)
-        far_ref[at, at] = value
-        flip_ref[at, at] = value.T
-
-    def part(name, ref, p, base):
-        if (name, p) not in spans:
-            return None
-        begin, end = spans[(name, p)]
-        left = ref[p * TILE : min(p + 2, side) * TILE, begin * TILE : end * TILE]
-        right = orb_ref[pl.ds(pl.multiple_of(base + begin * TILE, TILE), (end - begin) * TILE), :]
-        return jnp.dot(left, right, preferred_element_type=F32)
-
-    for p in range(0, side, 2):
-        one, two = part("near", near_ref, p, low), part("far", far_ref, p, up)
-        if one is not None or two is not None:
-            yield flip, p, one if two is None else two if one is None else one + two
-    for p in range(0, side, 2):
-        value = part("back", flip_ref, p, low)
-        if value is not None:
-            yield 1 - flip, p, value
-
-
-def apply_kernel(*refs, plan, blocks, side, extra, last):
+                put_block(mats["near"], j, i, value.T)
+        elif which == "far":
+            put_block(mats["far"], i, j, value)
+            put_block(mats["back"], j, i, value.T)
+        else:
+            at = pl.ds(pl.multiple_of((h * extra + i) * TILE, TILE), TILE)
+            mats["far"][at, at] = value
+            mats["back"][at, at] = value.T
+    return terms
+
+
+def apply_kernel(*refs, plan, given, velocities, count, side, extra, names):
     refs = list(refs)
     orb_ref = refs.pop(0)
-    vel_ref = refs.pop(0) if blocks["vel"] else None
-    bases = {b: refs.pop(0) for b in blocks["in"]}
+    vel_ref = refs.pop(0) if velocities else None
+    bases = {b: refs.pop(0) for b in given}
     pieces = [refs.pop(0) for _ in plan]
+    touched = set().union(*(reach(tiles, flip, side) for tiles, flip in plan))
+    last = count > 0
+    copies = []
     if last:
-        squares = [refs.pop(0) for _ in range(blocks["squares"])]
-        out_hbm, norm_ref = refs.pop(0), refs.pop(0)
-        scratch = refs.pop(0)
+        squares = [refs.pop(0) for _ in range(count)]
+        out_hbm, norm_ref, scratch, sems = refs.pop(0), refs.pop(0), refs.pop(0), refs.pop()
         outs = {b: scratch.at[b] for b in (0, 1)}
     else:
-        outs = {b: refs.pop(0) for b in blocks["out"]}
-    mats = refs[:3]
+        outs = {b: refs.pop(0) for b in sorted({b for b, _ in touched})}
     _, low, up = starts(0, side)
     base_row = (low, up)
-    written = set()
-    copies = []
 
     def rows_of(p):
         return slice(p * TILE, min(p + 2, side) * TILE)
 
+    def place(b, p):
+        rows = rows_of(p)
+        return pl.ds(pl.multiple_of(base_row[b] + rows.start, TILE), rows.stop - rows.start)
+
     def before(b, p):
-        if (b, p) in written:
-            return outs[b][rows_of(p), :]
-        if b in bases:
-            return bases[b][rows_of(p), :]
-        rows = rows_of(p)
-        at = pl.ds(pl.multiple_of(base_row[b] + rows.start, TILE), rows.stop - rows.start)
-        return vel_ref[at, :].astype(F32)
+        return bases[b][rows_of(p), :] if b in bases else vel_ref[place(b, p), :].astype(F32)
 
     def send(source, b, p):
-        rows = rows_of(p)
-        at = pl.ds(pl.multiple_of(base_row[b] + rows.start, TILE), rows.stop - rows.start)
-        copy = pltpu.make_async_copy(source.at[rows], out_hbm.at[at], refs[3].at[len(copies)])
+        copy = pltpu.make_async_copy(source.at[rows_of(p)], out_hbm.at[place(b, p)], sems.at[len(copies)])
         copy.start()
         copies.append(copy)
 
+    for b in outs:
+        for p in range(0, side, 2):
+            if (b, p) not in touched:
+                if last:
+                    send(bases[b], b, p)
+                else:
+                    outs[b][rows_of(p), :] = before(b, p)
+    terms = {}
+    for (tiles, flip), piece, own in zip(plan, pieces, names):
+        mats = {name: refs.pop(0) for name in own}
+        for key, value in fill(piece, tiles, flip, mats, side, extra).items():
+            terms.setdefault(key, []).extend(value)
+    for b, p in sorted(touched):
+        total = None
+        for ref, left, at, rows in terms[(b, p)]:
+            right = orb_ref[pl.ds(pl.multiple_of(at, TILE), rows), :]
+            value = jnp.dot(ref[left], right, preferred_element_type=F32)
+            total = value if total is None else total + value
+        outs[b][rows_of(p), :] = before(b, p) - 0.5 * total
+        if last:
+            send(outs[b], b, p)
     if last:
-        (tiles, flip), piece = plan[0], pieces[0]
-        touched = {("near", i // 2 * 2) for which, i, j in tiles if which == "near"}
-        touched |= {("near", j // 2 * 2) for which, i, j in tiles if which == "near"}
-        touched |= {("near", i // 2 * 2) for which, i, j in tiles if which == "far"}
-        touched |= {("back", j // 2 * 2) for which, i, j in tiles if which == "far"}
-        if any(which == "extra" for which, _, _ in tiles):
-            touched |= {(name, p) for name in ("near", "back") for p in range(0, side, 2)}
-        for b, name in ((flip, "near"), (1 - flip, "back")):
-            for p in range(0, side, 2):
-                if (name, p) not in touched:
-                    send(bases[b], b, p)
-    for (tiles, flip), piece in zip(plan, pieces):
-        for b, p, value in piece_values(piece, tiles, flip, orb_ref, mats, side, extra):
-            outs[b][rows_of(p), :] = before(b, p) - 0.5 * value
-            written.add((b, p))
-            if last:
-                send(outs[b], b, p)
-    if last:
-        count = len(squares) // 2
-        square = tails(squares[:count]) + tails(squares[count:])
+        square = tails(squares[: count // 2]) + tails(squares[count // 2 :])
         norm_ref[0] = (jnp.sqrt(square) / (2 * side * TILE))[0, 0]
         for copy in copies:
             copy.wait()
-    else:
-        for b in outs:
-            for p in range(0, side, 2):
-                if (b, p) not in written:
-                    outs[b][rows_of(p), :] = before(b, p)
-
-
-def apply(orb, vel, bases, plan, pieces, squares=None):
+
+
+def apply(orb, vel, bases, plan, pieces, squares=()):
     side, extra = geometry(orb.shape[0])
     wide, columns = side * TILE, orb.shape[1]
-    last = squares is not None
-    touched = set()
-    for tiles, flip in plan:
-        touched.add(flip)
-        if any(which != "near" for which, _, _ in tiles):
-            touched.add(1 - flip)
-    given = [b for b in (0, 1) if bases[b] is not None and (b in touched or last)]
-    blocks = {"in": given, "out": sorted(touched), "vel": any(bases[b] is None for b in touched)}
-    operands = [orb] + ([vel] if blocks["vel"] else []) + [bases[b] for b in given] + list(pieces)
-    mats = [pltpu.VMEM((wide, wide), BF16)] * 3
-    if last:
-        blocks["squares"] = len(squares)
-        operands += squares
-        panels = 2 * -(-side // 2)
+    blocks = [0, 1] if squares else sorted({b for tiles, flip in plan for b, _ in reach(tiles, flip, side)})
+    given = [b for b in blocks if bases[b] is not None]
+    velocities = len(given) < len(blocks)
+    names = [list(tables(tiles, side)) for tiles, _ in plan]
+    mats = [pltpu.VMEM((wide, wide), BF16) for own in names for _ in own]
+    kernel = lambda *refs: apply_kernel(
+        *refs,
+        plan=plan,
+        given=given,
+        velocities=velocities,
+        count=len(squares),
+        side=side,
+        extra=extra,
+        names=names,
+    )
+    operands = [orb] + ([vel] if velocities else []) + [bases[b] for b in given] + list(pieces) + list(squares)
+    if squares:
         return call(
-            lambda *refs: apply_kernel(*refs, plan=plan, blocks=blocks, side=side, extra=extra, last=True),
+            kernel,
             [jax.ShapeDtypeStruct(orb.shape, F32), jax.ShapeDtypeStruct((1,), F32)],
             14,
             *operands,
-            scratch=[pltpu.VMEM((2, wide, columns), F32)] + mats + [pltpu.SemaphoreType.DMA((panels,))],
+            scratch=[pltpu.VMEM((2, wide, columns), F32)] + mats + [pltpu.SemaphoreType.DMA((2 * -(-side // 2),))],
             out_specs=[HBM, SMEM],
         )
-    outs = call(
-        lambda *refs: apply_kernel(*refs, plan=plan, blocks=blocks, side=side, extra=extra, last=False),
-        [jax.ShapeDtypeStruct((wide, columns), F32)] * len(touched),
-        10,
-        *operands,
-        scratch=mats,
-    )
+    out = [jax.ShapeDtypeStruct((wide, columns), F32)] * len(blocks)
+    values = call(kernel, out, 8 + 2 * len(mats), *operands, scratch=mats)
     result = list(bases)
-    for b, value in zip(sorted(touched), outs):
+    for b, value in zip(blocks, values):
         result[b] = value
     return result
 
@@ -483,10 +470,9 @@
     first, second, third = TURNS
     blocks = [None, None]
     blocks = apply(orbitals, velocities, blocks, [(chunks[first], 0)], [joined[first]])
-    plan = [(chunks[first], 1), (chunks[second], 0)]
-    blocks = apply(orbitals, velocities, blocks, plan, [far[first], joined[second]])
-    plan = [(chunks[second], 1), (chunks[third], 0)]
-    blocks = apply(orbitals, velocities, blocks, plan, [far[second], joined[third]])
+    blocks = apply(orbitals, velocities, blocks, [(chunks[first], 1)], [far[first]])
+    plan = [(chunks[second], 0), (chunks[second], 1), (chunks[third], 0)]
+    blocks = apply(orbitals, velocities, blocks, plan, [joined[second], far[second], joined[third]])
     squares = [joined[k] for k in TURNS] + [far[k] for k in TURNS]
     return tuple(apply(orbitals, velocities, blocks, [(chunks[third], 1)], [far[third]], squares))
 

time: 76 us -> 77.7 us (1.022)
  waiting for transfers between devices: 31.6 us -> 33.7 us
    ppermute x24, waiting for transfers between devices: 31.6 us -> 33.7 us  [move(): lax.ppermute(value, AXES, swap if pair is None else permutation(nr, nc, p...]
  transfers between devices with their start and end apart: 24 -> 24, of which waited for: 11 -> 15; matrix products, arithmetic and copies ran while one was open for 0% -> 0% of each run, Pallas kernels for 13% -> 12%
where the time goes in v6:
time: 77.7 us; the launch traced here: 77.5 us
  waiting for transfers between devices  33.7 us (43%)
  starting transfers between devices  28.5 us (37%)
  Pallas kernels  14.5 us (19%)
  between operations  0.88 us (1%)
    ppermute x24, waiting for transfers between devices, move(): lax.ppermute(value, AXES, swap if pair is None else permutation(nr, nc, p...  33.7 us
    ppermute x24, starting transfers between devices, move(): lax.ppermute(value, AXES, swap if pair is None else permutation(nr, nc, p...  28.5 us
    pallas_call x31, Pallas kernels, call(): pl.pallas_call(kernel, out_shape=out, in_specs=in_specs or [VMEM] * len(o...  14.5 us
  transfers between devices with their start and end apart: 24, of which 15 were waited for; matrix products, arithmetic and copies ran while one was open for 0% of the time, Pallas kernels for 12%

profile of v6, /device:TPU:0, one launch (start us, length us, event | category | flops | bytes accessed | tf_op | source)
XLA Modules:
  0.0 77.5 jit_solution(7284510195742359818)
XLA Ops:
  0.6 2.4 %shard_map.41 = (bf16[2176,128]{1,0:T(8,128)(2,1)S(1)}, bf16[1536,512]{1,0:T(8,128)(2,1)S(1)}, bf16[1536,512]{1,0:T(8,128)(2,1)S(1)}) custom-call(bf16[1536,512]{1,0:T(8,128)(2,1)} %refs_0_.1, bf16[1536,512]{1,0:T(8,128)(2,1)} %refs_1_.1), custom_call_target="tpu_custom_call" | custom-call | tf_op jit(solution)/shard_map/pallas_call | solution.py:29
  3.0 0.6 collective-permute-start
  3.6 0.9 %shard_map.53 = bf16[1792,128]{1,0:T(8,128)(2,1)S(1)} custom-call(bf16[1536,512]{1,0:T(8,128)(2,1)S(1)} %get-tuple-element.19.refs_0_, bf16[1536,512]{1,0:T(8,128)(2,1)S(1)} %get-tuple-element.20.refs_1_), custom_call_target="tpu_custom_call" | custom-call | tf_op jit(solution)/shard_map/pallas_call | solution.py:29
  4.5 0.9 %shard_map.42.refs_0_ = bf16[2176,128]{1,0:T(8,128)(2,1)S(1)} custom-call(bf16[1536,512]{1,0:T(8,128)(2,1)S(1)} %get-tuple-element.19.refs_0_, bf16[1536,512]{1,0:T(8,128)(2,1)S(1)} %get-tuple-element.20.refs_1_), custom_call_target="tpu_custom_call" | custom-call | tf_op jit(solution)/shard_map/pallas_call | solution.py:29
  5.5 0.1 shard_map.43
  5.7 2.7 %collective-permute-start.1 = (bf16[1088,128]{1,0:T(8,128)(2,1)S(1)}, bf16[1088,128]{1,0:T(8,128)(2,1)S(1)}, u32[]{:S(2)}, u32[]{:S(2)}) collective-permute-start(bf16[1088,128]{1,0:T(8,128)(2,1)S(1)} %get-tuple-element.23), channel_id=1, source_target_pairs={{0,5},{1,2},{2,1},{3,6},{4,7},{5,0},{6,3},{7,4},{8,11},{9,12},{10,... | collective-permute-start | bytes 835592 | tf_op jit(solution)/shard_map/ppermute | solution.py:450
  8.3 4.2 %collective-permute-done.1.refs_1_ = bf16[1088,128]{1,0:T(8,128)(2,1)S(1)} collective-permute-done((bf16[1088,128]{1,0:T(8,128)(2,1)S(1)}, bf16[1088,128]{1,0:T(8,128)(2,1)S(1)}, u32[]{:S(2)}, u32[]{:S(2)}) %collective-permute-start.1) | collective-permute-done | bytes 278560 | tf_op jit(solution)/shard_map/ppermute | solution.py:450
  12.6 1.9 %collective-permute-start.2 = (bf16[544,128]{1,0:T(8,128)(2,1)S(1)}, bf16[544,128]{1,0:T(8,128)(2,1)S(1)}, u32[]{:S(2)}, u32[]{:S(2)}) collective-permute-start(bf16[544,128]{1,0:T(8,128)(2,1)S(1)} %get-tuple-element.25), channel_id=1, source_target_pairs={{0,3},{1,4},{2,7},{3,0},{4,1},{5,6},{6,5},{7,2},{8,13},{9,10},{10,... | collective-permute-start | bytes 417800 | tf_op jit(solution)/shard_map/ppermute | solution.py:450
  14.5 0.9 %shard_map.52.refs_0_ = bf16[1792,128]{1,0:T(8,128)(2,1)S(1)} custom-call(bf16[1536,512]{1,0:T(8,128)(2,1)S(1)} %get-tuple-element.19.refs_0_, bf16[1536,512]{1,0:T(8,128)(2,1)S(1)} %get-tuple-element.20.refs_1_), custom_call_target="tpu_custom_call" | custom-call | tf_op jit(solution)/shard_map/pallas_call | solution.py:29
  15.4 0.1 shard_map.54
  15.5 1.6 %collective-permute-start.9 = (bf16[896,128]{1,0:T(8,128)(2,1)S(1)}, bf16[896,128]{1,0:T(8,128)(2,1)S(1)}, u32[]{:S(2)}, u32[]{:S(2)}) collective-permute-start(bf16[896,128]{1,0:T(8,128)(2,1)S(1)} %get-tuple-element.27), channel_id=1, source_target_pairs={{0,5},{1,2},{2,1},{3,6},{4,7},{5,0},{6,3},{7,4},{8,11},{9,12},{10,... | collective-permute-start | bytes 688136 | tf_op jit(solution)/shard_map/ppermute | solution.py:450
  17.1 0.2 collective-permute-done.2.b_ref
  17.3 1.9 %collective-permute-start.3 = (bf16[544,128]{1,0:T(8,128)(2,1)S(1)}, bf16[544,128]{1,0:T(8,128)(2,1)S(1)}, u32[]{:S(2)}, u32[]{:S(2)}) collective-permute-start(bf16[544,128]{1,0:T(8,128)(2,1)S(1)} %shard_map.45.a_ref), channel_id=1, source_target_pairs={{0,9},{1,17},{2,18},{3,10},{4,20},{5,12},{6,15},{7,23},{8,24},{9,0... | collective-permute-start | bytes 417800 | tf_op jit(solution)/shard_map/ppermute | solution.py:450
  19.1 1.9 %collective-permute-done.9.refs_1_ = bf16[896,128]{1,0:T(8,128)(2,1)S(1)} collective-permute-done((bf16[896,128]{1,0:T(8,128)(2,1)S(1)}, bf16[896,128]{1,0:T(8,128)(2,1)S(1)}, u32[]{:S(2)}, u32[]{:S(2)}) %collective-permute-start.9) | collective-permute-done | bytes 229408 | tf_op jit(solution)/shard_map/ppermute | solution.py:450
  21.1 0.5 collective-permute-start.10
  21.6 1.8 %collective-permute-done.3.b_ref = bf16[544,128]{1,0:T(8,128)(2,1)S(1)} collective-permute-done((bf16[544,128]{1,0:T(8,128)(2,1)S(1)}, bf16[544,128]{1,0:T(8,128)(2,1)S(1)}, u32[]{:S(2)}, u32[]{:S(2)}) %collective-permute-start.3) | collective-permute-done | bytes 139296 | tf_op jit(solution)/shard_map/ppermute | solution.py:450
  23.4 2.6 %collective-permute-start.4 = (bf16[544,128]{1,0:T(8,128)(2,1)S(1)}, bf16[544,128]{1,0:T(8,128)(2,1)S(1)}, u32[]{:S(2)}, u32[]{:S(2)}) collective-permute-start(bf16[544,128]{1,0:T(8,128)(2,1)S(1)} %shard_map.46.refs_0_), channel_id=1, source_target_pairs={{0,16},{1,8},{2,11},{3,19},{4,13},{5,21},{6,22},{7,14},{8,1},{9,25... | collective-permute-start | bytes 417800 | tf_op jit(solution)/shard_map/ppermute | solution.py:450
  26.1 0.6 shard_map.62
  26.6 0.6 collective-permute-start.16
  27.3 0.1 collective-permute-start.11
  27.4 3.6 %collective-permute-done.4.refs_1_ = bf16[544,128]{1,0:T(8,128)(2,1)S(1)} collective-permute-done((bf16[544,128]{1,0:T(8,128)(2,1)S(1)}, bf16[544,128]{1,0:T(8,128)(2,1)S(1)}, u32[]{:S(2)}, u32[]{:S(2)}) %collective-permute-start.4) | collective-permute-done | bytes 139296 | tf_op jit(solution)/shard_map/ppermute | solution.py:450
  31.0 0.4 shard_map.47.refs_0_
  31.4 0.5 collective-permute-start.5
  31.9 1.5 %collective-permute-done.11.b_ref = bf16[448,128]{1,0:T(8,128)(2,1)S(1)} collective-permute-done((bf16[448,128]{1,0:T(8,128)(2,1)S(1)}, bf16[448,128]{1,0:T(8,128)(2,1)S(1)}, u32[]{:S(2)}, u32[]{:S(2)}) %collective-permute-start.11) | collective-permute-done | bytes 114720 | tf_op jit(solution)/shard_map/ppermute | solution.py:450
  33.4 1.4 %collective-permute-start.12 = (bf16[448,128]{1,0:T(8,128)(2,1)S(1)}, bf16[448,128]{1,0:T(8,128)(2,1)S(1)}, u32[]{:S(2)}, u32[]{:S(2)}) collective-permute-start(bf16[448,128]{1,0:T(8,128)(2,1)S(1)} %shard_map.57.refs_0_), channel_id=1, source_target_pairs={{0,16},{1,8},{2,11},{3,19},{4,13},{5,21},{6,22},{7,14},{8,1},{9,25... | collective-permute-start | bytes 344072 | tf_op jit(solution)/shard_map/ppermute | solution.py:450
  34.8 1.1 %collective-permute-done.5.refs_1_ = bf16[560,128]{1,0:T(8,128)(2,1)S(1)} collective-permute-done((bf16[560,128]{1,0:T(8,128)(2,1)S(1)}, bf16[560,128]{1,0:T(8,128)(2,1)S(1)}, u32[]{:S(2)}, u32[]{:S(2)}) %collective-permute-start.5) | collective-permute-done | bytes 143392 | tf_op jit(solution)/shard_map/ppermute | solution.py:450
  36.0 2.2 %collective-permute-start.6 = (bf16[1120,128]{1,0:T(8,128)(2,1)S(1)}, bf16[1120,128]{1,0:T(8,128)(2,1)S(1)}, u32[]{:S(2)}, u32[]{:S(2)}) collective-permute-start(bf16[1120,128]{1,0:T(8,128)(2,1)S(1)} %shard_map.48.refs_0_), channel_id=1, source_target_pairs={{0,5},{1,2},{2,1},{3,6},{4,7},{5,0},{6,3},{7,4},{8,11},{9,12},{10,... | collective-permute-start | bytes 860168 | tf_op jit(solution)/shard_map/ppermute | solution.py:450
  38.2 2.0 %collective-permute-done.12.refs_1_ = bf16[448,128]{1,0:T(8,128)(2,1)S(1)} collective-permute-done((bf16[448,128]{1,0:T(8,128)(2,1)S(1)}, bf16[448,128]{1,0:T(8,128)(2,1)S(1)}, u32[]{:S(2)}, u32[]{:S(2)}) %collective-permute-start.12) | collective-permute-done | bytes 114720 | tf_op jit(solution)/shard_map/ppermute | solution.py:450
  40.2 0.2 shard_map.58.refs_0_
  40.4 0.6 shard_map.61.refs_0_
  41.1 1.4 %collective-permute-start.17 = (bf16[512,128]{1,0:T(8,128)(2,1)S(1)}, bf16[512,128]{1,0:T(8,128)(2,1)S(1)}, u32[]{:S(2)}, u32[]{:S(2)}) collective-permute-start(bf16[512,128]{1,0:T(8,128)(2,1)S(1)} %get-tuple-element.31), channel_id=1, source_target_pairs={{0,9},{1,17},{2,18},{3,10},{4,20},{5,12},{6,15},{7,23},{8,24},{9,0... | collective-permute-start | bytes 393224 | tf_op jit(solution)/shard_map/ppermute | solution.py:450
  42.5 2.1 %collective-permute-done.13.refs_1_ = bf16[464,128]{1,0:T(8,128)(2,1)S(1)} collective-permute-done((bf16[464,128]{1,0:T(8,128)(2,1)S(1)}, bf16[464,128]{1,0:T(8,128)(2,1)S(1)}, u32[]{:S(2)}, u32[]{:S(2)}) %collective-permute-start.13) | collective-permute-done | bytes 118816 | tf_op jit(solution)/shard_map/ppermute | solution.py:450
  44.7 1.9 %collective-permute-start.14 = (bf16[928,128]{1,0:T(8,128)(2,1)S(1)}, bf16[928,128]{1,0:T(8,128)(2,1)S(1)}, u32[]{:S(2)}, u32[]{:S(2)}) collective-permute-start(bf16[928,128]{1,0:T(8,128)(2,1)S(1)} %shard_map.59.refs_0_), channel_id=1, source_target_pairs={{0,5},{1,2},{2,1},{3,6},{4,7},{5,0},{6,3},{7,4},{8,11},{9,12},{10,... | collective-permute-start | bytes 712712 | tf_op jit(solution)/shard_map/ppermute | solution.py:450
  46.6 0.4 collective-permute-done.17.refs_1_
  47.0 2.7 %collective-permute-start.18 = (bf16[256,128]{1,0:T(8,128)(2,1)S(1)}, bf16[256,128]{1,0:T(8,128)(2,1)S(1)}, u32[]{:S(2)}, u32[]{:S(2)}) collective-permute-start(bf16[256,128]{1,0:T(8,128)(2,1)S(1)} %get-tuple-element.33), channel_id=1, source_target_pairs={{0,16},{1,8},{2,11},{3,19},{4,13},{5,21},{6,22},{7,14},{8,1},{9,25... | collective-permute-start | bytes 196616 | tf_op jit(solution)/shard_map/ppermute | solution.py:450
  49.7 2.7 %collective-permute-done.18.b_ref = bf16[256,128]{1,0:T(8,128)(2,1)S(1)} collective-permute-done((bf16[256,128]{1,0:T(8,128)(2,1)S(1)}, bf16[256,128]{1,0:T(8,128)(2,1)S(1)}, u32[]{:S(2)}, u32[]{:S(2)}) %collective-permute-start.18) | collective-permute-done | bytes 65568 | tf_op jit(solution)/shard_map/ppermute | solution.py:450
  52.4 1.2 %collective-permute-start.19 = (bf16[256,128]{1,0:T(8,128)(2,1)S(1)}, bf16[256,128]{1,0:T(8,128)(2,1)S(1)}, u32[]{:S(2)}, u32[]{:S(2)}) collective-permute-start(bf16[256,128]{1,0:T(8,128)(2,1)S(1)} %shard_map.65.a_ref), channel_id=1, source_target_pairs={{0,5},{1,2},{2,1},{3,6},{4,7},{5,0},{6,3},{7,4},{8,11},{9,12},{10,... | collective-permute-start | bytes 196616 | tf_op jit(solution)/shard_map/ppermute | solution.py:450
  53.7 2.4 %collective-permute-done.19.b_ref = bf16[256,128]{1,0:T(8,128)(2,1)S(1)} collective-permute-done((bf16[256,128]{1,0:T(8,128)(2,1)S(1)}, bf16[256,128]{1,0:T(8,128)(2,1)S(1)}, u32[]{:S(2)}, u32[]{:S(2)}) %collective-permute-start.19) | collective-permute-done | bytes 65568 | tf_op jit(solution)/shard_map/ppermute | solution.py:450
  56.1 1.5 %collective-permute-start.20 = (bf16[256,128]{1,0:T(8,128)(2,1)S(1)}, bf16[256,128]{1,0:T(8,128)(2,1)S(1)}, u32[]{:S(2)}, u32[]{:S(2)}) collective-permute-start(bf16[256,128]{1,0:T(8,128)(2,1)S(1)} %shard_map.66.refs_0_), channel_id=1, source_target_pairs={{0,3},{1,4},{2,7},{3,0},{4,1},{5,6},{6,5},{7,2},{8,13},{9,10},{10,... | collective-permute-start | bytes 196616 | tf_op jit(solution)/shard_map/ppermute | solution.py:450
  57.7 2.2 %collective-permute-done.20.refs_1_ = bf16[256,128]{1,0:T(8,128)(2,1)S(1)} collective-permute-done((bf16[256,128]{1,0:T(8,128)(2,1)S(1)}, bf16[256,128]{1,0:T(8,128)(2,1)S(1)}, u32[]{:S(2)}, u32[]{:S(2)}) %collective-permute-start.20) | collective-permute-done | bytes 65568 | tf_op jit(solution)/shard_map/ppermute | solution.py:450
  59.9 0.1 shard_map.67.refs_0_
  60.0 2.9 %collective-permute-start.21 = (bf16[272,128]{1,0:T(8,128)(2,1)S(1)}, bf16[272,128]{1,0:T(8,128)(2,1)S(1)}, u32[]{:S(2)}, u32[]{:S(2)}) collective-permute-start(bf16[272,128]{1,0:T(8,128)(2,1)S(1)} %shard_map.67.refs_0_), channel_id=1, source_target_pairs={{0,16},{1,8},{2,11},{3,19},{4,13},{5,21},{6,22},{7,14},{8,1},{9,25... | collective-permute-start | bytes 208904 | tf_op jit(solution)/shard_map/ppermute | solution.py:450
  63.0 3.0 %collective-permute-done.21.refs_1_ = bf16[272,128]{1,0:T(8,128)(2,1)S(1)} collective-permute-done((bf16[272,128]{1,0:T(8,128)(2,1)S(1)}, bf16[272,128]{1,0:T(8,128)(2,1)S(1)}, u32[]{:S(2)}, u32[]{:S(2)}) %collective-permute-start.21) | collective-permute-done | bytes 69664 | tf_op jit(solution)/shard_map/ppermute | solution.py:450
  66.1 4.6 %collective-permute-done.22.refs_1_ = bf16[544,128]{1,0:T(8,128)(2,1)S(1)} collective-permute-done((bf16[544,128]{1,0:T(8,128)(2,1)S(1)}, bf16[544,128]{1,0:T(8,128)(2,1)S(1)}, u32[]{:S(2)}, u32[]{:S(2)}) %collective-permute-start.22) | collective-permute-done | bytes 139296 | tf_op jit(solution)/shard_map/ppermute | solution.py:450
  70.8 0.8 %shard_map.50.refs_1_ = f32[768,512]{1,0:T(8,128)S(1)} custom-call(bf16[1536,512]{1,0:T(8,128)(2,1)S(1)} %get-tuple-element.19.refs_0_, bf16[1536,512]{1,0:T(8,128)(2,1)S(1)} %get-tuple-element.20.refs_1_, bf16[2240,128]{1,0:T(8,128)(2,1)S(1)} %shard_map.49.refs_2_.refs_4_), custom_call_target="tpu_custom_call" | custom-call | tf_op jit(solution)/shard_map/pallas_call | solution.py:29
  71.6 0.8 %shard_map.51.refs_2_ = f32[768,512]{1,0:T(8,128)S(1)} custom-call(bf16[1536,512]{1,0:T(8,128)(2,1)S(1)} %get-tuple-element.19.refs_0_, bf16[1536,512]{1,0:T(8,128)(2,1)S(1)} %get-tuple-element.20.refs_1_, bf16[2240,128]{1,0:T(8,128)(2,1)S(1)} %collective-permute-done.7.refs_2_.refs_7_), custom_call_target="tpu_custom_call" | custom-call | tf_op jit(solution)/shard_map/pallas_call | solution.py:29
  72.5 2.4 %shard_map.70 = (f32[768,512]{1,0:T(8,128)S(1)}, f32[768,512]{1,0:T(8,128)S(1)}) custom-call(bf16[1536,512]{1,0:T(8,128)(2,1)S(1)} %get-tuple-element.19.refs_0_, f32[768,512]{1,0:T(8,128)S(1)} %shard_map.50.refs_1_, f32[768,512]{1,0:T(8,128)S(1)} %shard_map.51.refs_2_, bf16[1856,128]{1,0:T(8,128)(2,1)S(1)} %shard_map.60.refs_3_.refs_5_, ...), custom_call_target="tpu_custom_call" | custom-call | tf_op jit(solution)/shard_map/pallas_call | solution.py:29
  74.9 2.6 %shard_map.71 = (f32[1536,512]{1,0:T(8,128)}, f32[1]{0:T(128)}) custom-call(bf16[1536,512]{1,0:T(8,128)(2,1)S(1)} %get-tuple-element.19.refs_0_, f32[768,512]{1,0:T(8,128)S(1)} %get-tuple-element.34.refs_1_, f32[768,512]{1,0:T(8,128)S(1)} %get-tuple-element.35.refs_2_, bf16[1088,128]{1,0:T(8,128)(2,1)S(1)} %collective-permute-done.23.refs_3_.refs_9_, ...), custom_call_target="tpu_custom_call" | custom-call | tf_op jit(solution)/shard_map/pallas_call | solution.py:29
  (31 shorter events, 1.0 us)
Async XLA Ops:
  3.0 2.5 %collective-permute-start = (bf16[2176,128]{1,0:T(8,128)(2,1)S(1)}, bf16[2176,128]{1,0:T(8,128)(2,1)S(1)}, u32[]{:S(2)}, u32[]{:S(2)}) collective-permute-start(bf16[2176,128]{1,0:T(8,128)(2,1)S(1)} %get-tuple-element.21), channel_id=1, source_target_pairs={{0,1},{1,0},{2,3},{3,2},{4,5},{5,4},{6,7},{7,6},{8,9},{9,8},{10,11... | collective-permute-start | bytes 1671176 | tf_op jit(solution)/shard_map/ppermute | solution.py:450
  4.5 10.9 %collective-permute-start.8 = (bf16[1792,128]{1,0:T(8,128)(2,1)S(1)}, bf16[1792,128]{1,0:T(8,128)(2,1)S(1)}, u32[]{:S(2)}, u32[]{:S(2)}) collective-permute-start(bf16[1792,128]{1,0:T(8,128)(2,1)S(1)} %shard_map.53), channel_id=1, source_target_pairs={{0,1},{1,0},{2,3},{3,2},{4,5},{5,4},{6,7},{7,6},{8,9},{9,8},{10,11... | collective-permute-start | bytes 1376264 | tf_op jit(solution)/shard_map/ppermute | solution.py:450
  5.7 6.9 %collective-permute-start.1 = (bf16[1088,128]{1,0:T(8,128)(2,1)S(1)}, bf16[1088,128]{1,0:T(8,128)(2,1)S(1)}, u32[]{:S(2)}, u32[]{:S(2)}) collective-permute-start(bf16[1088,128]{1,0:T(8,128)(2,1)S(1)} %get-tuple-element.23), channel_id=1, source_target_pairs={{0,5},{1,2},{2,1},{3,6},{4,7},{5,0},{6,3},{7,4},{8,11},{9,12},{10,... | collective-permute-start | bytes 835592 | tf_op jit(solution)/shard_map/ppermute | solution.py:450
  12.6 4.7 %collective-permute-start.2 = (bf16[544,128]{1,0:T(8,128)(2,1)S(1)}, bf16[544,128]{1,0:T(8,128)(2,1)S(1)}, u32[]{:S(2)}, u32[]{:S(2)}) collective-permute-start(bf16[544,128]{1,0:T(8,128)(2,1)S(1)} %get-tuple-element.25), channel_id=1, source_target_pairs={{0,3},{1,4},{2,7},{3,0},{4,1},{5,6},{6,5},{7,2},{8,13},{9,10},{10,... | collective-permute-start | bytes 417800 | tf_op jit(solution)/shard_map/ppermute | solution.py:450
  15.5 5.5 %collective-permute-start.9 = (bf16[896,128]{1,0:T(8,128)(2,1)S(1)}, bf16[896,128]{1,0:T(8,128)(2,1)S(1)}, u32[]{:S(2)}, u32[]{:S(2)}) collective-permute-start(bf16[896,128]{1,0:T(8,128)(2,1)S(1)} %get-tuple-element.27), channel_id=1, source_target_pairs={{0,5},{1,2},{2,1},{3,6},{4,7},{5,0},{6,3},{7,4},{8,11},{9,12},{10,... | collective-permute-start | bytes 688136 | tf_op jit(solution)/shard_map/ppermute | solution.py:450
  17.3 6.1 %collective-permute-start.3 = (bf16[544,128]{1,0:T(8,128)(2,1)S(1)}, bf16[544,128]{1,0:T(8,128)(2,1)S(1)}, u32[]{:S(2)}, u32[]{:S(2)}) collective-permute-start(bf16[544,128]{1,0:T(8,128)(2,1)S(1)} %shard_map.45.a_ref), channel_id=1, source_target_pairs={{0,9},{1,17},{2,18},{3,10},{4,20},{5,12},{6,15},{7,23},{8,24},{9,0... | collective-permute-start | bytes 417800 | tf_op jit(solution)/shard_map/ppermute | solution.py:450
  21.1 6.2 %collective-permute-start.10 = (bf16[448,128]{1,0:T(8,128)(2,1)S(1)}, bf16[448,128]{1,0:T(8,128)(2,1)S(1)}, u32[]{:S(2)}, u32[]{:S(2)}) collective-permute-start(bf16[448,128]{1,0:T(8,128)(2,1)S(1)} %get-tuple-element.29), channel_id=1, source_target_pairs={{0,3},{1,4},{2,7},{3,0},{4,1},{5,6},{6,5},{7,2},{8,13},{9,10},{10,... | collective-permute-start | bytes 344072 | tf_op jit(solution)/shard_map/ppermute | solution.py:450
  23.4 7.6 %collective-permute-start.4 = (bf16[544,128]{1,0:T(8,128)(2,1)S(1)}, bf16[544,128]{1,0:T(8,128)(2,1)S(1)}, u32[]{:S(2)}, u32[]{:S(2)}) collective-permute-start(bf16[544,128]{1,0:T(8,128)(2,1)S(1)} %shard_map.46.refs_0_), channel_id=1, source_target_pairs={{0,16},{1,8},{2,11},{3,19},{4,13},{5,21},{6,22},{7,14},{8,1},{9,25... | collective-permute-start | bytes 417800 | tf_op jit(solution)/shard_map/ppermute | solution.py:450
  26.6 14.4 %collective-permute-start.16 = (bf16[1024,128]{1,0:T(8,128)(2,1)S(1)}, bf16[1024,128]{1,0:T(8,128)(2,1)S(1)}, u32[]{:S(2)}, u32[]{:S(2)}) collective-permute-start(bf16[1024,128]{1,0:T(8,128)(2,1)S(1)} %shard_map.62), channel_id=1, source_target_pairs={{0,1},{1,0},{2,3},{3,2},{4,5},{5,4},{6,7},{7,6},{8,9},{9,8},{10,11... | collective-permute-start | bytes 786440 | tf_op jit(solution)/shard_map/ppermute | solution.py:450
  27.3 6.1 %collective-permute-start.11 = (bf16[448,128]{1,0:T(8,128)(2,1)S(1)}, bf16[448,128]{1,0:T(8,128)(2,1)S(1)}, u32[]{:S(2)}, u32[]{:S(2)}) collective-permute-start(bf16[448,128]{1,0:T(8,128)(2,1)S(1)} %shard_map.56.a_ref), channel_id=1, source_target_pairs={{0,9},{1,17},{2,18},{3,10},{4,20},{5,12},{6,15},{7,23},{8,24},{9,0... | collective-permute-start | bytes 344072 | tf_op jit(solution)/shard_map/ppermute | solution.py:450
  31.4 4.5 %collective-permute-start.5 = (bf16[560,128]{1,0:T(8,128)(2,1)S(1)}, bf16[560,128]{1,0:T(8,128)(2,1)S(1)}, u32[]{:S(2)}, u32[]{:S(2)}) collective-permute-start(bf16[560,128]{1,0:T(8,128)(2,1)S(1)} %shard_map.47.refs_0_), channel_id=1, source_target_pairs={{0,3},{1,4},{2,7},{3,0},{4,1},{5,6},{6,5},{7,2},{8,13},{9,10},{10,... | collective-permute-start | bytes 430088 | tf_op jit(solution)/shard_map/ppermute | solution.py:450
  33.4 6.8 %collective-permute-start.12 = (bf16[448,128]{1,0:T(8,128)(2,1)S(1)}, bf16[448,128]{1,0:T(8,128)(2,1)S(1)}, u32[]{:S(2)}, u32[]{:S(2)}) collective-permute-start(bf16[448,128]{1,0:T(8,128)(2,1)S(1)} %shard_map.57.refs_0_), channel_id=1, source_target_pairs={{0,16},{1,8},{2,11},{3,19},{4,13},{5,21},{6,22},{7,14},{8,1},{9,25... | collective-permute-start | bytes 344072 | tf_op jit(solution)/shard_map/ppermute | solution.py:450
  36.0 17.6 %collective-permute-start.6 = (bf16[1120,128]{1,0:T(8,128)(2,1)S(1)}, bf16[1120,128]{1,0:T(8,128)(2,1)S(1)}, u32[]{:S(2)}, u32[]{:S(2)}) collective-permute-start(bf16[1120,128]{1,0:T(8,128)(2,1)S(1)} %shard_map.48.refs_0_), channel_id=1, source_target_pairs={{0,5},{1,2},{2,1},{3,6},{4,7},{5,0},{6,3},{7,4},{8,11},{9,12},{10,... | collective-permute-start | bytes 860168 | tf_op jit(solution)/shard_map/ppermute | solution.py:450
  40.4 4.3 %collective-permute-start.13 = (bf16[464,128]{1,0:T(8,128)(2,1)S(1)}, bf16[464,128]{1,0:T(8,128)(2,1)S(1)}, u32[]{:S(2)}, u32[]{:S(2)}) collective-permute-start(bf16[464,128]{1,0:T(8,128)(2,1)S(1)} %shard_map.58.refs_0_), channel_id=1, source_target_pairs={{0,3},{1,4},{2,7},{3,0},{4,1},{5,6},{6,5},{7,2},{8,13},{9,10},{10,... | collective-permute-start | bytes 356360 | tf_op jit(solution)/shard_map/ppermute | solution.py:450
  41.1 5.9 %collective-permute-start.17 = (bf16[512,128]{1,0:T(8,128)(2,1)S(1)}, bf16[512,128]{1,0:T(8,128)(2,1)S(1)}, u32[]{:S(2)}, u32[]{:S(2)}) collective-permute-start(bf16[512,128]{1,0:T(8,128)(2,1)S(1)} %get-tuple-element.31), channel_id=1, source_target_pairs={{0,9},{1,17},{2,18},{3,10},{4,20},{5,12},{6,15},{7,23},{8,24},{9,0... | collective-permute-start | bytes 393224 | tf_op jit(solution)/shard_map/ppermute | solution.py:450
  44.7 18.2 %collective-permute-start.14 = (bf16[928,128]{1,0:T(8,128)(2,1)S(1)}, bf16[928,128]{1,0:T(8,128)(2,1)S(1)}, u32[]{:S(2)}, u32[]{:S(2)}) collective-permute-start(bf16[928,128]{1,0:T(8,128)(2,1)S(1)} %shard_map.59.refs_0_), channel_id=1, source_target_pairs={{0,5},{1,2},{2,1},{3,6},{4,7},{5,0},{6,3},{7,4},{8,11},{9,12},{10,... | collective-permute-start | bytes 712712 | tf_op jit(solution)/shard_map/ppermute | solution.py:450
  47.0 5.3 %collective-permute-start.18 = (bf16[256,128]{1,0:T(8,128)(2,1)S(1)}, bf16[256,128]{1,0:T(8,128)(2,1)S(1)}, u32[]{:S(2)}, u32[]{:S(2)}) collective-permute-start(bf16[256,128]{1,0:T(8,128)(2,1)S(1)} %get-tuple-element.33), channel_id=1, source_target_pairs={{0,16},{1,8},{2,11},{3,19},{4,13},{5,21},{6,22},{7,14},{8,1},{9,25... | collective-permute-start | bytes 196616 | tf_op jit(solution)/shard_map/ppermute | solution.py:450
  52.4 3.8 %collective-permute-start.19 = (bf16[256,128]{1,0:T(8,128)(2,1)S(1)}, bf16[256,128]{1,0:T(8,128)(2,1)S(1)}, u32[]{:S(2)}, u32[]{:S(2)}) collective-permute-start(bf16[256,128]{1,0:T(8,128)(2,1)S(1)} %shard_map.65.a_ref), channel_id=1, source_target_pairs={{0,5},{1,2},{2,1},{3,6},{4,7},{5,0},{6,3},{7,4},{8,11},{9,12},{10,... | collective-permute-start | bytes 196616 | tf_op jit(solution)/shard_map/ppermute | solution.py:450
  53.6 18.0 %collective-permute-start.7 = (bf16[2240,128]{1,0:T(8,128)(2,1)S(1)}, bf16[2240,128]{1,0:T(8,128)(2,1)S(1)}, u32[]{:S(2)}, u32[]{:S(2)}) collective-permute-start(bf16[2240,128]{1,0:T(8,128)(2,1)S(1)} %shard_map.49.refs_2_.refs_4_), channel_id=1, source_target_pairs={{0,1},{1,0},{2,3},{3,2},{4,5},{5,4},{6,7},{7,6},{8,9},{9,8},{10,11... | collective-permute-start | bytes 1720328 | tf_op jit(solution)/shard_map/ppermute | solution.py:450
  56.1 3.8 %collective-permute-start.20 = (bf16[256,128]{1,0:T(8,128)(2,1)S(1)}, bf16[256,128]{1,0:T(8,128)(2,1)S(1)}, u32[]{:S(2)}, u32[]{:S(2)}) collective-permute-start(bf16[256,128]{1,0:T(8,128)(2,1)S(1)} %shard_map.66.refs_0_), channel_id=1, source_target_pairs={{0,3},{1,4},{2,7},{3,0},{4,1},{5,6},{6,5},{7,2},{8,13},{9,10},{10,... | collective-permute-start | bytes 196616 | tf_op jit(solution)/shard_map/ppermute | solution.py:450
  60.0 6.0 %collective-permute-start.21 = (bf16[272,128]{1,0:T(8,128)(2,1)S(1)}, bf16[272,128]{1,0:T(8,128)(2,1)S(1)}, u32[]{:S(2)}, u32[]{:S(2)}) collective-permute-start(bf16[272,128]{1,0:T(8,128)(2,1)S(1)} %shard_map.67.refs_0_), channel_id=1, source_target_pairs={{0,16},{1,8},{2,11},{3,19},{4,13},{5,21},{6,22},{7,14},{8,1},{9,25... | collective-permute-start | bytes 208904 | tf_op jit(solution)/shard_map/ppermute | solution.py:450
  63.0 9.5 %collective-permute-start.15 = (bf16[1856,128]{1,0:T(8,128)(2,1)S(1)}, bf16[1856,128]{1,0:T(8,128)(2,1)S(1)}, u32[]{:S(2)}, u32[]{:S(2)}) collective-permute-start(bf16[1856,128]{1,0:T(8,128)(2,1)S(1)} %shard_map.60.refs_3_.refs_5_), channel_id=1, source_target_pairs={{0,1},{1,0},{2,3},{3,2},{4,5},{5,4},{6,7},{7,6},{8,9},{9,8},{10,11... | collective-permute-start | bytes 1425416 | tf_op jit(solution)/shard_map/ppermute | solution.py:450
  66.0 4.7 %collective-permute-start.22 = (bf16[544,128]{1,0:T(8,128)(2,1)S(1)}, bf16[544,128]{1,0:T(8,128)(2,1)S(1)}, u32[]{:S(2)}, u32[]{:S(2)}) collective-permute-start(bf16[544,128]{1,0:T(8,128)(2,1)S(1)} %shard_map.68.refs_0_), channel_id=1, source_target_pairs={{0,9},{1,17},{2,18},{3,10},{4,20},{5,12},{6,15},{7,23},{8,24},{9,0... | collective-permute-start | bytes 417800 | tf_op jit(solution)/shard_map/ppermute | solution.py:450
  70.7 4.2 %collective-permute-start.23 = (bf16[1088,128]{1,0:T(8,128)(2,1)S(1)}, bf16[1088,128]{1,0:T(8,128)(2,1)S(1)}, u32[]{:S(2)}, u32[]{:S(2)}) collective-permute-start(bf16[1088,128]{1,0:T(8,128)(2,1)S(1)} %shard_map.69.refs_5_.refs_6_), channel_id=1, source_target_pairs={{0,1},{1,0},{2,3},{3,2},{4,5},{5,4},{6,7},{7,6},{8,9},{9,8},{10,11... | collective-permute-start | bytes 835592 | tf_op jit(solution)/shard_map/ppermute | solution.py:450

commit v7 on v6

--- a/solution.py
+++ b/solution.py
@@ -9,9 +9,13 @@
 TILE = 128
 PAD = 16
 SHARES = 4
-CUTS = (17 / 39, 31 / 39)
+CUT = 17 / 39
+LATE = (2, 2)
 TURNS = (0, 1, 2)
 FAR_FIRST = 2
+TWO = 1
+PIECE = 128
+PANEL = 2
 AXES = ("gr", "gc")
 BF16 = jnp.bfloat16
 F32 = jnp.float32
@@ -25,13 +29,14 @@
     return pltpu.CompilerParams(vmem_limit_bytes=mib * 2**20)
 
 
-def call(kernel, out, mib, *operands, scratch=(), in_specs=None, out_specs=None):
+def call(kernel, out, mib, *operands, scratch=(), in_specs=None, out_specs=None, aliases={}):
     return pl.pallas_call(
         kernel,
         out_shape=out,
         in_specs=in_specs or [VMEM] * len(operands),
         out_specs=out_specs or jax.tree.map(lambda _: VMEM, out),
         scratch_shapes=scratch,
+        input_output_aliases=aliases,
         compiler_params=params(mib),
     )(*operands)
 
@@ -43,11 +48,14 @@
 
 def chunk_tiles(total_rows):
     side, extra = geometry(total_rows)
-    tiles = [("near", i, j) for j in range(side) for i in range(j + 1)]
-    tiles += [("far", i, j) for j in range(side) for i in range(j + 1, side)]
+    near = [("near", i, j) for j in range(side) for i in range(j + 1)]
+    far = [("far", i, j) for j in range(side) for i in range(j + 1, side)]
+    late = [at for at in near if at[1] >= side - LATE[0] and at[2] == side - 1] + [at for at in far if at[2] >= LATE[1]]
+    tiles = [at for at in near if at not in late]
     tiles += [("extra", k, k) for k in range(extra)]
-    first, second = (round(cut * len(tiles)) for cut in CUTS)
-    return [tiles[:first], tiles[first:second], tiles[second:]]
+    tiles += [at for at in far if at not in late]
+    cut = round(CUT * (len(tiles) + len(late)))
+    return [tiles[:cut], tiles[cut:], late]
 
 
 def parity(r, c):
@@ -135,10 +143,13 @@
             part = pl.ds(pl.multiple_of(at, TILE), rows)
             copies.append(pltpu.make_async_copy(source.at[part], target.at[part], sems.at[len(copies)]))
             copies[-1].start()
-    for copy in copies[:4]:
+    ready = 4 if all(which == "near" for which, _, _ in tiles) else 8
+    if ready == 8 and all(which == "near" or (which == "far" and j * TILE < rows) for which, _, j in tiles):
+        ready = 6
+    for copy in copies[:ready]:
         copy.wait()
     product_kernel(orb_ref, vel_ref, away_ref, flip=1, tiles=tiles, side=side, extra=extra)
-    for copy in copies[4:]:
+    for copy in copies[ready:]:
         copy.wait()
 
 
@@ -266,8 +277,8 @@
 
 def spans_of(table, side):
     spans = {}
-    for p in range(0, side, 2):
-        columns = [j for (i, j) in table if i in (p, p + 1)]
+    for p in range(0, side, PANEL):
+        columns = [j for (i, j) in table if p <= i < p + PANEL]
         if columns:
             spans[p] = (min(columns), max(columns) + 1)
     return spans
@@ -288,7 +299,7 @@
     for name, table in found.items():
         ref = mats[name]
         for p, (begin, end) in spans_of(table, side).items():
-            last = min(p + 2, side)
+            last = min(p + PANEL, side)
             for i in range(p, last):
                 for j in range(begin, end):
                     if table.get((i, j)) is None:
@@ -313,26 +324,27 @@
     return terms
 
 
-def apply_kernel(*refs, plan, given, velocities, count, side, extra, names):
+def apply_kernel(*refs, plan, given, velocities, blocks, final, count, side, extra, names):
     refs = list(refs)
     orb_ref = refs.pop(0)
     vel_ref = refs.pop(0) if velocities else None
     bases = {b: refs.pop(0) for b in given}
     pieces = [refs.pop(0) for _ in plan]
+    squares = [refs.pop(0) for _ in range(count)]
+    if count:
+        refs.pop(0)
+    out_hbm = refs.pop(0) if final else None
+    norm_hbm = refs.pop(0) if count else None
+    outs = {b: refs.pop(0) for b in blocks}
+    sems = refs.pop() if final else None
+    norm_ref = refs.pop() if count else None
     touched = set().union(*(reach(tiles, flip, side) for tiles, flip in plan))
-    last = count > 0
     copies = []
-    if last:
-        squares = [refs.pop(0) for _ in range(count)]
-        out_hbm, norm_ref, scratch, sems = refs.pop(0), refs.pop(0), refs.pop(0), refs.pop()
-        outs = {b: scratch.at[b] for b in (0, 1)}
-    else:
-        outs = {b: refs.pop(0) for b in sorted({b for b, _ in touched})}
     _, low, up = starts(0, side)
     base_row = (low, up)
 
     def rows_of(p):
-        return slice(p * TILE, min(p + 2, side) * TILE)
+        return slice(p * TILE, min(p + PANEL, side) * TILE)
 
     def place(b, p):
         rows = rows_of(p)
@@ -342,42 +354,57 @@
         return bases[b][rows_of(p), :] if b in bases else vel_ref[place(b, p), :].astype(F32)
 
     def send(source, b, p):
-        copy = pltpu.make_async_copy(source.at[rows_of(p)], out_hbm.at[place(b, p)], sems.at[len(copies)])
-        copy.start()
-        copies.append(copy)
-
-    for b in outs:
-        for p in range(0, side, 2):
-            if (b, p) not in touched:
-                if last:
-                    send(bases[b], b, p)
-                else:
-                    outs[b][rows_of(p), :] = before(b, p)
+        rows = rows_of(p)
+        for row in range(rows.start, rows.stop, PIECE):
+            at = pl.ds(pl.multiple_of(base_row[b] + row, PIECE), PIECE)
+            copy = pltpu.make_async_copy(source.at[row : row + PIECE], out_hbm.at[at], sems.at[len(copies)])
+            copy.start()
+            copies.append(copy)
+
+    if count:
+        square = tails(squares[: count // 2]) + tails(squares[count // 2 :])
+        norm_ref[0] = (jnp.sqrt(square) / (2 * side * TILE))[0, 0]
+        copies.append(pltpu.make_async_copy(norm_ref, norm_hbm, sems.at[0]))
+        copies[0].start()
+    for b, p in sorted(final - touched):
+        if b in bases:
+            send(bases[b], b, p)
+        else:
+            outs[b][rows_of(p), :] = before(b, p)
+            send(outs[b], b, p)
+    for b in () if count else blocks:
+        for p in range(0, side, PANEL):
+            if (b, p) not in touched | final:
+                outs[b][rows_of(p), :] = before(b, p)
     terms = {}
     for (tiles, flip), piece, own in zip(plan, pieces, names):
         mats = {name: refs.pop(0) for name in own}
         for key, value in fill(piece, tiles, flip, mats, side, extra).items():
             terms.setdefault(key, []).extend(value)
-    for b, p in sorted(touched):
+    for b, p in sorted(touched, key=lambda key: (key not in final, key)):
         total = None
         for ref, left, at, rows in terms[(b, p)]:
             right = orb_ref[pl.ds(pl.multiple_of(at, TILE), rows), :]
             value = jnp.dot(ref[left], right, preferred_element_type=F32)
             total = value if total is None else total + value
         outs[b][rows_of(p), :] = before(b, p) - 0.5 * total
-        if last:
+        if (b, p) in final:
             send(outs[b], b, p)
-    if last:
-        square = tails(squares[: count // 2]) + tails(squares[count // 2 :])
-        norm_ref[0] = (jnp.sqrt(square) / (2 * side * TILE))[0, 0]
-        for copy in copies:
-            copy.wait()
-
-
-def apply(orb, vel, bases, plan, pieces, squares=()):
+    for copy in copies:
+        copy.wait()
+
+
+def apply(orb, vel, bases, plan, pieces, later=None, squares=(), out=None):
     side, extra = geometry(orb.shape[0])
     wide, columns = side * TILE, orb.shape[1]
-    blocks = [0, 1] if squares else sorted({b for tiles, flip in plan for b, _ in reach(tiles, flip, side)})
+    touched = set().union(*(reach(tiles, flip, side) for tiles, flip in plan))
+    final = set()
+    if later is not None:
+        kept = set().union(*(reach(tiles, flip, side) for tiles, flip in later))
+        final = {(b, p) for b in (0, 1) for p in range(0, side, PANEL)} - kept
+    if squares:
+        final = touched
+    blocks = [0, 1] if later is not None else sorted({b for b, _ in touched})
     given = [b for b in blocks if bases[b] is not None]
     velocities = len(given) < len(blocks)
     names = [list(tables(tiles, side)) for tiles, _ in plan]
@@ -387,27 +414,39 @@
         plan=plan,
         given=given,
         velocities=velocities,
+        blocks=blocks,
+        final=final,
         count=len(squares),
         side=side,
         extra=extra,
         names=names,
     )
     operands = [orb] + ([vel] if velocities else []) + [bases[b] for b in given] + list(pieces) + list(squares)
+    block = jax.ShapeDtypeStruct((wide, columns), F32)
+    whole = jax.ShapeDtypeStruct(orb.shape, F32)
+    sems = [pltpu.SemaphoreType.DMA((len(final) * PANEL * TILE // PIECE + 1,))] if final else []
+    mib = 8 + 2 * len(mats)
     if squares:
         return call(
             kernel,
-            [jax.ShapeDtypeStruct(orb.shape, F32), jax.ShapeDtypeStruct((1,), F32)],
-            14,
+            [whole, jax.ShapeDtypeStruct((1,), F32)],
+            mib,
             *operands,
-            scratch=[pltpu.VMEM((2, wide, columns), F32)] + mats + [pltpu.SemaphoreType.DMA((2 * -(-side // 2),))],
-            out_specs=[HBM, SMEM],
+            out,
+            scratch=[pltpu.VMEM((wide, columns), F32) for _ in blocks] + mats + [pltpu.SMEM((1,), F32)] + sems,
+            in_specs=[VMEM] * len(operands) + [HBM],
+            out_specs=[HBM, HBM],
+            aliases={len(operands): 0},
         )
-    out = [jax.ShapeDtypeStruct((wide, columns), F32)] * len(blocks)
-    values = call(kernel, out, 8 + 2 * len(mats), *operands, scratch=mats)
+    shapes, specs = [block] * len(blocks), [VMEM] * len(blocks)
+    if final:
+        shapes, specs = [whole] + shapes, [HBM] + specs
+    values = list(call(kernel, shapes, mib, *operands, scratch=mats + sems, out_specs=specs))
+    out = values.pop(0) if final else None
     result = list(bases)
     for b, value in zip(blocks, values):
         result[b] = value
-    return result
+    return (result, out) if later is not None else result
 
 
 def permutation(nr, nc, pair):
@@ -436,7 +475,6 @@
 
 def local(orbitals, velocities):
     nr, nc = lax.axis_size("gr"), lax.axis_size("gc")
-    _, _ = geometry(orbitals.shape[0])
     chunks = chunk_tiles(orbitals.shape[0])
     plans = routes(nr, nc)
     swap = [(d, d ^ 1) for d in range(nr * nc)]
@@ -470,11 +508,14 @@
     first, second, third = TURNS
     blocks = [None, None]
     blocks = apply(orbitals, velocities, blocks, [(chunks[first], 0)], [joined[first]])
-    blocks = apply(orbitals, velocities, blocks, [(chunks[first], 1)], [far[first]])
-    plan = [(chunks[second], 0), (chunks[second], 1), (chunks[third], 0)]
-    blocks = apply(orbitals, velocities, blocks, plan, [joined[second], far[second], joined[third]])
+    plan = [(chunks[first], 1)] + [(chunks[second], 0)] * TWO
+    blocks = apply(orbitals, velocities, blocks, plan, [far[first]] + [joined[second]] * TWO)
+    plan = [(chunks[second], 1), (chunks[third], 0)] + [(chunks[second], 0)] * (1 - TWO)
+    pieces = [far[second], joined[third]] + [joined[second]] * (1 - TWO)
+    later = [(chunks[third], 1)]
+    blocks, out = apply(orbitals, velocities, blocks, plan, pieces, later)
     squares = [joined[k] for k in TURNS] + [far[k] for k in TURNS]
-    return tuple(apply(orbitals, velocities, blocks, [(chunks[third], 1)], [far[third]], squares))
+    return tuple(apply(orbitals, velocities, blocks, later, [far[third]], None, squares, out))
 
 
 def solution(mesh):

time: 77.7 us -> 77.4 us (level)
  transfers between devices with their start and end apart: 24 -> 24, of which waited for: 15 -> 15; matrix products, arithmetic and copies ran while one was open for 0% -> 0% of each run, Pallas kernels for 12% -> 13%
where the time goes in v7:
time: 77.4 us; the launch traced here: 77.3 us
  waiting for transfers between devices  33.6 us (43%)
  starting transfers between devices  28.6 us (37%)
  Pallas kernels  14.3 us (18%)
  between operations  0.87 us (1%)
    ppermute x24, waiting for transfers between devices, move(): lax.ppermute(value, AXES, swap if pair is None else permutation(nr, nc, p...  33.6 us
    ppermute x24, starting transfers between devices, move(): lax.ppermute(value, AXES, swap if pair is None else permutation(nr, nc, p...  28.6 us
    pallas_call x31, Pallas kernels, call(): pl.pallas_call(kernel, out_shape=out, in_specs=in_specs or [VMEM] * len(o...  14.3 us
  transfers between devices with their start and end apart: 24, of which 15 were waited for; matrix products, arithmetic and copies ran while one was open for 0% of the time, Pallas kernels for 13%

profile of v7, /device:TPU:0, one launch (start us, length us, event | category | flops | bytes accessed | tf_op | source)
XLA Modules:
  0.0 77.3 jit_solution(6683978711686200870)
XLA Ops:
  0.6 2.4 %shard_map.41 = (bf16[2176,128]{1,0:T(8,128)(2,1)S(1)}, bf16[1536,512]{1,0:T(8,128)(2,1)S(1)}, bf16[1536,512]{1,0:T(8,128)(2,1)S(1)}) custom-call(bf16[1536,512]{1,0:T(8,128)(2,1)} %refs_0_.1, bf16[1536,512]{1,0:T(8,128)(2,1)} %refs_1_.1), custom_call_target="tpu_custom_call" | custom-call | tf_op jit(solution)/shard_map/pallas_call | solution.py:33
  3.0 0.6 collective-permute-start
  3.6 0.9 %shard_map.52 = bf16[1792,128]{1,0:T(8,128)(2,1)S(1)} custom-call(bf16[1536,512]{1,0:T(8,128)(2,1)S(1)} %get-tuple-element.22.refs_0_, bf16[1536,512]{1,0:T(8,128)(2,1)S(1)} %get-tuple-element.23.refs_1_), custom_call_target="tpu_custom_call" | custom-call | tf_op jit(solution)/shard_map/pallas_call | solution.py:33
  4.6 0.9 %shard_map.42.refs_0_ = bf16[2176,128]{1,0:T(8,128)(2,1)S(1)} custom-call(bf16[1536,512]{1,0:T(8,128)(2,1)S(1)} %get-tuple-element.22.refs_0_, bf16[1536,512]{1,0:T(8,128)(2,1)S(1)} %get-tuple-element.23.refs_1_), custom_call_target="tpu_custom_call" | custom-call | tf_op jit(solution)/shard_map/pallas_call | solution.py:33
  5.5 0.1 shard_map.43
  5.7 2.7 %collective-permute-start.1 = (bf16[1088,128]{1,0:T(8,128)(2,1)S(1)}, bf16[1088,128]{1,0:T(8,128)(2,1)S(1)}, u32[]{:S(2)}, u32[]{:S(2)}) collective-permute-start(bf16[1088,128]{1,0:T(8,128)(2,1)S(1)} %get-tuple-element.26), channel_id=1, source_target_pairs={{0,5},{1,2},{2,1},{3,6},{4,7},{5,0},{6,3},{7,4},{8,11},{9,12},{10,... | collective-permute-start | bytes 835592 | tf_op jit(solution)/shard_map/ppermute | solution.py:488
  8.3 4.2 %collective-permute-done.1.refs_1_ = bf16[1088,128]{1,0:T(8,128)(2,1)S(1)} collective-permute-done((bf16[1088,128]{1,0:T(8,128)(2,1)S(1)}, bf16[1088,128]{1,0:T(8,128)(2,1)S(1)}, u32[]{:S(2)}, u32[]{:S(2)}) %collective-permute-start.1) | collective-permute-done | bytes 278560 | tf_op jit(solution)/shard_map/ppermute | solution.py:488
  12.6 1.9 %collective-permute-start.2 = (bf16[544,128]{1,0:T(8,128)(2,1)S(1)}, bf16[544,128]{1,0:T(8,128)(2,1)S(1)}, u32[]{:S(2)}, u32[]{:S(2)}) collective-permute-start(bf16[544,128]{1,0:T(8,128)(2,1)S(1)} %get-tuple-element.28), channel_id=1, source_target_pairs={{0,3},{1,4},{2,7},{3,0},{4,1},{5,6},{6,5},{7,2},{8,13},{9,10},{10,... | collective-permute-start | bytes 417800 | tf_op jit(solution)/shard_map/ppermute | solution.py:488
  14.5 0.9 %shard_map.51.refs_0_ = bf16[1792,128]{1,0:T(8,128)(2,1)S(1)} custom-call(bf16[1536,512]{1,0:T(8,128)(2,1)S(1)} %get-tuple-element.22.refs_0_, bf16[1536,512]{1,0:T(8,128)(2,1)S(1)} %get-tuple-element.23.refs_1_), custom_call_target="tpu_custom_call" | custom-call | tf_op jit(solution)/shard_map/pallas_call | solution.py:33
  15.4 0.1 shard_map.53
  15.5 1.6 %collective-permute-start.9 = (bf16[896,128]{1,0:T(8,128)(2,1)S(1)}, bf16[896,128]{1,0:T(8,128)(2,1)S(1)}, u32[]{:S(2)}, u32[]{:S(2)}) collective-permute-start(bf16[896,128]{1,0:T(8,128)(2,1)S(1)} %get-tuple-element.30), channel_id=1, source_target_pairs={{0,5},{1,2},{2,1},{3,6},{4,7},{5,0},{6,3},{7,4},{8,11},{9,12},{10,... | collective-permute-start | bytes 688136 | tf_op jit(solution)/shard_map/ppermute | solution.py:488
  17.1 0.2 collective-permute-done.2.b_ref
  17.3 1.9 %collective-permute-start.3 = (bf16[544,128]{1,0:T(8,128)(2,1)S(1)}, bf16[544,128]{1,0:T(8,128)(2,1)S(1)}, u32[]{:S(2)}, u32[]{:S(2)}) collective-permute-start(bf16[544,128]{1,0:T(8,128)(2,1)S(1)} %shard_map.45.a_ref), channel_id=1, source_target_pairs={{0,9},{1,17},{2,18},{3,10},{4,20},{5,12},{6,15},{7,23},{8,24},{9,0... | collective-permute-start | bytes 417800 | tf_op jit(solution)/shard_map/ppermute | solution.py:488
  19.2 1.9 %collective-permute-done.9.refs_1_ = bf16[896,128]{1,0:T(8,128)(2,1)S(1)} collective-permute-done((bf16[896,128]{1,0:T(8,128)(2,1)S(1)}, bf16[896,128]{1,0:T(8,128)(2,1)S(1)}, u32[]{:S(2)}, u32[]{:S(2)}) %collective-permute-start.9) | collective-permute-done | bytes 229408 | tf_op jit(solution)/shard_map/ppermute | solution.py:488
  21.1 0.5 collective-permute-start.10
  21.6 1.8 %collective-permute-done.3.b_ref = bf16[544,128]{1,0:T(8,128)(2,1)S(1)} collective-permute-done((bf16[544,128]{1,0:T(8,128)(2,1)S(1)}, bf16[544,128]{1,0:T(8,128)(2,1)S(1)}, u32[]{:S(2)}, u32[]{:S(2)}) %collective-permute-start.3) | collective-permute-done | bytes 139296 | tf_op jit(solution)/shard_map/ppermute | solution.py:488
  23.4 2.6 %collective-permute-start.4 = (bf16[544,128]{1,0:T(8,128)(2,1)S(1)}, bf16[544,128]{1,0:T(8,128)(2,1)S(1)}, u32[]{:S(2)}, u32[]{:S(2)}) collective-permute-start(bf16[544,128]{1,0:T(8,128)(2,1)S(1)} %shard_map.46.refs_0_), channel_id=1, source_target_pairs={{0,16},{1,8},{2,11},{3,19},{4,13},{5,21},{6,22},{7,14},{8,1},{9,25... | collective-permute-start | bytes 417800 | tf_op jit(solution)/shard_map/ppermute | solution.py:488
  26.1 0.6 shard_map.62
  26.6 0.6 collective-permute-start.16
  27.3 0.1 collective-permute-start.11
  27.4 3.6 %collective-permute-done.4.refs_1_ = bf16[544,128]{1,0:T(8,128)(2,1)S(1)} collective-permute-done((bf16[544,128]{1,0:T(8,128)(2,1)S(1)}, bf16[544,128]{1,0:T(8,128)(2,1)S(1)}, u32[]{:S(2)}, u32[]{:S(2)}) %collective-permute-start.4) | collective-permute-done | bytes 139296 | tf_op jit(solution)/shard_map/ppermute | solution.py:488
  31.0 0.4 shard_map.47.refs_0_
  31.4 0.5 collective-permute-start.5
  31.9 1.5 %collective-permute-done.11.b_ref = bf16[448,128]{1,0:T(8,128)(2,1)S(1)} collective-permute-done((bf16[448,128]{1,0:T(8,128)(2,1)S(1)}, bf16[448,128]{1,0:T(8,128)(2,1)S(1)}, u32[]{:S(2)}, u32[]{:S(2)}) %collective-permute-start.11) | collective-permute-done | bytes 114720 | tf_op jit(solution)/shard_map/ppermute | solution.py:488
  33.4 1.4 %collective-permute-start.12 = (bf16[448,128]{1,0:T(8,128)(2,1)S(1)}, bf16[448,128]{1,0:T(8,128)(2,1)S(1)}, u32[]{:S(2)}, u32[]{:S(2)}) collective-permute-start(bf16[448,128]{1,0:T(8,128)(2,1)S(1)} %shard_map.56.refs_0_), channel_id=1, source_target_pairs={{0,16},{1,8},{2,11},{3,19},{4,13},{5,21},{6,22},{7,14},{8,1},{9,25... | collective-permute-start | bytes 344072 | tf_op jit(solution)/shard_map/ppermute | solution.py:488
  34.8 1.1 %collective-permute-done.5.refs_1_ = bf16[560,128]{1,0:T(8,128)(2,1)S(1)} collective-permute-done((bf16[560,128]{1,0:T(8,128)(2,1)S(1)}, bf16[560,128]{1,0:T(8,128)(2,1)S(1)}, u32[]{:S(2)}, u32[]{:S(2)}) %collective-permute-start.5) | collective-permute-done | bytes 143392 | tf_op jit(solution)/shard_map/ppermute | solution.py:488
  36.0 2.2 %collective-permute-start.6 = (bf16[1120,128]{1,0:T(8,128)(2,1)S(1)}, bf16[1120,128]{1,0:T(8,128)(2,1)S(1)}, u32[]{:S(2)}, u32[]{:S(2)}) collective-permute-start(bf16[1120,128]{1,0:T(8,128)(2,1)S(1)} %shard_map.48.refs_0_), channel_id=1, source_target_pairs={{0,5},{1,2},{2,1},{3,6},{4,7},{5,0},{6,3},{7,4},{8,11},{9,12},{10,... | collective-permute-start | bytes 860168 | tf_op jit(solution)/shard_map/ppermute | solution.py:488
  38.1 2.0 %collective-permute-done.12.refs_1_ = bf16[448,128]{1,0:T(8,128)(2,1)S(1)} collective-permute-done((bf16[448,128]{1,0:T(8,128)(2,1)S(1)}, bf16[448,128]{1,0:T(8,128)(2,1)S(1)}, u32[]{:S(2)}, u32[]{:S(2)}) %collective-permute-start.12) | collective-permute-done | bytes 114720 | tf_op jit(solution)/shard_map/ppermute | solution.py:488
  40.2 0.2 shard_map.57.refs_0_
  40.4 0.6 shard_map.61.refs_0_
  41.1 1.4 %collective-permute-start.17 = (bf16[512,128]{1,0:T(8,128)(2,1)S(1)}, bf16[512,128]{1,0:T(8,128)(2,1)S(1)}, u32[]{:S(2)}, u32[]{:S(2)}) collective-permute-start(bf16[512,128]{1,0:T(8,128)(2,1)S(1)} %get-tuple-element.36), channel_id=1, source_target_pairs={{0,9},{1,17},{2,18},{3,10},{4,20},{5,12},{6,15},{7,23},{8,24},{9,0... | collective-permute-start | bytes 393224 | tf_op jit(solution)/shard_map/ppermute | solution.py:488
  42.5 2.1 %collective-permute-done.13.refs_1_ = bf16[464,128]{1,0:T(8,128)(2,1)S(1)} collective-permute-done((bf16[464,128]{1,0:T(8,128)(2,1)S(1)}, bf16[464,128]{1,0:T(8,128)(2,1)S(1)}, u32[]{:S(2)}, u32[]{:S(2)}) %collective-permute-start.13) | collective-permute-done | bytes 118816 | tf_op jit(solution)/shard_map/ppermute | solution.py:488
  44.7 1.9 %collective-permute-start.14 = (bf16[928,128]{1,0:T(8,128)(2,1)S(1)}, bf16[928,128]{1,0:T(8,128)(2,1)S(1)}, u32[]{:S(2)}, u32[]{:S(2)}) collective-permute-start(bf16[928,128]{1,0:T(8,128)(2,1)S(1)} %shard_map.58.refs_0_), channel_id=1, source_target_pairs={{0,5},{1,2},{2,1},{3,6},{4,7},{5,0},{6,3},{7,4},{8,11},{9,12},{10,... | collective-permute-start | bytes 712712 | tf_op jit(solution)/shard_map/ppermute | solution.py:488
  46.6 0.4 collective-permute-done.17.refs_1_
  47.0 2.7 %collective-permute-start.18 = (bf16[256,128]{1,0:T(8,128)(2,1)S(1)}, bf16[256,128]{1,0:T(8,128)(2,1)S(1)}, u32[]{:S(2)}, u32[]{:S(2)}) collective-permute-start(bf16[256,128]{1,0:T(8,128)(2,1)S(1)} %get-tuple-element.38), channel_id=1, source_target_pairs={{0,16},{1,8},{2,11},{3,19},{4,13},{5,21},{6,22},{7,14},{8,1},{9,25... | collective-permute-start | bytes 196616 | tf_op jit(solution)/shard_map/ppermute | solution.py:488
  49.6 2.6 %collective-permute-done.18.b_ref = bf16[256,128]{1,0:T(8,128)(2,1)S(1)} collective-permute-done((bf16[256,128]{1,0:T(8,128)(2,1)S(1)}, bf16[256,128]{1,0:T(8,128)(2,1)S(1)}, u32[]{:S(2)}, u32[]{:S(2)}) %collective-permute-start.18) | collective-permute-done | bytes 65568 | tf_op jit(solution)/shard_map/ppermute | solution.py:488
  52.3 1.2 %collective-permute-start.19 = (bf16[256,128]{1,0:T(8,128)(2,1)S(1)}, bf16[256,128]{1,0:T(8,128)(2,1)S(1)}, u32[]{:S(2)}, u32[]{:S(2)}) collective-permute-start(bf16[256,128]{1,0:T(8,128)(2,1)S(1)} %shard_map.65.a_ref), channel_id=1, source_target_pairs={{0,5},{1,2},{2,1},{3,6},{4,7},{5,0},{6,3},{7,4},{8,11},{9,12},{10,... | collective-permute-start | bytes 196616 | tf_op jit(solution)/shard_map/ppermute | solution.py:488
  53.7 2.4 %collective-permute-done.19.b_ref = bf16[256,128]{1,0:T(8,128)(2,1)S(1)} collective-permute-done((bf16[256,128]{1,0:T(8,128)(2,1)S(1)}, bf16[256,128]{1,0:T(8,128)(2,1)S(1)}, u32[]{:S(2)}, u32[]{:S(2)}) %collective-permute-start.19) | collective-permute-done | bytes 65568 | tf_op jit(solution)/shard_map/ppermute | solution.py:488
  56.1 1.5 %collective-permute-start.20 = (bf16[256,128]{1,0:T(8,128)(2,1)S(1)}, bf16[256,128]{1,0:T(8,128)(2,1)S(1)}, u32[]{:S(2)}, u32[]{:S(2)}) collective-permute-start(bf16[256,128]{1,0:T(8,128)(2,1)S(1)} %shard_map.66.refs_0_), channel_id=1, source_target_pairs={{0,3},{1,4},{2,7},{3,0},{4,1},{5,6},{6,5},{7,2},{8,13},{9,10},{10,... | collective-permute-start | bytes 196616 | tf_op jit(solution)/shard_map/ppermute | solution.py:488
  57.6 2.2 %collective-permute-done.20.refs_1_ = bf16[256,128]{1,0:T(8,128)(2,1)S(1)} collective-permute-done((bf16[256,128]{1,0:T(8,128)(2,1)S(1)}, bf16[256,128]{1,0:T(8,128)(2,1)S(1)}, u32[]{:S(2)}, u32[]{:S(2)}) %collective-permute-start.20) | collective-permute-done | bytes 65568 | tf_op jit(solution)/shard_map/ppermute | solution.py:488
  59.8 0.1 shard_map.67.refs_0_
  60.0 2.9 %collective-permute-start.21 = (bf16[272,128]{1,0:T(8,128)(2,1)S(1)}, bf16[272,128]{1,0:T(8,128)(2,1)S(1)}, u32[]{:S(2)}, u32[]{:S(2)}) collective-permute-start(bf16[272,128]{1,0:T(8,128)(2,1)S(1)} %shard_map.67.refs_0_), channel_id=1, source_target_pairs={{0,16},{1,8},{2,11},{3,19},{4,13},{5,21},{6,22},{7,14},{8,1},{9,25... | collective-permute-start | bytes 208904 | tf_op jit(solution)/shard_map/ppermute | solution.py:488
  63.0 2.9 %collective-permute-done.21.refs_1_ = bf16[272,128]{1,0:T(8,128)(2,1)S(1)} collective-permute-done((bf16[272,128]{1,0:T(8,128)(2,1)S(1)}, bf16[272,128]{1,0:T(8,128)(2,1)S(1)}, u32[]{:S(2)}, u32[]{:S(2)}) %collective-permute-start.21) | collective-permute-done | bytes 69664 | tf_op jit(solution)/shard_map/ppermute | solution.py:488
  66.1 4.6 %collective-permute-done.22.refs_1_ = bf16[544,128]{1,0:T(8,128)(2,1)S(1)} collective-permute-done((bf16[544,128]{1,0:T(8,128)(2,1)S(1)}, bf16[544,128]{1,0:T(8,128)(2,1)S(1)}, u32[]{:S(2)}, u32[]{:S(2)}) %collective-permute-start.22) | collective-permute-done | bytes 139296 | tf_op jit(solution)/shard_map/ppermute | solution.py:488
  70.8 0.8 %shard_map.50.refs_2_ = f32[768,512]{1,0:T(8,128)S(1)} custom-call(bf16[1536,512]{1,0:T(8,128)(2,1)S(1)} %get-tuple-element.22.refs_0_, bf16[1536,512]{1,0:T(8,128)(2,1)S(1)} %get-tuple-element.23.refs_1_, bf16[2240,128]{1,0:T(8,128)(2,1)S(1)} %shard_map.49.refs_2_.refs_4_), custom_call_target="tpu_custom_call" | custom-call | tf_op jit(solution)/shard_map/pallas_call | solution.py:33
  71.6 1.9 %shard_map.60 = (f32[768,512]{1,0:T(8,128)S(1)}, f32[768,512]{1,0:T(8,128)S(1)}) custom-call(bf16[1536,512]{1,0:T(8,128)(2,1)S(1)} %get-tuple-element.22.refs_0_, bf16[1536,512]{1,0:T(8,128)(2,1)S(1)} %get-tuple-element.23.refs_1_, f32[768,512]{1,0:T(8,128)S(1)} %shard_map.50.refs_2_, bf16[2240,128]{1,0:T(8,128)(2,1)S(1)} %collective-permute-done.7.refs_3_.refs_7_, ...), custom_call_target="tpu_custom_call" | custom-call | tf_op jit(solution)/shard_map/pallas_call | solution.py:33
  73.5 2.0 %shard_map.70 = (f32[1536,512]{1,0:T(8,128)}, f32[768,512]{1,0:T(8,128)S(1)}, f32[768,512]{1,0:T(8,128)S(1)}) custom-call(bf16[1536,512]{1,0:T(8,128)(2,1)S(1)} %get-tuple-element.22.refs_0_, f32[768,512]{1,0:T(8,128)S(1)} %get-tuple-element.33.refs_1_, f32[768,512]{1,0:T(8,128)S(1)} %get-tuple-element.34.refs_2_, ...), custom_call_target="tpu_custom_call" | custom-call | tf_op jit(solution)/shard_map/pallas_call | solution.py:33
  75.6 1.7 %shard_map.71 = (f32[1536,512]{1,0:T(8,128)}, f32[1]{0:T(128)}) custom-call(bf16[1536,512]{1,0:T(8,128)(2,1)S(1)} %get-tuple-element.22.refs_0_, f32[768,512]{1,0:T(8,128)S(1)} %get-tuple-element.39.refs_1_, f32[768,512]{1,0:T(8,128)S(1)} %get-tuple-element.40.refs_2_, ...), custom_call_target="tpu_custom_call", output_to_operand_aliasing={{0}: (10, {})} | custom-call | tf_op jit(solution)/shard_map/pallas_call | solution.py:33
  (31 shorter events, 1.0 us)
Async XLA Ops:
  3.0 2.5 %collective-permute-start = (bf16[2176,128]{1,0:T(8,128)(2,1)S(1)}, bf16[2176,128]{1,0:T(8,128)(2,1)S(1)}, u32[]{:S(2)}, u32[]{:S(2)}) collective-permute-start(bf16[2176,128]{1,0:T(8,128)(2,1)S(1)} %get-tuple-element.24), channel_id=1, source_target_pairs={{0,1},{1,0},{2,3},{3,2},{4,5},{5,4},{6,7},{7,6},{8,9},{9,8},{10,11... | collective-permute-start | bytes 1671176 | tf_op jit(solution)/shard_map/ppermute | solution.py:488
  4.5 10.9 %collective-permute-start.8 = (bf16[1792,128]{1,0:T(8,128)(2,1)S(1)}, bf16[1792,128]{1,0:T(8,128)(2,1)S(1)}, u32[]{:S(2)}, u32[]{:S(2)}) collective-permute-start(bf16[1792,128]{1,0:T(8,128)(2,1)S(1)} %shard_map.52), channel_id=1, source_target_pairs={{0,1},{1,0},{2,3},{3,2},{4,5},{5,4},{6,7},{7,6},{8,9},{9,8},{10,11... | collective-permute-start | bytes 1376264 | tf_op jit(solution)/shard_map/ppermute | solution.py:488
  5.7 6.9 %collective-permute-start.1 = (bf16[1088,128]{1,0:T(8,128)(2,1)S(1)}, bf16[1088,128]{1,0:T(8,128)(2,1)S(1)}, u32[]{:S(2)}, u32[]{:S(2)}) collective-permute-start(bf16[1088,128]{1,0:T(8,128)(2,1)S(1)} %get-tuple-element.26), channel_id=1, source_target_pairs={{0,5},{1,2},{2,1},{3,6},{4,7},{5,0},{6,3},{7,4},{8,11},{9,12},{10,... | collective-permute-start | bytes 835592 | tf_op jit(solution)/shard_map/ppermute | solution.py:488
  12.6 4.7 %collective-permute-start.2 = (bf16[544,128]{1,0:T(8,128)(2,1)S(1)}, bf16[544,128]{1,0:T(8,128)(2,1)S(1)}, u32[]{:S(2)}, u32[]{:S(2)}) collective-permute-start(bf16[544,128]{1,0:T(8,128)(2,1)S(1)} %get-tuple-element.28), channel_id=1, source_target_pairs={{0,3},{1,4},{2,7},{3,0},{4,1},{5,6},{6,5},{7,2},{8,13},{9,10},{10,... | collective-permute-start | bytes 417800 | tf_op jit(solution)/shard_map/ppermute | solution.py:488
  15.5 5.5 %collective-permute-start.9 = (bf16[896,128]{1,0:T(8,128)(2,1)S(1)}, bf16[896,128]{1,0:T(8,128)(2,1)S(1)}, u32[]{:S(2)}, u32[]{:S(2)}) collective-permute-start(bf16[896,128]{1,0:T(8,128)(2,1)S(1)} %get-tuple-element.30), channel_id=1, source_target_pairs={{0,5},{1,2},{2,1},{3,6},{4,7},{5,0},{6,3},{7,4},{8,11},{9,12},{10,... | collective-permute-start | bytes 688136 | tf_op jit(solution)/shard_map/ppermute | solution.py:488
  17.3 6.1 %collective-permute-start.3 = (bf16[544,128]{1,0:T(8,128)(2,1)S(1)}, bf16[544,128]{1,0:T(8,128)(2,1)S(1)}, u32[]{:S(2)}, u32[]{:S(2)}) collective-permute-start(bf16[544,128]{1,0:T(8,128)(2,1)S(1)} %shard_map.45.a_ref), channel_id=1, source_target_pairs={{0,9},{1,17},{2,18},{3,10},{4,20},{5,12},{6,15},{7,23},{8,24},{9,0... | collective-permute-start | bytes 417800 | tf_op jit(solution)/shard_map/ppermute | solution.py:488
  21.1 6.2 %collective-permute-start.10 = (bf16[448,128]{1,0:T(8,128)(2,1)S(1)}, bf16[448,128]{1,0:T(8,128)(2,1)S(1)}, u32[]{:S(2)}, u32[]{:S(2)}) collective-permute-start(bf16[448,128]{1,0:T(8,128)(2,1)S(1)} %get-tuple-element.32), channel_id=1, source_target_pairs={{0,3},{1,4},{2,7},{3,0},{4,1},{5,6},{6,5},{7,2},{8,13},{9,10},{10,... | collective-permute-start | bytes 344072 | tf_op jit(solution)/shard_map/ppermute | solution.py:488
  23.4 7.6 %collective-permute-start.4 = (bf16[544,128]{1,0:T(8,128)(2,1)S(1)}, bf16[544,128]{1,0:T(8,128)(2,1)S(1)}, u32[]{:S(2)}, u32[]{:S(2)}) collective-permute-start(bf16[544,128]{1,0:T(8,128)(2,1)S(1)} %shard_map.46.refs_0_), channel_id=1, source_target_pairs={{0,16},{1,8},{2,11},{3,19},{4,13},{5,21},{6,22},{7,14},{8,1},{9,25... | collective-permute-start | bytes 417800 | tf_op jit(solution)/shard_map/ppermute | solution.py:488
  26.6 14.3 %collective-permute-start.16 = (bf16[1024,128]{1,0:T(8,128)(2,1)S(1)}, bf16[1024,128]{1,0:T(8,128)(2,1)S(1)}, u32[]{:S(2)}, u32[]{:S(2)}) collective-permute-start(bf16[1024,128]{1,0:T(8,128)(2,1)S(1)} %shard_map.62), channel_id=1, source_target_pairs={{0,1},{1,0},{2,3},{3,2},{4,5},{5,4},{6,7},{7,6},{8,9},{9,8},{10,11... | collective-permute-start | bytes 786440 | tf_op jit(solution)/shard_map/ppermute | solution.py:488
  27.3 6.1 %collective-permute-start.11 = (bf16[448,128]{1,0:T(8,128)(2,1)S(1)}, bf16[448,128]{1,0:T(8,128)(2,1)S(1)}, u32[]{:S(2)}, u32[]{:S(2)}) collective-permute-start(bf16[448,128]{1,0:T(8,128)(2,1)S(1)} %shard_map.55.a_ref), channel_id=1, source_target_pairs={{0,9},{1,17},{2,18},{3,10},{4,20},{5,12},{6,15},{7,23},{8,24},{9,0... | collective-permute-start | bytes 344072 | tf_op jit(solution)/shard_map/ppermute | solution.py:488
  31.4 4.5 %collective-permute-start.5 = (bf16[560,128]{1,0:T(8,128)(2,1)S(1)}, bf16[560,128]{1,0:T(8,128)(2,1)S(1)}, u32[]{:S(2)}, u32[]{:S(2)}) collective-permute-start(bf16[560,128]{1,0:T(8,128)(2,1)S(1)} %shard_map.47.refs_0_), channel_id=1, source_target_pairs={{0,3},{1,4},{2,7},{3,0},{4,1},{5,6},{6,5},{7,2},{8,13},{9,10},{10,... | collective-permute-start | bytes 430088 | tf_op jit(solution)/shard_map/ppermute | solution.py:488
  33.4 6.7 %collective-permute-start.12 = (bf16[448,128]{1,0:T(8,128)(2,1)S(1)}, bf16[448,128]{1,0:T(8,128)(2,1)S(1)}, u32[]{:S(2)}, u32[]{:S(2)}) collective-permute-start(bf16[448,128]{1,0:T(8,128)(2,1)S(1)} %shard_map.56.refs_0_), channel_id=1, source_target_pairs={{0,16},{1,8},{2,11},{3,19},{4,13},{5,21},{6,22},{7,14},{8,1},{9,25... | collective-permute-start | bytes 344072 | tf_op jit(solution)/shard_map/ppermute | solution.py:488
  36.0 17.6 %collective-permute-start.6 = (bf16[1120,128]{1,0:T(8,128)(2,1)S(1)}, bf16[1120,128]{1,0:T(8,128)(2,1)S(1)}, u32[]{:S(2)}, u32[]{:S(2)}) collective-permute-start(bf16[1120,128]{1,0:T(8,128)(2,1)S(1)} %shard_map.48.refs_0_), channel_id=1, source_target_pairs={{0,5},{1,2},{2,1},{3,6},{4,7},{5,0},{6,3},{7,4},{8,11},{9,12},{10,... | collective-permute-start | bytes 860168 | tf_op jit(solution)/shard_map/ppermute | solution.py:488
  40.4 4.3 %collective-permute-start.13 = (bf16[464,128]{1,0:T(8,128)(2,1)S(1)}, bf16[464,128]{1,0:T(8,128)(2,1)S(1)}, u32[]{:S(2)}, u32[]{:S(2)}) collective-permute-start(bf16[464,128]{1,0:T(8,128)(2,1)S(1)} %shard_map.57.refs_0_), channel_id=1, source_target_pairs={{0,3},{1,4},{2,7},{3,0},{4,1},{5,6},{6,5},{7,2},{8,13},{9,10},{10,... | collective-permute-start | bytes 356360 | tf_op jit(solution)/shard_map/ppermute | solution.py:488
  41.1 5.9 %collective-permute-start.17 = (bf16[512,128]{1,0:T(8,128)(2,1)S(1)}, bf16[512,128]{1,0:T(8,128)(2,1)S(1)}, u32[]{:S(2)}, u32[]{:S(2)}) collective-permute-start(bf16[512,128]{1,0:T(8,128)(2,1)S(1)} %get-tuple-element.36), channel_id=1, source_target_pairs={{0,9},{1,17},{2,18},{3,10},{4,20},{5,12},{6,15},{7,23},{8,24},{9,0... | collective-permute-start | bytes 393224 | tf_op jit(solution)/shard_map/ppermute | solution.py:488
  44.7 18.2 %collective-permute-start.14 = (bf16[928,128]{1,0:T(8,128)(2,1)S(1)}, bf16[928,128]{1,0:T(8,128)(2,1)S(1)}, u32[]{:S(2)}, u32[]{:S(2)}) collective-permute-start(bf16[928,128]{1,0:T(8,128)(2,1)S(1)} %shard_map.58.refs_0_), channel_id=1, source_target_pairs={{0,5},{1,2},{2,1},{3,6},{4,7},{5,0},{6,3},{7,4},{8,11},{9,12},{10,... | collective-permute-start | bytes 712712 | tf_op jit(solution)/shard_map/ppermute | solution.py:488
  47.0 5.3 %collective-permute-start.18 = (bf16[256,128]{1,0:T(8,128)(2,1)S(1)}, bf16[256,128]{1,0:T(8,128)(2,1)S(1)}, u32[]{:S(2)}, u32[]{:S(2)}) collective-permute-start(bf16[256,128]{1,0:T(8,128)(2,1)S(1)} %get-tuple-element.38), channel_id=1, source_target_pairs={{0,16},{1,8},{2,11},{3,19},{4,13},{5,21},{6,22},{7,14},{8,1},{9,25... | collective-permute-start | bytes 196616 | tf_op jit(solution)/shard_map/ppermute | solution.py:488
  52.3 3.8 %collective-permute-start.19 = (bf16[256,128]{1,0:T(8,128)(2,1)S(1)}, bf16[256,128]{1,0:T(8,128)(2,1)S(1)}, u32[]{:S(2)}, u32[]{:S(2)}) collective-permute-start(bf16[256,128]{1,0:T(8,128)(2,1)S(1)} %shard_map.65.a_ref), channel_id=1, source_target_pairs={{0,5},{1,2},{2,1},{3,6},{4,7},{5,0},{6,3},{7,4},{8,11},{9,12},{10,... | collective-permute-start | bytes 196616 | tf_op jit(solution)/shard_map/ppermute | solution.py:488
  53.6 18.0 %collective-permute-start.7 = (bf16[2240,128]{1,0:T(8,128)(2,1)S(1)}, bf16[2240,128]{1,0:T(8,128)(2,1)S(1)}, u32[]{:S(2)}, u32[]{:S(2)}) collective-permute-start(bf16[2240,128]{1,0:T(8,128)(2,1)S(1)} %shard_map.49.refs_2_.refs_4_), channel_id=1, source_target_pairs={{0,1},{1,0},{2,3},{3,2},{4,5},{5,4},{6,7},{7,6},{8,9},{9,8},{10,11... | collective-permute-start | bytes 1720328 | tf_op jit(solution)/shard_map/ppermute | solution.py:488
  56.1 3.8 %collective-permute-start.20 = (bf16[256,128]{1,0:T(8,128)(2,1)S(1)}, bf16[256,128]{1,0:T(8,128)(2,1)S(1)}, u32[]{:S(2)}, u32[]{:S(2)}) collective-permute-start(bf16[256,128]{1,0:T(8,128)(2,1)S(1)} %shard_map.66.refs_0_), channel_id=1, source_target_pairs={{0,3},{1,4},{2,7},{3,0},{4,1},{5,6},{6,5},{7,2},{8,13},{9,10},{10,... | collective-permute-start | bytes 196616 | tf_op jit(solution)/shard_map/ppermute | solution.py:488
  60.0 6.0 %collective-permute-start.21 = (bf16[272,128]{1,0:T(8,128)(2,1)S(1)}, bf16[272,128]{1,0:T(8,128)(2,1)S(1)}, u32[]{:S(2)}, u32[]{:S(2)}) collective-permute-start(bf16[272,128]{1,0:T(8,128)(2,1)S(1)} %shard_map.67.refs_0_), channel_id=1, source_target_pairs={{0,16},{1,8},{2,11},{3,19},{4,13},{5,21},{6,22},{7,14},{8,1},{9,25... | collective-permute-start | bytes 208904 | tf_op jit(solution)/shard_map/ppermute | solution.py:488
  62.9 10.5 %collective-permute-start.15 = (bf16[1856,128]{1,0:T(8,128)(2,1)S(1)}, bf16[1856,128]{1,0:T(8,128)(2,1)S(1)}, u32[]{:S(2)}, u32[]{:S(2)}) collective-permute-start(bf16[1856,128]{1,0:T(8,128)(2,1)S(1)} %shard_map.59.refs_4_.refs_5_), channel_id=1, source_target_pairs={{0,1},{1,0},{2,3},{3,2},{4,5},{5,4},{6,7},{7,6},{8,9},{9,8},{10,11... | collective-permute-start | bytes 1425416 | tf_op jit(solution)/shard_map/ppermute | solution.py:488
  66.0 4.7 %collective-permute-start.22 = (bf16[544,128]{1,0:T(8,128)(2,1)S(1)}, bf16[544,128]{1,0:T(8,128)(2,1)S(1)}, u32[]{:S(2)}, u32[]{:S(2)}) collective-permute-start(bf16[544,128]{1,0:T(8,128)(2,1)S(1)} %shard_map.68.refs_0_), channel_id=1, source_target_pairs={{0,9},{1,17},{2,18},{3,10},{4,20},{5,12},{6,15},{7,23},{8,24},{9,0... | collective-permute-start | bytes 417800 | tf_op jit(solution)/shard_map/ppermute | solution.py:488
  70.7 4.8 %collective-permute-start.23 = (bf16[1088,128]{1,0:T(8,128)(2,1)S(1)}, bf16[1088,128]{1,0:T(8,128)(2,1)S(1)}, u32[]{:S(2)}, u32[]{:S(2)}) collective-permute-start(bf16[1088,128]{1,0:T(8,128)(2,1)S(1)} %shard_map.69.refs_4_.refs_6_), channel_id=1, source_target_pairs={{0,1},{1,0},{2,3},{3,2},{4,5},{5,4},{6,7},{7,6},{8,9},{9,8},{10,11... | collective-permute-start | bytes 835592 | tf_op jit(solution)/shard_map/ppermute | solution.py:488

commit v8 on v7

--- a/solution.py
+++ b/solution.py
@@ -10,12 +10,13 @@
 PAD = 16
 SHARES = 4
 CUT = 17 / 39
-LATE = (2, 2)
+LATE = (1, 2)
 TURNS = (0, 1, 2)
 FAR_FIRST = 2
 TWO = 1
 PIECE = 128
-PANEL = 2
+PANEL = 1
+LOADS = 2
 AXES = ("gr", "gc")
 BF16 = jnp.bfloat16
 F32 = jnp.float32
@@ -136,16 +137,19 @@
     total_rows = orb_hbm.shape[0]
     side, extra = geometry(total_rows)
     _, low, up = starts(1, side)
-    rows = total_rows // 4
+    half = side * TILE
     copies = []
-    for at in (low, low + rows, up, up + rows):
-        for source, target in ((orb_hbm, orb_ref), (vel_hbm, vel_ref)):
-            part = pl.ds(pl.multiple_of(at, TILE), rows)
-            copies.append(pltpu.make_async_copy(source.at[part], target.at[part], sems.at[len(copies)]))
-            copies[-1].start()
-    ready = 4 if all(which == "near" for which, _, _ in tiles) else 8
-    if ready == 8 and all(which == "near" or (which == "far" and j * TILE < rows) for which, _, j in tiles):
-        ready = 6
+
+    def start(begin, parts):
+        for at in range(0, half, half // parts):
+            for source, target in ((orb_hbm, orb_ref), (vel_hbm, vel_ref)):
+                part = pl.ds(pl.multiple_of(begin + at, TILE), half // parts)
+                copies.append(pltpu.make_async_copy(source.at[part], target.at[part], sems.at[len(copies)]))
+                copies[-1].start()
+
+    start(low, LOADS)
+    start(up, LOADS)
+    ready = 2 * LOADS if all(which == "near" for which, _, _ in tiles) else 4 * LOADS
     for copy in copies[:ready]:
         copy.wait()
     product_kernel(orb_ref, vel_ref, away_ref, flip=1, tiles=tiles, side=side, extra=extra)
@@ -161,7 +165,7 @@
         12,
         pltpu.with_memory_space_constraint(orb, pltpu.HBM),
         pltpu.with_memory_space_constraint(vel, pltpu.HBM),
-        scratch=[pltpu.SemaphoreType.DMA((8,))],
+        scratch=[pltpu.SemaphoreType.DMA((4 * LOADS,))],
         in_specs=[HBM, HBM],
     )
 

time: 77.4 us -> 81.7 us (1.056)
  waiting for transfers between devices: 33.6 us -> 44.8 us
  starting transfers between devices: 28.6 us -> 22.3 us
    ppermute x24, waiting for transfers between devices: 33.6 us -> 44.8 us  [move(): lax.ppermute(value, AXES, swap if pair is None else permutation(nr, nc, p...]
    ppermute x24, starting transfers between devices: 28.6 us -> 22.3 us  [move(): lax.ppermute(value, AXES, swap if pair is None else permutation(nr, nc, p...]
  transfers between devices with their start and end apart: 24 -> 24, of which waited for: 15 -> 12; matrix products, arithmetic and copies ran while one was open for 0% -> 0% of each run, Pallas kernels for 13% -> 12%
where the time goes in v8:
time: 81.7 us; the launch traced here: 81.6 us
  waiting for transfers between devices  44.8 us (55%)
  starting transfers between devices  22.3 us (27%)
  Pallas kernels  13.5 us (17%)
  between operations  0.92 us (1%)
    ppermute x24, waiting for transfers between devices, move(): lax.ppermute(value, AXES, swap if pair is None else permutation(nr, nc, p...  44.8 us
    ppermute x24, starting transfers between devices, move(): lax.ppermute(value, AXES, swap if pair is None else permutation(nr, nc, p...  22.3 us
    pallas_call x31, Pallas kernels, call(): pl.pallas_call(kernel, out_shape=out, in_specs=in_specs or [VMEM] * len(o...  13.5 us
  transfers between devices with their start and end apart: 24, of which 12 were waited for; matrix products, arithmetic and copies ran while one was open for 0% of the time, Pallas kernels for 12%

profile of v8, /device:TPU:0, one launch (start us, length us, event | category | flops | bytes accessed | tf_op | source)
XLA Modules:
  0.0 81.6 jit_solution(3795575097973526875)
XLA Ops:
  0.6 2.4 %shard_map.41 = (bf16[2176,128]{1,0:T(8,128)(2,1)S(1)}, bf16[1536,512]{1,0:T(8,128)(2,1)S(1)}, bf16[1536,512]{1,0:T(8,128)(2,1)S(1)}) custom-call(bf16[1536,512]{1,0:T(8,128)(2,1)} %refs_0_.1, bf16[1536,512]{1,0:T(8,128)(2,1)} %refs_1_.1), custom_call_target="tpu_custom_call" | custom-call | tf_op jit(solution)/shard_map/pallas_call | solution.py:34
  3.0 0.6 collective-permute-start
  3.6 0.9 %shard_map.52 = bf16[1920,128]{1,0:T(8,128)(2,1)S(1)} custom-call(bf16[1536,512]{1,0:T(8,128)(2,1)S(1)} %get-tuple-element.22.refs_0_, bf16[1536,512]{1,0:T(8,128)(2,1)S(1)} %get-tuple-element.23.refs_1_), custom_call_target="tpu_custom_call" | custom-call | tf_op jit(solution)/shard_map/pallas_call | solution.py:34
  4.5 0.1 collective-permute-start.8
  4.6 0.9 %shard_map.42.refs_0_ = bf16[2176,128]{1,0:T(8,128)(2,1)S(1)} custom-call(bf16[1536,512]{1,0:T(8,128)(2,1)S(1)} %get-tuple-element.22.refs_0_, bf16[1536,512]{1,0:T(8,128)(2,1)S(1)} %get-tuple-element.23.refs_1_), custom_call_target="tpu_custom_call" | custom-call | tf_op jit(solution)/shard_map/pallas_call | solution.py:34
  5.6 0.1 shard_map.43
  5.7 2.7 %collective-permute-start.1 = (bf16[1088,128]{1,0:T(8,128)(2,1)S(1)}, bf16[1088,128]{1,0:T(8,128)(2,1)S(1)}, u32[]{:S(2)}, u32[]{:S(2)}) collective-permute-start(bf16[1088,128]{1,0:T(8,128)(2,1)S(1)} %get-tuple-element.26), channel_id=1, source_target_pairs={{0,5},{1,2},{2,1},{3,6},{4,7},{5,0},{6,3},{7,4},{8,11},{9,12},{10,... | collective-permute-start | bytes 835592 | tf_op jit(solution)/shard_map/ppermute | solution.py:492
  8.4 0.9 %shard_map.51.refs_0_ = bf16[1920,128]{1,0:T(8,128)(2,1)S(1)} custom-call(bf16[1536,512]{1,0:T(8,128)(2,1)S(1)} %get-tuple-element.22.refs_0_, bf16[1536,512]{1,0:T(8,128)(2,1)S(1)} %get-tuple-element.23.refs_1_), custom_call_target="tpu_custom_call" | custom-call | tf_op jit(solution)/shard_map/pallas_call | solution.py:34
  9.3 0.1 shard_map.53
  9.4 0.1 collective-permute-start.9
  9.5 3.1 %collective-permute-done.1.refs_1_ = bf16[1088,128]{1,0:T(8,128)(2,1)S(1)} collective-permute-done((bf16[1088,128]{1,0:T(8,128)(2,1)S(1)}, bf16[1088,128]{1,0:T(8,128)(2,1)S(1)}, u32[]{:S(2)}, u32[]{:S(2)}) %collective-permute-start.1) | collective-permute-done | bytes 278560 | tf_op jit(solution)/shard_map/ppermute | solution.py:492
  12.7 2.1 %collective-permute-start.2 = (bf16[544,128]{1,0:T(8,128)(2,1)S(1)}, bf16[544,128]{1,0:T(8,128)(2,1)S(1)}, u32[]{:S(2)}, u32[]{:S(2)}) collective-permute-start(bf16[544,128]{1,0:T(8,128)(2,1)S(1)} %get-tuple-element.28), channel_id=1, source_target_pairs={{0,3},{1,4},{2,7},{3,0},{4,1},{5,6},{6,5},{7,2},{8,13},{9,10},{10,... | collective-permute-start | bytes 417800 | tf_op jit(solution)/shard_map/ppermute | solution.py:492
  14.8 2.7 %collective-permute-done.2.b_ref = bf16[544,128]{1,0:T(8,128)(2,1)S(1)} collective-permute-done((bf16[544,128]{1,0:T(8,128)(2,1)S(1)}, bf16[544,128]{1,0:T(8,128)(2,1)S(1)}, u32[]{:S(2)}, u32[]{:S(2)}) %collective-permute-start.2) | collective-permute-done | bytes 139296 | tf_op jit(solution)/shard_map/ppermute | solution.py:492
  17.6 1.9 %collective-permute-start.3 = (bf16[544,128]{1,0:T(8,128)(2,1)S(1)}, bf16[544,128]{1,0:T(8,128)(2,1)S(1)}, u32[]{:S(2)}, u32[]{:S(2)}) collective-permute-start(bf16[544,128]{1,0:T(8,128)(2,1)S(1)} %shard_map.45.a_ref), channel_id=1, source_target_pairs={{0,9},{1,17},{2,18},{3,10},{4,20},{5,12},{6,15},{7,23},{8,24},{9,0... | collective-permute-start | bytes 417800 | tf_op jit(solution)/shard_map/ppermute | solution.py:492
  19.5 1.4 %collective-permute-start.10 = (bf16[480,128]{1,0:T(8,128)(2,1)S(1)}, bf16[480,128]{1,0:T(8,128)(2,1)S(1)}, u32[]{:S(2)}, u32[]{:S(2)}) collective-permute-start(bf16[480,128]{1,0:T(8,128)(2,1)S(1)} %get-tuple-element.32), channel_id=1, source_target_pairs={{0,3},{1,4},{2,7},{3,0},{4,1},{5,6},{6,5},{7,2},{8,13},{9,10},{10,... | collective-permute-start | bytes 368648 | tf_op jit(solution)/shard_map/ppermute | solution.py:492
  20.9 2.8 %collective-permute-done.3.b_ref = bf16[544,128]{1,0:T(8,128)(2,1)S(1)} collective-permute-done((bf16[544,128]{1,0:T(8,128)(2,1)S(1)}, bf16[544,128]{1,0:T(8,128)(2,1)S(1)}, u32[]{:S(2)}, u32[]{:S(2)}) %collective-permute-start.3) | collective-permute-done | bytes 139296 | tf_op jit(solution)/shard_map/ppermute | solution.py:492
  23.7 2.4 %collective-permute-start.4 = (bf16[544,128]{1,0:T(8,128)(2,1)S(1)}, bf16[544,128]{1,0:T(8,128)(2,1)S(1)}, u32[]{:S(2)}, u32[]{:S(2)}) collective-permute-start(bf16[544,128]{1,0:T(8,128)(2,1)S(1)} %shard_map.46.refs_0_), channel_id=1, source_target_pairs={{0,16},{1,8},{2,11},{3,19},{4,13},{5,21},{6,22},{7,14},{8,1},{9,25... | collective-permute-start | bytes 417800 | tf_op jit(solution)/shard_map/ppermute | solution.py:492
  26.1 1.1 %collective-permute-start.11 = (bf16[480,128]{1,0:T(8,128)(2,1)S(1)}, bf16[480,128]{1,0:T(8,128)(2,1)S(1)}, u32[]{:S(2)}, u32[]{:S(2)}) collective-permute-start(bf16[480,128]{1,0:T(8,128)(2,1)S(1)} %shard_map.55.a_ref), channel_id=1, source_target_pairs={{0,9},{1,17},{2,18},{3,10},{4,20},{5,12},{6,15},{7,23},{8,24},{9,0... | collective-permute-start | bytes 368648 | tf_op jit(solution)/shard_map/ppermute | solution.py:492
  27.2 6.5 %collective-permute-done.11.b_ref = bf16[480,128]{1,0:T(8,128)(2,1)S(1)} collective-permute-done((bf16[480,128]{1,0:T(8,128)(2,1)S(1)}, bf16[480,128]{1,0:T(8,128)(2,1)S(1)}, u32[]{:S(2)}, u32[]{:S(2)}) %collective-permute-start.11) | collective-permute-done | bytes 122912 | tf_op jit(solution)/shard_map/ppermute | solution.py:492
  33.8 0.1 collective-permute-start.12
  33.9 0.4 shard_map.47.refs_0_
  34.2 0.8 %collective-permute-start.5 = (bf16[560,128]{1,0:T(8,128)(2,1)S(1)}, bf16[560,128]{1,0:T(8,128)(2,1)S(1)}, u32[]{:S(2)}, u32[]{:S(2)}) collective-permute-start(bf16[560,128]{1,0:T(8,128)(2,1)S(1)} %shard_map.47.refs_0_), channel_id=1, source_target_pairs={{0,3},{1,4},{2,7},{3,0},{4,1},{5,6},{6,5},{7,2},{8,13},{9,10},{10,... | collective-permute-start | bytes 430088 | tf_op jit(solution)/shard_map/ppermute | solution.py:492
  35.1 0.5 shard_map.62
  35.6 1.0 %collective-permute-start.16 = (bf16[896,128]{1,0:T(8,128)(2,1)S(1)}, bf16[896,128]{1,0:T(8,128)(2,1)S(1)}, u32[]{:S(2)}, u32[]{:S(2)}) collective-permute-start(bf16[896,128]{1,0:T(8,128)(2,1)S(1)} %shard_map.62), channel_id=1, source_target_pairs={{0,1},{1,0},{2,3},{3,2},{4,5},{5,4},{6,7},{7,6},{8,9},{9,8},{10,11... | collective-permute-start | bytes 688136 | tf_op jit(solution)/shard_map/ppermute | solution.py:492
  36.6 4.1 %collective-permute-done.12.refs_1_ = bf16[480,128]{1,0:T(8,128)(2,1)S(1)} collective-permute-done((bf16[480,128]{1,0:T(8,128)(2,1)S(1)}, bf16[480,128]{1,0:T(8,128)(2,1)S(1)}, u32[]{:S(2)}, u32[]{:S(2)}) %collective-permute-start.12) | collective-permute-done | bytes 122912 | tf_op jit(solution)/shard_map/ppermute | solution.py:492
  40.7 0.2 shard_map.57.refs_0_
  41.0 2.8 %collective-permute-start.6 = (bf16[1120,128]{1,0:T(8,128)(2,1)S(1)}, bf16[1120,128]{1,0:T(8,128)(2,1)S(1)}, u32[]{:S(2)}, u32[]{:S(2)}) collective-permute-start(bf16[1120,128]{1,0:T(8,128)(2,1)S(1)} %shard_map.48.refs_0_), channel_id=1, source_target_pairs={{0,5},{1,2},{2,1},{3,6},{4,7},{5,0},{6,3},{7,4},{8,11},{9,12},{10,... | collective-permute-start | bytes 860168 | tf_op jit(solution)/shard_map/ppermute | solution.py:492
  43.7 2.9 %collective-permute-done.13.refs_1_ = bf16[496,128]{1,0:T(8,128)(2,1)S(1)} collective-permute-done((bf16[496,128]{1,0:T(8,128)(2,1)S(1)}, bf16[496,128]{1,0:T(8,128)(2,1)S(1)}, u32[]{:S(2)}, u32[]{:S(2)}) %collective-permute-start.13) | collective-permute-done | bytes 127008 | tf_op jit(solution)/shard_map/ppermute | solution.py:492
  46.6 1.3 %collective-permute-start.14 = (bf16[992,128]{1,0:T(8,128)(2,1)S(1)}, bf16[992,128]{1,0:T(8,128)(2,1)S(1)}, u32[]{:S(2)}, u32[]{:S(2)}) collective-permute-start(bf16[992,128]{1,0:T(8,128)(2,1)S(1)} %shard_map.58.refs_0_), channel_id=1, source_target_pairs={{0,5},{1,2},{2,1},{3,6},{4,7},{5,0},{6,3},{7,4},{8,11},{9,12},{10,... | collective-permute-start | bytes 761864 | tf_op jit(solution)/shard_map/ppermute | solution.py:492
  48.0 0.5 shard_map.61.refs_0_
  48.6 0.6 collective-permute-start.17
  49.2 3.7 %collective-permute-done.17.refs_1_ = bf16[448,128]{1,0:T(8,128)(2,1)S(1)} collective-permute-done((bf16[448,128]{1,0:T(8,128)(2,1)S(1)}, bf16[448,128]{1,0:T(8,128)(2,1)S(1)}, u32[]{:S(2)}, u32[]{:S(2)}) %collective-permute-start.17) | collective-permute-done | bytes 114720 | tf_op jit(solution)/shard_map/ppermute | solution.py:492
  53.1 0.8 collective-permute-start.7
  53.9 4.2 %collective-permute-done.18.b_ref = bf16[224,128]{1,0:T(8,128)(2,1)S(1)} collective-permute-done((bf16[224,128]{1,0:T(8,128)(2,1)S(1)}, bf16[224,128]{1,0:T(8,128)(2,1)S(1)}, u32[]{:S(2)}, u32[]{:S(2)}) %collective-permute-start.18) | collective-permute-done | bytes 57376 | tf_op jit(solution)/shard_map/ppermute | solution.py:492
  58.1 1.2 %collective-permute-start.19 = (bf16[224,128]{1,0:T(8,128)(2,1)S(1)}, bf16[224,128]{1,0:T(8,128)(2,1)S(1)}, u32[]{:S(2)}, u32[]{:S(2)}) collective-permute-start(bf16[224,128]{1,0:T(8,128)(2,1)S(1)} %shard_map.65.a_ref), channel_id=1, source_target_pairs={{0,5},{1,2},{2,1},{3,6},{4,7},{5,0},{6,3},{7,4},{8,11},{9,12},{10,... | collective-permute-start | bytes 172040 | tf_op jit(solution)/shard_map/ppermute | solution.py:492
  59.4 0.1 collective-permute-start.15
  59.4 2.3 %collective-permute-done.19.b_ref = bf16[224,128]{1,0:T(8,128)(2,1)S(1)} collective-permute-done((bf16[224,128]{1,0:T(8,128)(2,1)S(1)}, bf16[224,128]{1,0:T(8,128)(2,1)S(1)}, u32[]{:S(2)}, u32[]{:S(2)}) %collective-permute-start.19) | collective-permute-done | bytes 57376 | tf_op jit(solution)/shard_map/ppermute | solution.py:492
  61.8 0.6 collective-permute-start.20
  62.4 3.1 %collective-permute-done.20.refs_1_ = bf16[224,128]{1,0:T(8,128)(2,1)S(1)} collective-permute-done((bf16[224,128]{1,0:T(8,128)(2,1)S(1)}, bf16[224,128]{1,0:T(8,128)(2,1)S(1)}, u32[]{:S(2)}, u32[]{:S(2)}) %collective-permute-start.20) | collective-permute-done | bytes 57376 | tf_op jit(solution)/shard_map/ppermute | solution.py:492
  65.4 0.1 shard_map.67.refs_0_
  65.6 0.5 collective-permute-start.21
  66.1 5.1 %collective-permute-done.21.refs_1_ = bf16[240,128]{1,0:T(8,128)(2,1)S(1)} collective-permute-done((bf16[240,128]{1,0:T(8,128)(2,1)S(1)}, bf16[240,128]{1,0:T(8,128)(2,1)S(1)}, u32[]{:S(2)}, u32[]{:S(2)}) %collective-permute-start.21) | collective-permute-done | bytes 61472 | tf_op jit(solution)/shard_map/ppermute | solution.py:492
  71.3 0.1 collective-permute-start.22
  71.4 4.3 %collective-permute-done.22.refs_1_ = bf16[480,128]{1,0:T(8,128)(2,1)S(1)} collective-permute-done((bf16[480,128]{1,0:T(8,128)(2,1)S(1)}, bf16[480,128]{1,0:T(8,128)(2,1)S(1)}, u32[]{:S(2)}, u32[]{:S(2)}) %collective-permute-start.22) | collective-permute-done | bytes 122912 | tf_op jit(solution)/shard_map/ppermute | solution.py:492
  75.8 0.8 shard_map.50.refs_2_
  76.5 1.8 %shard_map.60 = (f32[768,512]{1,0:T(8,128)S(1)}, f32[768,512]{1,0:T(8,128)S(1)}) custom-call(bf16[1536,512]{1,0:T(8,128)(2,1)S(1)} %get-tuple-element.22.refs_0_, bf16[1536,512]{1,0:T(8,128)(2,1)S(1)} %get-tuple-element.23.refs_1_, f32[768,512]{1,0:T(8,128)S(1)} %shard_map.50.refs_2_, bf16[2240,128]{1,0:T(8,128)(2,1)S(1)} %collective-permute-done.7.refs_3_.refs_7_, ...), custom_call_target="tpu_custom_call" | custom-call | tf_op jit(solution)/shard_map/pallas_call | solution.py:34
  78.3 1.7 %shard_map.70 = (f32[1536,512]{1,0:T(8,128)}, f32[768,512]{1,0:T(8,128)S(1)}, f32[768,512]{1,0:T(8,128)S(1)}) custom-call(bf16[1536,512]{1,0:T(8,128)(2,1)S(1)} %get-tuple-element.22.refs_0_, f32[768,512]{1,0:T(8,128)S(1)} %get-tuple-element.33.refs_1_, f32[768,512]{1,0:T(8,128)S(1)} %get-tuple-element.34.refs_2_, ...), custom_call_target="tpu_custom_call" | custom-call | tf_op jit(solution)/shard_map/pallas_call | solution.py:34
  80.1 1.5 %shard_map.71 = (f32[1536,512]{1,0:T(8,128)}, f32[1]{0:T(128)}) custom-call(bf16[1536,512]{1,0:T(8,128)(2,1)S(1)} %get-tuple-element.22.refs_0_, f32[768,512]{1,0:T(8,128)S(1)} %get-tuple-element.39.refs_1_, f32[768,512]{1,0:T(8,128)S(1)} %get-tuple-element.40.refs_2_, ...), custom_call_target="tpu_custom_call", output_to_operand_aliasing={{0}: (10, {})} | custom-call | tf_op jit(solution)/shard_map/pallas_call | solution.py:34
  (31 shorter events, 0.8 us)
Async XLA Ops:
  3.0 2.5 %collective-permute-start = (bf16[2176,128]{1,0:T(8,128)(2,1)S(1)}, bf16[2176,128]{1,0:T(8,128)(2,1)S(1)}, u32[]{:S(2)}, u32[]{:S(2)}) collective-permute-start(bf16[2176,128]{1,0:T(8,128)(2,1)S(1)} %get-tuple-element.24), channel_id=1, source_target_pairs={{0,1},{1,0},{2,3},{3,2},{4,5},{5,4},{6,7},{7,6},{8,9},{9,8},{10,11... | collective-permute-start | bytes 1671176 | tf_op jit(solution)/shard_map/ppermute | solution.py:492
  4.5 4.8 %collective-permute-start.8 = (bf16[1920,128]{1,0:T(8,128)(2,1)S(1)}, bf16[1920,128]{1,0:T(8,128)(2,1)S(1)}, u32[]{:S(2)}, u32[]{:S(2)}) collective-permute-start(bf16[1920,128]{1,0:T(8,128)(2,1)S(1)} %shard_map.52), channel_id=1, source_target_pairs={{0,1},{1,0},{2,3},{3,2},{4,5},{5,4},{6,7},{7,6},{8,9},{9,8},{10,11... | collective-permute-start | bytes 1474568 | tf_op jit(solution)/shard_map/ppermute | solution.py:492
  5.7 6.9 %collective-permute-start.1 = (bf16[1088,128]{1,0:T(8,128)(2,1)S(1)}, bf16[1088,128]{1,0:T(8,128)(2,1)S(1)}, u32[]{:S(2)}, u32[]{:S(2)}) collective-permute-start(bf16[1088,128]{1,0:T(8,128)(2,1)S(1)} %get-tuple-element.26), channel_id=1, source_target_pairs={{0,5},{1,2},{2,1},{3,6},{4,7},{5,0},{6,3},{7,4},{8,11},{9,12},{10,... | collective-permute-start | bytes 835592 | tf_op jit(solution)/shard_map/ppermute | solution.py:492
  9.4 10.0 %collective-permute-start.9 = (bf16[960,128]{1,0:T(8,128)(2,1)S(1)}, bf16[960,128]{1,0:T(8,128)(2,1)S(1)}, u32[]{:S(2)}, u32[]{:S(2)}) collective-permute-start(bf16[960,128]{1,0:T(8,128)(2,1)S(1)} %get-tuple-element.30), channel_id=1, source_target_pairs={{0,5},{1,2},{2,1},{3,6},{4,7},{5,0},{6,3},{7,4},{8,11},{9,12},{10,... | collective-permute-start | bytes 737288 | tf_op jit(solution)/shard_map/ppermute | solution.py:492
  12.7 4.9 %collective-permute-start.2 = (bf16[544,128]{1,0:T(8,128)(2,1)S(1)}, bf16[544,128]{1,0:T(8,128)(2,1)S(1)}, u32[]{:S(2)}, u32[]{:S(2)}) collective-permute-start(bf16[544,128]{1,0:T(8,128)(2,1)S(1)} %get-tuple-element.28), channel_id=1, source_target_pairs={{0,3},{1,4},{2,7},{3,0},{4,1},{5,6},{6,5},{7,2},{8,13},{9,10},{10,... | collective-permute-start | bytes 417800 | tf_op jit(solution)/shard_map/ppermute | solution.py:492
  17.6 6.1 %collective-permute-start.3 = (bf16[544,128]{1,0:T(8,128)(2,1)S(1)}, bf16[544,128]{1,0:T(8,128)(2,1)S(1)}, u32[]{:S(2)}, u32[]{:S(2)}) collective-permute-start(bf16[544,128]{1,0:T(8,128)(2,1)S(1)} %shard_map.45.a_ref), channel_id=1, source_target_pairs={{0,9},{1,17},{2,18},{3,10},{4,20},{5,12},{6,15},{7,23},{8,24},{9,0... | collective-permute-start | bytes 417800 | tf_op jit(solution)/shard_map/ppermute | solution.py:492
  19.5 6.6 %collective-permute-start.10 = (bf16[480,128]{1,0:T(8,128)(2,1)S(1)}, bf16[480,128]{1,0:T(8,128)(2,1)S(1)}, u32[]{:S(2)}, u32[]{:S(2)}) collective-permute-start(bf16[480,128]{1,0:T(8,128)(2,1)S(1)} %get-tuple-element.32), channel_id=1, source_target_pairs={{0,3},{1,4},{2,7},{3,0},{4,1},{5,6},{6,5},{7,2},{8,13},{9,10},{10,... | collective-permute-start | bytes 368648 | tf_op jit(solution)/shard_map/ppermute | solution.py:492
  23.7 10.2 %collective-permute-start.4 = (bf16[544,128]{1,0:T(8,128)(2,1)S(1)}, bf16[544,128]{1,0:T(8,128)(2,1)S(1)}, u32[]{:S(2)}, u32[]{:S(2)}) collective-permute-start(bf16[544,128]{1,0:T(8,128)(2,1)S(1)} %shard_map.46.refs_0_), channel_id=1, source_target_pairs={{0,16},{1,8},{2,11},{3,19},{4,13},{5,21},{6,22},{7,14},{8,1},{9,25... | collective-permute-start | bytes 417800 | tf_op jit(solution)/shard_map/ppermute | solution.py:492
  26.1 7.6 %collective-permute-start.11 = (bf16[480,128]{1,0:T(8,128)(2,1)S(1)}, bf16[480,128]{1,0:T(8,128)(2,1)S(1)}, u32[]{:S(2)}, u32[]{:S(2)}) collective-permute-start(bf16[480,128]{1,0:T(8,128)(2,1)S(1)} %shard_map.55.a_ref), channel_id=1, source_target_pairs={{0,9},{1,17},{2,18},{3,10},{4,20},{5,12},{6,15},{7,23},{8,24},{9,0... | collective-permute-start | bytes 368648 | tf_op jit(solution)/shard_map/ppermute | solution.py:492
  33.8 6.9 %collective-permute-start.12 = (bf16[480,128]{1,0:T(8,128)(2,1)S(1)}, bf16[480,128]{1,0:T(8,128)(2,1)S(1)}, u32[]{:S(2)}, u32[]{:S(2)}) collective-permute-start(bf16[480,128]{1,0:T(8,128)(2,1)S(1)} %shard_map.56.refs_0_), channel_id=1, source_target_pairs={{0,16},{1,8},{2,11},{3,19},{4,13},{5,21},{6,22},{7,14},{8,1},{9,25... | collective-permute-start | bytes 368648 | tf_op jit(solution)/shard_map/ppermute | solution.py:492
  34.2 6.7 %collective-permute-start.5 = (bf16[560,128]{1,0:T(8,128)(2,1)S(1)}, bf16[560,128]{1,0:T(8,128)(2,1)S(1)}, u32[]{:S(2)}, u32[]{:S(2)}) collective-permute-start(bf16[560,128]{1,0:T(8,128)(2,1)S(1)} %shard_map.47.refs_0_), channel_id=1, source_target_pairs={{0,3},{1,4},{2,7},{3,0},{4,1},{5,6},{6,5},{7,2},{8,13},{9,10},{10,... | collective-permute-start | bytes 430088 | tf_op jit(solution)/shard_map/ppermute | solution.py:492
  35.6 12.9 %collective-permute-start.16 = (bf16[896,128]{1,0:T(8,128)(2,1)S(1)}, bf16[896,128]{1,0:T(8,128)(2,1)S(1)}, u32[]{:S(2)}, u32[]{:S(2)}) collective-permute-start(bf16[896,128]{1,0:T(8,128)(2,1)S(1)} %shard_map.62), channel_id=1, source_target_pairs={{0,1},{1,0},{2,3},{3,2},{4,5},{5,4},{6,7},{7,6},{8,9},{9,8},{10,11... | collective-permute-start | bytes 688136 | tf_op jit(solution)/shard_map/ppermute | solution.py:492
  40.9 5.7 %collective-permute-start.13 = (bf16[496,128]{1,0:T(8,128)(2,1)S(1)}, bf16[496,128]{1,0:T(8,128)(2,1)S(1)}, u32[]{:S(2)}, u32[]{:S(2)}) collective-permute-start(bf16[496,128]{1,0:T(8,128)(2,1)S(1)} %shard_map.57.refs_0_), channel_id=1, source_target_pairs={{0,3},{1,4},{2,7},{3,0},{4,1},{5,6},{6,5},{7,2},{8,13},{9,10},{10,... | collective-permute-start | bytes 380936 | tf_op jit(solution)/shard_map/ppermute | solution.py:492
  41.0 12.0 %collective-permute-start.6 = (bf16[1120,128]{1,0:T(8,128)(2,1)S(1)}, bf16[1120,128]{1,0:T(8,128)(2,1)S(1)}, u32[]{:S(2)}, u32[]{:S(2)}) collective-permute-start(bf16[1120,128]{1,0:T(8,128)(2,1)S(1)} %shard_map.48.refs_0_), channel_id=1, source_target_pairs={{0,5},{1,2},{2,1},{3,6},{4,7},{5,0},{6,3},{7,4},{8,11},{9,12},{10,... | collective-permute-start | bytes 860168 | tf_op jit(solution)/shard_map/ppermute | solution.py:492
  46.6 12.6 %collective-permute-start.14 = (bf16[992,128]{1,0:T(8,128)(2,1)S(1)}, bf16[992,128]{1,0:T(8,128)(2,1)S(1)}, u32[]{:S(2)}, u32[]{:S(2)}) collective-permute-start(bf16[992,128]{1,0:T(8,128)(2,1)S(1)} %shard_map.58.refs_0_), channel_id=1, source_target_pairs={{0,5},{1,2},{2,1},{3,6},{4,7},{5,0},{6,3},{7,4},{8,11},{9,12},{10,... | collective-permute-start | bytes 761864 | tf_op jit(solution)/shard_map/ppermute | solution.py:492
  48.6 4.3 %collective-permute-start.17 = (bf16[448,128]{1,0:T(8,128)(2,1)S(1)}, bf16[448,128]{1,0:T(8,128)(2,1)S(1)}, u32[]{:S(2)}, u32[]{:S(2)}) collective-permute-start(bf16[448,128]{1,0:T(8,128)(2,1)S(1)} %get-tuple-element.36), channel_id=1, source_target_pairs={{0,9},{1,17},{2,18},{3,10},{4,20},{5,12},{6,15},{7,23},{8,24},{9,0... | collective-permute-start | bytes 344072 | tf_op jit(solution)/shard_map/ppermute | solution.py:492
  52.9 5.1 %collective-permute-start.18 = (bf16[224,128]{1,0:T(8,128)(2,1)S(1)}, bf16[224,128]{1,0:T(8,128)(2,1)S(1)}, u32[]{:S(2)}, u32[]{:S(2)}) collective-permute-start(bf16[224,128]{1,0:T(8,128)(2,1)S(1)} %get-tuple-element.38), channel_id=1, source_target_pairs={{0,16},{1,8},{2,11},{3,19},{4,13},{5,21},{6,22},{7,14},{8,1},{9,25... | collective-permute-start | bytes 172040 | tf_op jit(solution)/shard_map/ppermute | solution.py:492
  53.1 23.5 %collective-permute-start.7 = (bf16[2240,128]{1,0:T(8,128)(2,1)S(1)}, bf16[2240,128]{1,0:T(8,128)(2,1)S(1)}, u32[]{:S(2)}, u32[]{:S(2)}) collective-permute-start(bf16[2240,128]{1,0:T(8,128)(2,1)S(1)} %shard_map.49.refs_2_.refs_4_), channel_id=1, source_target_pairs={{0,1},{1,0},{2,3},{3,2},{4,5},{5,4},{6,7},{7,6},{8,9},{9,8},{10,11... | collective-permute-start | bytes 1720328 | tf_op jit(solution)/shard_map/ppermute | solution.py:492
  58.1 3.7 %collective-permute-start.19 = (bf16[224,128]{1,0:T(8,128)(2,1)S(1)}, bf16[224,128]{1,0:T(8,128)(2,1)S(1)}, u32[]{:S(2)}, u32[]{:S(2)}) collective-permute-start(bf16[224,128]{1,0:T(8,128)(2,1)S(1)} %shard_map.65.a_ref), channel_id=1, source_target_pairs={{0,5},{1,2},{2,1},{3,6},{4,7},{5,0},{6,3},{7,4},{8,11},{9,12},{10,... | collective-permute-start | bytes 172040 | tf_op jit(solution)/shard_map/ppermute | solution.py:492
  59.4 19.0 %collective-permute-start.15 = (bf16[1984,128]{1,0:T(8,128)(2,1)S(1)}, bf16[1984,128]{1,0:T(8,128)(2,1)S(1)}, u32[]{:S(2)}, u32[]{:S(2)}) collective-permute-start(bf16[1984,128]{1,0:T(8,128)(2,1)S(1)} %shard_map.59.refs_4_.refs_5_), channel_id=1, source_target_pairs={{0,1},{1,0},{2,3},{3,2},{4,5},{5,4},{6,7},{7,6},{8,9},{9,8},{10,11... | collective-permute-start | bytes 1523720 | tf_op jit(solution)/shard_map/ppermute | solution.py:492
  61.8 3.7 %collective-permute-start.20 = (bf16[224,128]{1,0:T(8,128)(2,1)S(1)}, bf16[224,128]{1,0:T(8,128)(2,1)S(1)}, u32[]{:S(2)}, u32[]{:S(2)}) collective-permute-start(bf16[224,128]{1,0:T(8,128)(2,1)S(1)} %shard_map.66.refs_0_), channel_id=1, source_target_pairs={{0,3},{1,4},{2,7},{3,0},{4,1},{5,6},{6,5},{7,2},{8,13},{9,10},{10,... | collective-permute-start | bytes 172040 | tf_op jit(solution)/shard_map/ppermute | solution.py:492
  65.6 5.7 %collective-permute-start.21 = (bf16[240,128]{1,0:T(8,128)(2,1)S(1)}, bf16[240,128]{1,0:T(8,128)(2,1)S(1)}, u32[]{:S(2)}, u32[]{:S(2)}) collective-permute-start(bf16[240,128]{1,0:T(8,128)(2,1)S(1)} %shard_map.67.refs_0_), channel_id=1, source_target_pairs={{0,16},{1,8},{2,11},{3,19},{4,13},{5,21},{6,22},{7,14},{8,1},{9,25... | collective-permute-start | bytes 184328 | tf_op jit(solution)/shard_map/ppermute | solution.py:492
  71.3 4.4 %collective-permute-start.22 = (bf16[480,128]{1,0:T(8,128)(2,1)S(1)}, bf16[480,128]{1,0:T(8,128)(2,1)S(1)}, u32[]{:S(2)}, u32[]{:S(2)}) collective-permute-start(bf16[480,128]{1,0:T(8,128)(2,1)S(1)} %shard_map.68.refs_0_), channel_id=1, source_target_pairs={{0,9},{1,17},{2,18},{3,10},{4,20},{5,12},{6,15},{7,23},{8,24},{9,0... | collective-permute-start | bytes 368648 | tf_op jit(solution)/shard_map/ppermute | solution.py:492
  75.7 4.4 %collective-permute-start.23 = (bf16[960,128]{1,0:T(8,128)(2,1)S(1)}, bf16[960,128]{1,0:T(8,128)(2,1)S(1)}, u32[]{:S(2)}, u32[]{:S(2)}) collective-permute-start(bf16[960,128]{1,0:T(8,128)(2,1)S(1)} %shard_map.69.refs_4_.refs_6_), channel_id=1, source_target_pairs={{0,1},{1,0},{2,3},{3,2},{4,5},{5,4},{6,7},{7,6},{8,9},{9,8},{10,11... | collective-permute-start | bytes 737288 | tf_op jit(solution)/shard_map/ppermute | solution.py:492
